TPU v7x, 32 devices: a whole 2x2x4 slice. The times are simulated.
32 devices in a mesh: fsdp: 4 (over z), seq: 8 (over y, x, core).
Axes of the slice: x: 2, y: 2, z: 4, core: 2. Of those that a mesh axis runs over, the one named last changes fastest.
Arguments:
- block_input: bfloat16 [4, 1024, 2048], P('fsdp', 'seq'), may hold values from -6 to 6
- cotangent: bfloat16 [4, 1024, 2048], P('fsdp', 'seq'), may hold values from -6 to 6
- ln1_gain: bfloat16 [2048], P(('fsdp', 'seq')), may hold values from 0.5 to 1.5
- ln1_bias: bfloat16 [2048], P(('fsdp', 'seq')), may hold values from -1.5 to 1.5
- qkv_weight: bfloat16 [2048, 3, 2048], P('fsdp', None, 'seq'), may hold values from -0.125 to 0.125
- qkv_bias: bfloat16 [3, 2048], P(None, ('fsdp', 'seq')), may hold values from -8 to 8
- out_weight: bfloat16 [2048, 2048], P('seq', 'fsdp'), may hold values from -3 to 3
- ln2_gain: bfloat16 [2048], P(('fsdp', 'seq')), may hold values from 0.5 to 1.5
- ln2_bias: bfloat16 [2048], P(('fsdp', 'seq')), may hold values from -1.5 to 1.5
- gate_up_weight: bfloat16 [2048, 2, 5632], P('fsdp', None, 'seq'), may hold values from -0.125 to 0.125
- down_weight: bfloat16 [5632, 2048], P('seq', 'fsdp'), may hold values from -0.078125 to 0.078125
Outputs:
- block_output: bfloat16 [4, 1024, 2048], P('fsdp', 'seq')
- input_grad: float32 [4, 1024, 2048], P('fsdp', 'seq')
- grad_ln1_gain: float32 [2048], P(('fsdp', 'seq'))
- grad_ln1_bias: float32 [2048], P(('fsdp', 'seq'))
- grad_qkv_weight: float32 [2048, 3, 2048], P('fsdp', None, 'seq')
- grad_qkv_bias: float32 [3, 2048], P(None, ('fsdp', 'seq'))
- grad_out_weight: float32 [2048, 2048], P('seq', 'fsdp')
- grad_ln2_gain: float32 [2048], P(('fsdp', 'seq'))
- grad_ln2_bias: float32 [2048], P(('fsdp', 'seq'))
- grad_gate_up_weight: float32 [2048, 2, 5632], P('fsdp', None, 'seq')
- grad_down_weight: float32 [5632, 2048], P('seq', 'fsdp')
All inputs are finite; a program needn't handle non-finite values.
Results may differ from a plain program's by a relative error of at most 0.023.
The roundings to bfloat16 on the way count: a program that leaves them out, or rounds other values in their place, can miss the bound.
Values may be sent and summed in bfloat16 or wider, within the bound.
A program may use at most 512 MiB of HBM per device.

v0:
```python
import jax
import jax.numpy as jnp
from jax import lax
from jax.sharding import PartitionSpec as P

HEADS = 32
HEAD_DIM = 64
FF = 5632
ROTARY = 16


epsilon = 1e-05
masked_score = -1e30


def layer_norm(rows_in, gain, shift):
    center = rows_in - jnp.mean(rows_in, axis=-1, keepdims=True)
    inverse = lax.rsqrt(jnp.mean(center * center, axis=-1, keepdims=True) + epsilon)
    normed = center * inverse
    return (normed * gain + shift, normed, inverse)


def norm_back(grad_rows, normed, inverse, gain):
    scaled = grad_rows * gain
    return inverse * (
        scaled
        - jnp.mean(scaled, axis=-1, keepdims=True)
        - normed * jnp.mean(scaled * normed, axis=-1, keepdims=True)
    )


def rotary_tables(positions):
    half_rot = ROTARY // 2
    frequency = 10000.0 ** (-2.0 * jnp.arange(half_rot, dtype=jnp.float32) / ROTARY)
    angles = positions[:, None] * frequency[None, :]
    angles = jnp.concatenate([angles, angles], axis=1)
    return (jnp.cos(angles)[:, None, :], jnp.sin(angles)[:, None, :])


def rotate(field, cosine, sine_part, direction):
    half_rot = ROTARY // 2
    head_part = field[..., :ROTARY]
    turned = jnp.concatenate([-head_part[..., half_rot:], head_part[..., :half_rot]], axis=-1)
    moved = head_part * cosine + direction * turned * sine_part
    return jnp.concatenate([moved, field[..., ROTARY:]], axis=-1)


def attend(queries, key_rows, value_rows):
    length, head_count, head_width = queries.shape
    block_rows = min(512, length)
    score_scale = head_width ** (-0.5)
    key_pos = jnp.arange(length, dtype=jnp.int32)

    def one_block(row_start):
        query_block = lax.dynamic_slice_in_dim(queries, row_start, block_rows, 0)
        scores = (
            jnp.einsum("qhd,khd->hqk", query_block, key_rows, preferred_element_type=jnp.float32)
            * score_scale
        )
        query_pos = row_start + jnp.arange(block_rows, dtype=jnp.int32)
        causal = key_pos[None, :] <= query_pos[:, None]
        scores = jnp.where(causal[None], scores, masked_score)
        row_max = jnp.max(scores, axis=-1, keepdims=True)
        log_total = row_max + jnp.log(jnp.sum(jnp.exp(scores - row_max), axis=-1, keepdims=True))
        attn_probs = jnp.exp(scores - log_total).astype(jnp.bfloat16)
        attn_out = jnp.einsum(
            "hqk,khd->qhd", attn_probs, value_rows, preferred_element_type=jnp.float32
        ).astype(jnp.bfloat16)
        return (attn_out, log_total[..., 0])

    starts = jnp.arange(length // block_rows, dtype=jnp.int32) * block_rows
    outs, totals = lax.map(one_block, starts)
    return (
        outs.reshape(length, head_count, head_width),
        jnp.transpose(totals, (1, 0, 2)).reshape(head_count, length),
    )


def attend_back(queries, key_rows, value_rows, attn_out, log_total, grad_out):
    length, head_count, head_width = queries.shape
    block_rows = min(512, length)
    score_scale = head_width ** (-0.5)
    key_pos = jnp.arange(length, dtype=jnp.int32)
    delta = jnp.sum(grad_out.astype(jnp.float32) * attn_out.astype(jnp.float32), axis=-1)

    def one_block(carried, row_start):
        grad_keys, grad_values = carried
        query_block = lax.dynamic_slice_in_dim(queries, row_start, block_rows, 0)
        grad_block = lax.dynamic_slice_in_dim(grad_out, row_start, block_rows, 0)
        total_block = lax.dynamic_slice_in_dim(log_total, row_start, block_rows, 1)
        delta_block = lax.dynamic_slice_in_dim(delta, row_start, block_rows, 0)
        scores = (
            jnp.einsum("qhd,khd->hqk", query_block, key_rows, preferred_element_type=jnp.float32)
            * score_scale
        )
        query_pos = row_start + jnp.arange(block_rows, dtype=jnp.int32)
        causal = key_pos[None, :] <= query_pos[:, None]
        scores = jnp.where(causal[None], scores, masked_score)
        attn_probs = jnp.exp(scores - total_block[..., None])
        grad_values = grad_values + jnp.einsum(
            "hqk,qhd->khd",
            attn_probs.astype(jnp.bfloat16),
            grad_block,
            preferred_element_type=jnp.float32,
        )
        grad_probs = jnp.einsum(
            "qhd,khd->hqk", grad_block, value_rows, preferred_element_type=jnp.float32
        )
        grad_scores = (attn_probs * (grad_probs - jnp.transpose(delta_block)[:, :, None])).astype(
            jnp.bfloat16
        )
        grad_query = (
            jnp.einsum("hqk,khd->qhd", grad_scores, key_rows, preferred_element_type=jnp.float32)
            * score_scale
        )
        grad_keys = (
            grad_keys
            + jnp.einsum(
                "hqk,qhd->khd", grad_scores, query_block, preferred_element_type=jnp.float32
            )
            * score_scale
        )
        return ((grad_keys, grad_values), grad_query)

    zeros = jnp.zeros((length, head_count, head_width), jnp.float32)
    starts = jnp.arange(length // block_rows, dtype=jnp.int32) * block_rows
    (grad_keys, grad_values), grad_queries = lax.scan(one_block, (zeros, zeros), starts)
    return (grad_queries.reshape(length, head_count, head_width), grad_keys, grad_values)


def column_sums(wide_part, tall_part):
    return (
        lax.psum_scatter(
            wide_part.astype(jnp.bfloat16), "seq", scatter_dimension=2, tiled=True
        ).astype(jnp.float32),
        lax.psum_scatter(
            tall_part.astype(jnp.bfloat16), "seq", scatter_dimension=0, tiled=True
        ).astype(jnp.float32),
    )


def sequence_layer(
    block_float,
    cot_float,
    cot_rows_here,
    input_one,
    normed_one,
    inverse_one,
    weight_slabs,
    norm_set,
    bias_full,
    head_cos,
    head_sin,
    seq_here,
):
    gain_one, gain_two, shift_two = norm_set
    weights = (
        lax.all_gather(weight_slabs[0], "seq", axis=2, tiled=True),
        lax.all_gather(weight_slabs[1], "seq", axis=2, tiled=True),
        lax.all_gather(weight_slabs[2], "seq", axis=0, tiled=True),
        lax.all_gather(weight_slabs[3], "seq", axis=0, tiled=True),
    )
    row_total, model_width = block_float.shape
    qkv_full = weights[0].reshape(model_width, 3 * model_width)
    gate_full = weights[1].reshape(model_width, 2 * FF)
    out_full = weights[2]
    down_full = weights[3]
    groups = lax.axis_size("seq")
    heads_here = HEADS // groups
    cols_here = heads_here * HEAD_DIM
    tok_here = row_total // seq_here
    length = tok_here * groups
    projected = jnp.dot(
        input_one, qkv_full, preferred_element_type=jnp.float32
    ) + bias_full.reshape(3 * model_width)
    projected = projected.reshape(row_total, 3, HEADS, HEAD_DIM)
    local_pos = (lax.axis_index("seq") * tok_here + jnp.arange(tok_here, dtype=jnp.int32)).astype(
        jnp.float32
    )
    cosine, sine_part = rotary_tables(jnp.tile(local_pos, seq_here))
    packed = jnp.stack(
        [
            rotate(projected[:, 0], cosine, sine_part, 1.0),
            rotate(projected[:, 1], cosine, sine_part, 1.0),
            projected[:, 2],
        ],
        axis=1,
    ).astype(jnp.bfloat16)
    packed = packed.reshape(seq_here, tok_here, 3, model_width)
    grouped = lax.all_to_all(packed, "seq", split_axis=3, concat_axis=1, tiled=True).reshape(
        seq_here, length, 3, heads_here, HEAD_DIM
    )

    def forward_one(parts):
        return attend(parts[:, 0], parts[:, 1], parts[:, 2])

    head_out, head_total = lax.map(forward_one, grouped)
    mixed = lax.all_to_all(
        head_out.reshape(seq_here, length, cols_here),
        "seq",
        split_axis=1,
        concat_axis=2,
        tiled=True,
    )
    mixed = mixed.reshape(row_total, model_width)
    residual = block_float + jnp.dot(mixed, out_full, preferred_element_type=jnp.float32)
    norm_two, normed_two, inverse_two = layer_norm(residual, gain_two, shift_two)
    input_two = norm_two.astype(jnp.bfloat16)
    gate_up = jnp.dot(input_two, gate_full, preferred_element_type=jnp.float32)
    gate_part = gate_up[:, :FF]
    up_part = gate_up[:, FF:]
    sigmoid_gate = jax.nn.sigmoid(gate_part)
    silu_gate = gate_part * sigmoid_gate
    hidden = (silu_gate * up_part).astype(jnp.bfloat16)
    block_output = residual + jnp.dot(hidden, down_full, preferred_element_type=jnp.float32)
    grad_down_full = jnp.einsum(
        "tf,td->fd", hidden, cot_rows_here, preferred_element_type=jnp.float32
    )
    grad_hidden = jnp.einsum(
        "td,fd->tf", cot_rows_here, down_full, preferred_element_type=jnp.float32
    )
    grad_gate = grad_hidden * up_part * sigmoid_gate * (1.0 + gate_part * (1.0 - sigmoid_gate))
    grad_up = grad_hidden * silu_gate
    grad_gate_up_rows = jnp.concatenate([grad_gate, grad_up], axis=1).astype(jnp.bfloat16)
    grad_gate_up_full = jnp.einsum(
        "tc,tf->cf", input_two, grad_gate_up_rows, preferred_element_type=jnp.float32
    )
    mlp_cols = column_sums(grad_gate_up_full.reshape(model_width, 2, FF), grad_down_full)
    grad_norm_two = jnp.einsum(
        "tf,cf->tc", grad_gate_up_rows, gate_full, preferred_element_type=jnp.float32
    )
    grad_gain_two = jnp.sum(grad_norm_two * normed_two, axis=0)
    grad_shift_two = jnp.sum(grad_norm_two, axis=0)
    grad_residual = cot_float + norm_back(grad_norm_two, normed_two, inverse_two, gain_two)
    grad_mixed_rows = grad_residual.astype(jnp.bfloat16)
    grad_out = jnp.einsum("tc,td->cd", mixed, grad_mixed_rows, preferred_element_type=jnp.float32)
    grad_mixed = jnp.einsum(
        "td,cd->tc", grad_mixed_rows, out_full, preferred_element_type=jnp.float32
    ).astype(jnp.bfloat16)
    grad_heads = lax.all_to_all(
        grad_mixed.reshape(seq_here, tok_here, model_width),
        "seq",
        split_axis=2,
        concat_axis=1,
        tiled=True,
    )
    grad_heads = grad_heads.reshape(seq_here, length, heads_here, HEAD_DIM)

    def backward_one(parts):
        group, out_part, total_part, grad_part = parts
        grad_query, grad_keys, grad_values = attend_back(
            group[:, 0], group[:, 1], group[:, 2], out_part, total_part, grad_part
        )
        grad_query = rotate(grad_query, head_cos, head_sin, -1.0)
        grad_keys = rotate(grad_keys, head_cos, head_sin, -1.0)
        return jnp.stack([grad_query, grad_keys, grad_values], axis=1).astype(jnp.bfloat16)

    grad_packed = lax.map(backward_one, (grouped, head_out, head_total, grad_heads))
    grad_qkv = lax.all_to_all(
        grad_packed.reshape(seq_here, length, 3, cols_here),
        "seq",
        split_axis=1,
        concat_axis=3,
        tiled=True,
    )
    grad_qkv = grad_qkv.reshape(row_total, 3 * model_width)
    bias_grad = jnp.sum(grad_qkv.astype(jnp.float32), axis=0).reshape(3, model_width)
    grad_qkv_full = jnp.einsum("tc,tf->cf", input_one, grad_qkv, preferred_element_type=jnp.float32)
    grad_norm_one = jnp.einsum("tf,cf->tc", grad_qkv, qkv_full, preferred_element_type=jnp.float32)
    attn_cols = column_sums(grad_qkv_full.reshape(model_width, 3, model_width), grad_out)
    grad_gain_one = jnp.sum(grad_norm_one * normed_one, axis=0)
    grad_shift_one = jnp.sum(grad_norm_one, axis=0)
    input_grad = grad_residual + norm_back(grad_norm_one, normed_one, inverse_one, gain_one)
    return (
        block_output,
        input_grad,
        (grad_gain_one, grad_shift_one, grad_gain_two, grad_shift_two, bias_grad),
        (attn_cols[0], mlp_cols[0], attn_cols[1], mlp_cols[1]),
    )


def local(
    block_input,
    cotangent,
    ln1_gain,
    ln1_bias,
    qkv_weight,
    qkv_bias,
    out_weight,
    ln2_gain,
    ln2_bias,
    gate_up_weight,
    down_weight,
):
    seq_here, tok_here, model_width = block_input.shape
    length = tok_here * lax.axis_size("seq")
    row_total = seq_here * tok_here
    weight_slabs = (
        lax.all_gather(qkv_weight, "fsdp", axis=0, tiled=True),
        lax.all_gather(gate_up_weight, "fsdp", axis=0, tiled=True),
        lax.all_gather(out_weight, "fsdp", axis=1, tiled=True),
        lax.all_gather(down_weight, "fsdp", axis=1, tiled=True),
    )
    smalls = (
        lax.all_gather(ln1_gain, ("fsdp", "seq"), axis=0, tiled=True),
        lax.all_gather(ln1_bias, ("fsdp", "seq"), axis=0, tiled=True),
        lax.all_gather(ln2_gain, ("fsdp", "seq"), axis=0, tiled=True),
        lax.all_gather(ln2_bias, ("fsdp", "seq"), axis=0, tiled=True),
        lax.all_gather(qkv_bias, ("fsdp", "seq"), axis=1, tiled=True),
    )
    gain_one = smalls[0].astype(jnp.float32)
    shift_one = smalls[1].astype(jnp.float32)
    gain_two = smalls[2].astype(jnp.float32)
    shift_two = smalls[3].astype(jnp.float32)
    bias_full = smalls[4].astype(jnp.float32)
    block_float = block_input.reshape(row_total, model_width).astype(jnp.float32)
    cot_rows_here = cotangent.reshape(row_total, model_width)
    cot_float = cot_rows_here.astype(jnp.float32)
    norm_one, normed_one, inverse_one = layer_norm(block_float, gain_one, shift_one)
    input_one = norm_one.astype(jnp.bfloat16)
    head_cos, head_sin = rotary_tables(jnp.arange(length, dtype=jnp.float32))
    norm_set = (gain_one, gain_two, shift_two)
    block_output, input_grad, vector_grads, slab_grads = sequence_layer(
        block_float,
        cot_float,
        cot_rows_here,
        input_one,
        normed_one,
        inverse_one,
        weight_slabs,
        norm_set,
        bias_full,
        head_cos,
        head_sin,
        seq_here,
    )
    slab_sums = (
        lax.psum_scatter(
            slab_grads[0].astype(jnp.bfloat16), "fsdp", scatter_dimension=0, tiled=True
        ).astype(jnp.float32),
        lax.psum_scatter(
            slab_grads[1].astype(jnp.bfloat16), "fsdp", scatter_dimension=0, tiled=True
        ).astype(jnp.float32),
        lax.psum_scatter(
            slab_grads[2].astype(jnp.bfloat16), "fsdp", scatter_dimension=1, tiled=True
        ).astype(jnp.float32),
        lax.psum_scatter(
            slab_grads[3].astype(jnp.bfloat16), "fsdp", scatter_dimension=1, tiled=True
        ).astype(jnp.float32),
    )
    vector_sums = (
        lax.psum_scatter(vector_grads[0], ("fsdp", "seq"), scatter_dimension=0, tiled=True),
        lax.psum_scatter(vector_grads[1], ("fsdp", "seq"), scatter_dimension=0, tiled=True),
        lax.psum_scatter(vector_grads[2], ("fsdp", "seq"), scatter_dimension=0, tiled=True),
        lax.psum_scatter(vector_grads[3], ("fsdp", "seq"), scatter_dimension=0, tiled=True),
        lax.psum_scatter(vector_grads[4], ("fsdp", "seq"), scatter_dimension=1, tiled=True),
    )
    return (
        block_output.astype(jnp.bfloat16).reshape(seq_here, tok_here, model_width),
        input_grad.reshape(seq_here, tok_here, model_width),
        vector_sums[0],
        vector_sums[1],
        slab_sums[0],
        vector_sums[4],
        slab_sums[2],
        vector_sums[2],
        vector_sums[3],
        slab_sums[1],
        slab_sums[3],
    )


def solution(mesh):
    placed = (
        P("fsdp", "seq", None),
        P("fsdp", "seq", None),
        P(("fsdp", "seq")),
        P(("fsdp", "seq")),
        P("fsdp", None, "seq"),
        P(None, ("fsdp", "seq")),
        P("seq", "fsdp"),
        P(("fsdp", "seq")),
        P(("fsdp", "seq")),
        P("fsdp", None, "seq"),
        P("seq", "fsdp"),
    )
    return jax.shard_map(
        local,
        mesh=mesh,
        in_specs=placed,
        out_specs=(
            P("fsdp", "seq", None),
            P("fsdp", "seq", None),
            P(("fsdp", "seq")),
            P(("fsdp", "seq")),
            P("fsdp", None, "seq"),
            P(None, ("fsdp", "seq")),
            P("seq", "fsdp"),
            P(("fsdp", "seq")),
            P(("fsdp", "seq")),
            P("fsdp", None, "seq"),
            P("seq", "fsdp"),
        ),
        check_vma=False,
    )
```

profile of v0, /device:TPU:0, one launch (start us, length us, event | category | flops | bytes accessed | tf_op | source)
XLA Modules:
  0.0 1935.0 jit_solution(10079372093101176569)
XLA Ops:
  11.6 64.7 %all-gather.10.cloned.1.call-done = bf16[2048,3,256]{0,2,1:T(8,128)(2,1)} async-done(((bf16[512,3,256]{0,2,1:T(8,128)(2,1)}), bf16[2048,3,256]{0,2,1:T(8,128)(2,1)}) %all-gather.10.cloned.1.call-update) | async-done | bytes 3145744 | tf_op jit(solution)/shard_map/all_gather | solution.py:299
  76.4 28.2 %all-gather.14.cloned.1.call-done = bf16[256,2048]{1,0:T(8,128)(2,1)} async-done(((bf16[256,512]{1,0:T(8,128)(2,1)}), bf16[256,2048]{1,0:T(8,128)(2,1)}) %all-gather.14.cloned.1.call-update) | async-done | bytes 1048592 | tf_op jit(solution)/shard_map/all_gather | solution.py:301
  104.6 107.6 %all-gather.18.cloned.1.call-done = bf16[2048,2,704]{0,2,1:T(8,128)(2,1)} async-done(((bf16[512,2,704]{0,2,1:T(8,128)(2,1)}), bf16[2048,2,704]{0,2,1:T(8,128)(2,1)}) %all-gather.18.cloned.1.call-update) | async-done | bytes 5767184 | tf_op jit(solution)/shard_map/all_gather | solution.py:300
  212.3 58.7 %all-gather.22.cloned.1.call-done = bf16[704,2048]{1,0:T(8,128)(2,1)} async-done(((bf16[704,512]{1,0:T(8,128)(2,1)}), bf16[704,2048]{1,0:T(8,128)(2,1)}) %all-gather.22.cloned.1.call-update) | async-done | bytes 2883600 | tf_op jit(solution)/shard_map/all_gather | solution.py:302
  271.1 39.2 %all-gather = bf16[32,64,3]{1,2,0:T(4,128)(2,1)S(1)} all-gather(bf16[1,64,3]{1,2,0:T(4,128)(2,1)S(1)} %bitcast.225), channel_id=1, replica_groups=mesh['fsdp'=4,'seq'=8] {'fsdp','seq'}, dimensions={0}, use_global_device_ids=true | all-gather | bytes 12672 | tf_op jit(solution)/shard_map/all_gather | solution.py:309
  311.5 38.5 %all-reduce.9 = (bf16[2048]{0:T(1024)(128)(2,1)S(1)}, bf16[2048]{0:T(1024)(128)(2,1)S(1)}, bf16[2048]{0:T(1024)(128)(2,1)S(1)}, bf16[2048]{0:T(1024)(128)(2,1)S(1)}) all-reduce(bf16[2048]{0:T(1024)(128)(2,1)S(1)} %dynamic-update-slice.1, bf16[2048]{0:T(1024)(128)(2,1)S(1)} %dynamic-update-slice, ...), channel_id=1, replica_groups=mesh['fsdp'=4,'seq'=8] {'fsdp','seq'}, use_global_device_ids=true, to_apply=%add.1 | all-reduce | flops 8192 | bytes 32768
  350.6 47.5 %all-gather.12.cloned.1.call-done = bf16[2048,3,2048]{0,2,1:T(8,128)(2,1)} async-done(((bf16[2048,3,256]{0,2,1:T(8,128)(2,1)}), bf16[2048,3,2048]{0,2,1:T(8,128)(2,1)}) %all-gather.12.cloned.1.call-update) | async-done | bytes 25165840 | tf_op jit(solution)/shard_map/all_gather | solution.py:158
  434.9 40.8 %all-to-all-done = bf16[1,128,3,2048]{1,2,0,3:T(4,128)(2,1)} async-done(((bf16[1,128,3,2048]{1,2,0,3:T(4,128)(2,1)}), bf16[1,128,3,2048]{1,2,0,3:T(4,128)(2,1)}, u32[]{:S(2)}, u32[]{:S(2)}) %all-to-all-start) | async-done | bytes 1572896 | tf_op jit(solution)/shard_map/all_to_all | solution.py:190
  483.4 24.2 %while.46 = (s32[]{:T(128)}, bf16[2,512,4,64]{1,3,2,0:T(8,128)(2,1)}, f32[2,4,512]{2,1,0:T(4,128)S(1)}, s32[2]{0:T(128)S(1)}, bf16[1024,4,64]{0,2,1:T(8,128)(2,1...) while((s32[]{:T(128)}, ...), condition=%wide.region_5.6_spmd.clone, body=%wide.region_2.5_spmd.clone.sunk | while | flops 560593408 | bytes 35197184 | solution.py:72
  544.2 153.9 %all-gather.20.cloned.1.call-done = bf16[2048,2,5632]{0,2,1:T(8,128)(2,1)} async-done(((bf16[2048,2,704]{0,2,1:T(8,128)(2,1)}), bf16[2048,2,5632]{0,2,1:T(8,128)(2,1)}) %all-gather.20.cloned.1.call-update) | async-done | bytes 46137360 | tf_op jit(solution)/shard_map/all_gather | solution.py:159
  698.2 25.0 %fusion.85 = f32[128,11264]{1,0:T(8,128)} fusion(bf16[2048,11264]{0,1:T(8,128)(2,1)} %bitcast.196, f32[128,2048]{1,0:T(8,128)S(1)} %get-tuple-element.294, f32[2048]{0:T(1024)S(1)} %convert_element_type.152, f32[2048]{0:T(1024)S(1)} %convert_element_type.151, f32[128]{0:T(128)S(1)} %add_rsqrt_fusion, f32[128]{0:T(128)S(1)} %broadcast_multiply_fusion.5), kind=kOutput, calls=%fused_computation.161 | convolution fusion | flops 5906890752 | bytes 52970496 | tf_op jit(solution)/shard_map/dot_general | solution.py:209
  723.1 93.3 %all-gather.24.cloned.1.call-done = bf16[5632,2048]{1,0:T(8,128)(2,1)} async-done(((bf16[704,2048]{1,0:T(8,128)(2,1)}), bf16[5632,2048]{1,0:T(8,128)(2,1)}) %all-gather.24.cloned.1.call-update) | async-done | bytes 23068688 | tf_op jit(solution)/shard_map/all_gather | solution.py:161
  925.2 67.4 %while.47 = (s32[]{:T(128)}, f32[1024,4,64]{0,2,1:T(8,128)S(1)}, f32[1024,4,64]{0,2,1:T(8,128)}, f32[2,512,4,64]{1,0,3,2:T(2,128)}, s32[2]{0:T(128)S(1)}, /*inde...) while((s32[]{:T(128)}, f32[1024,4,64]{0,2,1:T(8,128)S(1)}, ...), condition=%wide.region_12.13_spmd.clone, body=%wide.region_11.12_spmd.clone.sunk | while | flops 1365115392 | bytes 143192480 | solution.py:127
  1004.8 52.1 %all_to_all.60 = bf16[1,1024,3,256]{3,2,0,1:T(4,128)(2,1)S(1)} all-to-all(bf16[1,1024,3,256]{3,2,0,1:T(4,128)(2,1)S(1)} %copy.167), channel_id=1, replica_groups=mesh['fsdp'=4,'seq'=8] {'seq'}, dimensions={1} | all-to-all | bytes 3145728 | tf_op jit(solution)/shard_map/all_to_all | solution.py:259
  1073.9 20.4 %convolution_convert_fusion = bf16[2048,11264]{1,0:T(8,128)(2,1)} fusion(bf16[128,5632]{1,0:T(8,128)(2,1)} %get-tuple-element.270, bf16[128,5632]{1,0:T(8,128)(2,1)S(1)} %copy-done.18, f32[128,2048]{1,0:T(8,128)S(1)} %get-tuple-element.294, f32[2048]{0:T(1024)S(1)} %copy-done.17, f32[2048]{0:T(1024)S(1)} %convert_element_type.151, ...), kind=kOutput, calls=%fused_computation.47 | convolution fusion | flops 5935726592 | bytes 50086912 | tf_op jit(solution)/shard_map/tc,tf->cf/dot_general | solution.py:225
  1094.3 62.3 %copy.176 = bf16[2048,11264]{0,1:T(8,128)(2,1)} copy(bf16[2048,11264]{1,0:T(8,128)(2,1)} %convolution_convert_fusion) | data formatting | bytes 92274688 | tf_op jit(solution)/shard_map/convert_element_type | solution.py:134
  1160.8 107.1 %reduce-scatter.12.cloned.1.call-done = bf16[2048,3,256]{2,0,1:T(8,128)(2,1)} async-done(((bf16[2048,3,2048]{2,0,1:T(8,128)(2,1)}), bf16[2048,3,256]{2,0,1:T(8,128)(2,1)}) %reduce-scatter.12.cloned.1.call-update) | async-done | bytes 3145744 | tf_op jit(solution)/shard_map/reduce_scatter | solution.py:133
  1268.0 268.2 %reduce-scatter.20.cloned.1.call-done = bf16[2048,2,704]{0,2,1:T(8,128)(2,1)} async-done(((bf16[2048,2,5632]{0,2,1:T(8,128)(2,1)}), bf16[2048,2,704]{0,2,1:T(8,128)(2,1)}) %reduce-scatter.20.cloned.1.call-update) | async-done | bytes 5767184 | tf_op jit(solution)/shard_map/reduce_scatter | solution.py:133
  1558.5 39.9 %all-reduce.8 = (f32[2048]{0:T(1024)S(1)}, f32[2048]{0:T(1024)S(1)}, f32[2048]{0:T(1024)S(1)}, f32[2048]{0:T(1024)S(1)}) all-reduce(f32[2048]{0:T(1024)S(1)} %get-tuple-element.215, f32[2048]{0:T(1024)S(1)} %get-tuple-element.220, f32[2048]{0:T(1024)S(1)} %copy-done.31, ...), channel_id=2, replica_groups=mesh['fsdp'=4,'seq'=8] {'fsdp','seq'}, use_global_device_ids=true, to_apply=%region_16.17.clone | all-reduce | flops 8192 | bytes 65536
  1602.1 73.7 %reduce-scatter.28.cloned.1.call-done = f32[64,3]{1,0:T(8,128)} async-done(((f32[2048,3]{1,0:T(8,128)}), f32[64,3]{1,0:T(8,128)}) %reduce-scatter.28.cloned.1.call-update) | async-done | bytes 784
  1677.2 23.9 %reduce-scatter.18.cloned.1.call-done = bf16[256,512]{1,0:T(8,128)(2,1)} async-done(((bf16[256,2048]{1,0:T(8,128)(2,1)}), bf16[256,512]{1,0:T(8,128)(2,1)}) %reduce-scatter.18.cloned.1.call-update) | async-done | bytes 262160 | tf_op jit(solution)/shard_map/reduce_scatter | solution.py:344
  1702.9 55.2 %reduce-scatter.26.cloned.1.call-done = bf16[704,512]{1,0:T(8,128)(2,1)} async-done(((bf16[704,2048]{1,0:T(8,128)(2,1)}), bf16[704,512]{1,0:T(8,128)(2,1)}) %reduce-scatter.26.cloned.1.call-update) | async-done | bytes 720912 | tf_op jit(solution)/shard_map/reduce_scatter | solution.py:347
  1760.5 59.9 %reduce-scatter.14.cloned.1.call-done = bf16[512,3,256]{2,0,1:T(8,128)(2,1)} async-done(((bf16[2048,3,256]{2,0,1:T(8,128)(2,1)}), bf16[512,3,256]{2,0,1:T(8,128)(2,1)}) %reduce-scatter.14.cloned.1.call-update) | async-done | bytes 786448 | tf_op jit(solution)/shard_map/reduce_scatter | solution.py:338
  1822.9 102.0 %reduce-scatter.22.cloned.1.call-done = bf16[512,2,704]{0,2,1:T(8,128)(2,1)} async-done(((bf16[2048,2,704]{0,2,1:T(8,128)(2,1)}), bf16[512,2,704]{0,2,1:T(8,128)(2,1)}) %reduce-scatter.22.cloned.1.call-update) | async-done | bytes 1441808 | tf_op jit(solution)/shard_map/reduce_scatter | solution.py:341
  (287 shorter events, 349.9 us)
Async XLA Ops:
  7.2 69.1 %all-gather.10.cloned.1.call-start = ((), (), s32[]{:S(2)}) async-start(), calls=%async_computation.13 | async-start | bytes 3932160 | tf_op jit(solution)/shard_map/all_gather | solution.py:299
  9.5 95.0 %all-gather.14.cloned.1.call-start = ((), (), s32[]{:S(2)}) async-start(), calls=%async_computation.15 | async-start | bytes 1310720 | tf_op jit(solution)/shard_map/all_gather | solution.py:301
  10.3 201.9 %all-gather.18.cloned.1.call-start = ((), (), s32[]{:S(2)}) async-start(), calls=%async_computation.17 | async-start | bytes 7208960 | tf_op jit(solution)/shard_map/all_gather | solution.py:300
  11.0 260.0 %all-gather.22.cloned.1.call-start = ((), (), s32[]{:S(2)}) async-start(), calls=%async_computation.19 | async-start | bytes 3604480 | tf_op jit(solution)/shard_map/all_gather | solution.py:302
  11.6 386.5 %all-gather.12.cloned.1.call-start = ((), (), s32[]{:S(2)}) async-start(), calls=%async_computation.14 | async-start | bytes 28311552 | tf_op jit(solution)/shard_map/all_gather | solution.py:158
  76.3 462.8 %all-gather.16.cloned.1.call-start = ((), (), s32[]{:S(2)}) async-start(), calls=%async_computation.16 | async-start | bytes 9437184 | tf_op jit(solution)/shard_map/all_gather | solution.py:160
  104.6 593.6 %all-gather.20.cloned.1.call-start = ((), (), s32[]{:S(2)}) async-start(), calls=%async_computation.18 | async-start | bytes 51904512 | tf_op jit(solution)/shard_map/all_gather | solution.py:159
  212.2 137.9 %copy-start.3 = (bf16[1,128,2048]{2,1,0:T(8,128)(2,1)S(1)}, bf16[1,128,2048]{2,1,0:T(8,128)(2,1)}, u32[]{:S(2)}) copy-start(bf16[1,128,2048]{2,1,0:T(8,128)(2,1)} %param.15) | copy-start | bytes 1572868
  212.3 604.1 %all-gather.24.cloned.1.call-start = ((), (), s32[]{:S(2)}) async-start(), calls=%async_computation.20 | async-start | bytes 25952256 | tf_op jit(solution)/shard_map/all_gather | solution.py:161
  430.3 45.3 %all-to-all-start = ((bf16[1,128,3,2048]{1,2,0,3:T(4,128)(2,1)}), bf16[1,128,3,2048]{1,2,0,3:T(4,128)(2,1)}, u32[]{:S(2)}, u32[]{:S(2)}) async-start(bf16[1,128,3,2048]{1,2,0,3:T(4,128)(2,1)} %copy.157), calls=%async_computation | async-start | bytes 4194304 | tf_op jit(solution)/shard_map/all_to_all | solution.py:190
  519.1 19.2 all-to-all-start.1
  522.6 637.1 %reduce-scatter.16.cloned.1.call-start = ((), (), s32[]{:S(2)}) async-start(), calls=%async_computation.23 | async-start | bytes 9437184 | tf_op jit(solution)/shard_map/reduce_scatter | solution.py:136
  522.9 175.3 %copy-start.16 = (f32[2048]{0:T(1024)}, f32[2048]{0:T(1024)S(1)}, u32[]{:S(2)}) copy-start(f32[2048]{0:T(1024)S(1)} %convert_element_type.152) | copy-start | bytes 24580
  698.2 118.2 %copy-start.11 = (bf16[1,128,2048]{2,1,0:T(8,128)(2,1)S(1)}, bf16[1,128,2048]{2,1,0:T(8,128)(2,1)}, u32[]{:S(2)}) copy-start(bf16[1,128,2048]{2,1,0:T(8,128)(2,1)} %param.16) | copy-start | bytes 1572868
  858.9 301.4 %reduce-scatter.24.cloned.1.call-start = ((), (), s32[]{:S(2)}) async-start(), calls=%async_computation.27 | async-start | bytes 25952256 | tf_op jit(solution)/shard_map/reduce_scatter | solution.py:136
  899.2 16.4 all-to-all-start.2
  903.3 364.6 %reduce-scatter.12.cloned.1.call-start = ((), (), s32[]{:S(2)}) async-start(), calls=%async_computation.21 | async-start | bytes 28311552 | tf_op jit(solution)/shard_map/reduce_scatter | solution.py:133
  1072.4 463.8 %reduce-scatter.20.cloned.1.call-start = ((), (), s32[]{:S(2)}) async-start(), calls=%async_computation.25 | async-start | bytes 51904512 | tf_op jit(solution)/shard_map/reduce_scatter | solution.py:133
  1156.6 519.2 %reduce-scatter.28.cloned.1.call-start = ((), (), s32[]{:S(2)}) async-start(), calls=%async_computation.29 | async-start | bytes 1081344
  1159.6 541.5 %reduce-scatter.18.cloned.1.call-start = ((), (), s32[]{:S(2)}) async-start(), calls=%async_computation.24 | async-start | bytes 1310720 | tf_op jit(solution)/shard_map/reduce_scatter | solution.py:344
  1160.2 597.9 %reduce-scatter.26.cloned.1.call-start = ((), (), s32[]{:S(2)}) async-start(), calls=%async_computation.28 | async-start | bytes 3604480 | tf_op jit(solution)/shard_map/reduce_scatter | solution.py:347
  1160.8 659.7 %reduce-scatter.14.cloned.1.call-start = ((), (), s32[]{:S(2)}) async-start(), calls=%async_computation.22 | async-start | bytes 3932160 | tf_op jit(solution)/shard_map/reduce_scatter | solution.py:338
  1267.9 268.3 %copy-start.10 = (bf16[128,5632]{1,0:T(8,128)(2,1)S(1)}, bf16[128,5632]{1,0:T(8,128)(2,1)}, u32[]{:S(2)}) copy-start(bf16[128,5632]{1,0:T(8,128)(2,1)} %get-tuple-element.271) | copy-start | bytes 4325380
  1267.9 656.9 %reduce-scatter.22.cloned.1.call-start = ((), (), s32[]{:S(2)}) async-start(), calls=%async_computation.26 | async-start | bytes 7208960 | tf_op jit(solution)/shard_map/reduce_scatter | solution.py:341
  (45 other events, 1011.8 us)
Sparse Core Ops, SparseCore 0:
  10.1 66.1 all-gather.9
  77.9 26.6 all-gather.13
  106.1 106.0 all-gather.17
  213.6 57.3 all-gather.21
  272.8 125.2 all-gather.11
  399.9 71.0 all-gather.15
  472.9 225.2 all-gather.19
  700.0 116.3 all-gather.23
  859.0 76.9 reduce-scatter.15
  939.4 168.8 reduce-scatter.23
  1111.9 155.9 reduce-scatter.11
  1271.4 264.7 reduce-scatter.19
  1539.0 136.7 reduce-scatter.27
  1677.9 23.1 reduce-scatter.17
  1703.3 54.8 reduce-scatter.25
  1760.3 60.1 reduce-scatter.13
  1822.6 102.1 reduce-scatter.21
where the time goes:
time: 1940 us; the launch traced here: 1930 us
  waiting for transfers between devices  1310 us (68%)
  matrix products  207 us (11%)
  blocking collectives  170 us (9%)
  local copies, waits for them, and re-layouts  162 us (8%)
  other arithmetic  46.4 us (2%)
    reduce_scatter x2, waiting for transfers between devices, column_sums(): lax.psum_scatter(wide_part.astype(jnp.bfloat16), 'seq', scatter_dimension...  375 us
    all_gather x1, waiting for transfers between devices, sequence_layer(): lax.all_gather(weight_slabs[1], 'seq', axis=2, tiled=True)  154 us
    all_gather x1, waiting for transfers between devices, local(): lax.all_gather(gate_up_weight, 'fsdp', axis=0, tiled=True)  108 us
    reduce_scatter x1, waiting for transfers between devices, local(): lax.psum_scatter(slab_grads[1].astype(jnp.bfloat16), 'fsdp', scatter_dime...  102 us
    all_gather x1, waiting for transfers between devices, sequence_layer(): lax.all_gather(weight_slabs[3], 'seq', axis=0, tiled=True)  93.3 us
    unnamed x2, blocking collectives  78.3 us
    unnamed x18, waiting for transfers between devices  76.8 us
    all_gather x1, waiting for transfers between devices, local(): lax.all_gather(qkv_weight, 'fsdp', axis=0, tiled=True)  64.7 us
  transfers between devices with their start and end apart: 20, of which 17 were waited for; matrix products, arithmetic and copies ran while one was open for 19% of the time, Pallas kernels for 0%

commit v1 on v0

v1 whole, which is shorter than its diff:
```python
import functools

import jax
import jax.numpy as jnp
from jax import lax
from jax.experimental import pallas as pl
from jax.experimental.pallas import tpu as pltpu
from jax.sharding import PartitionSpec as P

HEADS = 32
HEAD_DIM = 64
FF = 5632
ROTARY = 16


epsilon = 1e-05
masked_score = -1e30


def layer_norm(rows_in, gain, shift):
    center = rows_in - jnp.mean(rows_in, axis=-1, keepdims=True)
    inverse = lax.rsqrt(jnp.mean(center * center, axis=-1, keepdims=True) + epsilon)
    normed = center * inverse
    return (normed * gain + shift, normed, inverse)


def norm_back(grad_rows, normed, inverse, gain):
    scaled = grad_rows * gain
    return inverse * (
        scaled
        - jnp.mean(scaled, axis=-1, keepdims=True)
        - normed * jnp.mean(scaled * normed, axis=-1, keepdims=True)
    )


def rotary_tables(positions):
    half_rot = ROTARY // 2
    frequency = 10000.0 ** (-2.0 * jnp.arange(half_rot, dtype=jnp.float32) / ROTARY)
    angles = positions[:, None] * frequency[None, :]
    angles = jnp.concatenate([angles, angles], axis=1)
    return (jnp.cos(angles)[:, None, :], jnp.sin(angles)[:, None, :])


def rotate(field, cosine, sine_part, direction):
    half_rot = ROTARY // 2
    head_part = field[..., :ROTARY]
    turned = jnp.concatenate([-head_part[..., half_rot:], head_part[..., :half_rot]], axis=-1)
    moved = head_part * cosine + direction * turned * sine_part
    return jnp.concatenate([moved, field[..., ROTARY:]], axis=-1)


def attend(queries, key_rows, value_rows):
    length, head_count, head_width = queries.shape
    block_rows = min(512, length)
    score_scale = head_width ** (-0.5)
    key_pos = jnp.arange(length, dtype=jnp.int32)

    def one_block(row_start):
        query_block = lax.dynamic_slice_in_dim(queries, row_start, block_rows, 0)
        scores = (
            jnp.einsum("qhd,khd->hqk", query_block, key_rows, preferred_element_type=jnp.float32)
            * score_scale
        )
        query_pos = row_start + jnp.arange(block_rows, dtype=jnp.int32)
        causal = key_pos[None, :] <= query_pos[:, None]
        scores = jnp.where(causal[None], scores, masked_score)
        row_max = jnp.max(scores, axis=-1, keepdims=True)
        log_total = row_max + jnp.log(jnp.sum(jnp.exp(scores - row_max), axis=-1, keepdims=True))
        attn_probs = jnp.exp(scores - log_total).astype(jnp.bfloat16)
        attn_out = jnp.einsum(
            "hqk,khd->qhd", attn_probs, value_rows, preferred_element_type=jnp.float32
        ).astype(jnp.bfloat16)
        return (attn_out, log_total[..., 0])

    starts = jnp.arange(length // block_rows, dtype=jnp.int32) * block_rows
    outs, totals = lax.map(one_block, starts)
    return (
        outs.reshape(length, head_count, head_width),
        jnp.transpose(totals, (1, 0, 2)).reshape(head_count, length),
    )


def attend_back(queries, key_rows, value_rows, attn_out, log_total, grad_out):
    length, head_count, head_width = queries.shape
    block_rows = min(512, length)
    score_scale = head_width ** (-0.5)
    key_pos = jnp.arange(length, dtype=jnp.int32)
    delta = jnp.sum(grad_out.astype(jnp.float32) * attn_out.astype(jnp.float32), axis=-1)

    def one_block(carried, row_start):
        grad_keys, grad_values = carried
        query_block = lax.dynamic_slice_in_dim(queries, row_start, block_rows, 0)
        grad_block = lax.dynamic_slice_in_dim(grad_out, row_start, block_rows, 0)
        total_block = lax.dynamic_slice_in_dim(log_total, row_start, block_rows, 1)
        delta_block = lax.dynamic_slice_in_dim(delta, row_start, block_rows, 0)
        scores = (
            jnp.einsum("qhd,khd->hqk", query_block, key_rows, preferred_element_type=jnp.float32)
            * score_scale
        )
        query_pos = row_start + jnp.arange(block_rows, dtype=jnp.int32)
        causal = key_pos[None, :] <= query_pos[:, None]
        scores = jnp.where(causal[None], scores, masked_score)
        attn_probs = jnp.exp(scores - total_block[..., None])
        grad_values = grad_values + jnp.einsum(
            "hqk,qhd->khd",
            attn_probs.astype(jnp.bfloat16),
            grad_block,
            preferred_element_type=jnp.float32,
        )
        grad_probs = jnp.einsum(
            "qhd,khd->hqk", grad_block, value_rows, preferred_element_type=jnp.float32
        )
        grad_scores = (attn_probs * (grad_probs - jnp.transpose(delta_block)[:, :, None])).astype(
            jnp.bfloat16
        )
        grad_query = (
            jnp.einsum("hqk,khd->qhd", grad_scores, key_rows, preferred_element_type=jnp.float32)
            * score_scale
        )
        grad_keys = (
            grad_keys
            + jnp.einsum(
                "hqk,qhd->khd", grad_scores, query_block, preferred_element_type=jnp.float32
            )
            * score_scale
        )
        return ((grad_keys, grad_values), grad_query)

    zeros = jnp.zeros((length, head_count, head_width), jnp.float32)
    starts = jnp.arange(length // block_rows, dtype=jnp.int32) * block_rows
    (grad_keys, grad_values), grad_queries = lax.scan(one_block, (zeros, zeros), starts)
    return (grad_queries.reshape(length, head_count, head_width), grad_keys, grad_values)


MESH = pl.DeviceIdType.MESH
NT = (((1,), (1,)), ((), ()))
TN = (((0,), (0,)), ((), ()))
f32, bf16 = jnp.float32, jnp.bfloat16


def dot_nn(a, b):
    return jnp.dot(a, b, preferred_element_type=f32)


def dot_nt(a, b):
    return lax.dot_general(a, b, NT, preferred_element_type=f32)


def dot_tn(a, b):
    return lax.dot_general(a, b, TN, preferred_element_type=f32)


def remote(src, dst, send_sem, recv_sem, device):
    return pltpu.make_async_remote_copy(
        src_ref=src, dst_ref=dst, send_sem=send_sem, recv_sem=recv_sem,
        device_id=device, device_id_type=MESH)


def line_barrier(f, n):
    barrier = pltpu.get_barrier_semaphore()

    @pl.when(f > 0)
    def _():
        pl.semaphore_signal(barrier, inc=1, device_id={"fsdp": f - 1}, device_id_type=MESH)

    @pl.when(f < n - 1)
    def _():
        pl.semaphore_signal(barrier, inc=1, device_id={"fsdp": f + 1}, device_id_type=MESH)

    pl.semaphore_wait(barrier, (f > 0).astype(jnp.int32) + (f < n - 1).astype(jnp.int32))


class LineGather:
    def __init__(self, f, n, count, own, slot, sems):
        self.f, self.n, self.count, self.own, self.slot = f, n, count, own, slot
        self.send_r, self.recv_r, self.send_l, self.recv_l = sems

    def copy(self, src, p, h, source, rightward):
        f = self.f
        send, recv = (self.send_r, self.recv_r) if rightward else (self.send_l, self.recv_l)
        target = f + 1 if rightward else f - 1
        return remote(src, self.slot(p, source), send.at[p, h], recv.at[p, h], {"fsdp": target})

    def tick(self, t):
        f, n, count = self.f, self.n, self.count

        @pl.when((t >= 0) & (t < count))
        def _():
            @pl.when(f < n - 1)
            def _():
                self.own(t, lambda src: self.copy(src, t, 0, f, True).start())

            @pl.when(f > 0)
            def _():
                self.own(t, lambda src: self.copy(src, t, 0, f, False).start())

        for h in range(1, n):
            p = t - h
            valid = (p >= 0) & (p < count)

            @pl.when(valid & (f - h >= 0))
            def _(p=p, h=h):
                here = self.slot(p, f - h)
                self.copy(here, p, h - 1, f - h, True).wait_recv()

                @pl.when(f < n - 1)
                def _():
                    self.copy(here, p, h, f - h, True).start()

            @pl.when(valid & (f + h <= n - 1))
            def _(p=p, h=h):
                here = self.slot(p, f + h)
                self.copy(here, p, h - 1, f + h, False).wait_recv()

                @pl.when(f > 0)
                def _():
                    self.copy(here, p, h, f + h, False).start()

    def drain(self, p):
        f, n = self.f, self.n
        for h in range(0, n - 1):
            @pl.when((f - h >= 0) & (f < n - 1))
            def _(h=h):
                self.copy(self.slot(p, f - h), p, h, f - h, True).wait_send()

            @pl.when((f + h <= n - 1) & (f > 0))
            def _(h=h):
                self.copy(self.slot(p, f + h), p, h, f + h, False).wait_send()


class LineReduce:
    def __init__(self, f, n, count, block, from_left, from_right, sems, finish):
        self.f, self.n, self.count, self.block = f, n, count, block
        self.from_left, self.from_right, self.finish = from_left, from_right, finish
        self.send_r, self.recv_r, self.send_l, self.recv_l = sems

    def right(self, p, j):
        return remote(self.block(p, j), self.from_left.at[p, j - 1], self.send_r.at[p, j - 1],
                      self.recv_r.at[p, j - 1], {"fsdp": self.f + 1})

    def left(self, p, j):
        return remote(self.block(p, j), self.from_right.at[p, j], self.send_l.at[p, j],
                      self.recv_l.at[p, j], {"fsdp": self.f - 1})

    def tick(self, u):
        f, n, count = self.f, self.n, self.count
        p = u - f

        @pl.when((p >= 0) & (p < count))
        def _():
            for j in range(n - 1, 0, -1):
                @pl.when((f > 0) & (j >= f))
                def _(j=j):
                    self.right(p, j).wait_recv()

                @pl.when((f > 0) & (j > f))
                def _(j=j):
                    here = self.block(p, j)
                    here[...] = (here[...].astype(f32) + self.from_left[p, j - 1].astype(f32)).astype(bf16)

                @pl.when(j > f)
                def _(j=j):
                    self.right(p, j).start()

        q = u - (n - 1 - f)

        @pl.when((q >= 0) & (q < count))
        def _():
            for j in range(0, n - 1):
                @pl.when((f < n - 1) & (j <= f))
                def _(j=j):
                    self.left(q, j).wait_recv()

                @pl.when((f < n - 1) & (j < f))
                def _(j=j):
                    here = self.block(q, j)
                    here[...] = (here[...].astype(f32) + self.from_right[q, j].astype(f32)).astype(bf16)

                @pl.when(j < f)
                def _(j=j):
                    self.left(q, j).start()

        e = u - (n - 1)

        @pl.when((e >= 0) & (e < count))
        def _():
            for j in range(n):
                @pl.when(j > f)
                def _(j=j):
                    self.right(e, j).wait_send()

                @pl.when(j < f)
                def _(j=j):
                    self.left(e, j).wait_send()
            self.finish(e)


def mlp_kernel(n, r, rb, in2_hbm, cot_hbm, wgu_hbm, wd_hbm,
               out_hbm, gin_hbm, ggu_hbm, gd_hbm,
               in2, cot, acc_o, acc_g, w, hid, dga, dup, parts, from_left, from_right,
               stage, load_sems, own_sems, ag_sr, ag_rr, ag_sl, ag_rl, rs_sr, rs_rr, rs_sl, rs_rl,
               stage_sems):
    f = lax.axis_index("fsdp")
    tokens, width = in2.shape
    wz = width // n
    ff = wd_hbm.shape[0]
    nc = ff // r
    count = 3 * nc
    ring = parts.shape[0]
    loads = [pltpu.make_async_copy(in2_hbm, in2, load_sems.at[0]),
             pltpu.make_async_copy(cot_hbm, cot, load_sems.at[1])]
    for c in loads:
        c.start()

    def rows_of(p):
        return pl.ds(pl.multiple_of(p // 3 * r, r), r)

    def own(p, use):
        kind = lax.rem(p, 3)

        @pl.when(kind < 2)
        def _():
            use(wgu_hbm.at[kind, rows_of(p)])

        @pl.when(kind == 2)
        def _():
            use(wd_hbm.at[rows_of(p)])

    def slot(p, source):
        return w.at[p, :, pl.ds(pl.multiple_of(source * wz, wz), wz)]

    def own_copy(p, act):
        own(p, lambda src: act(pltpu.make_async_copy(src, slot(p, f), own_sems.at[p])))

    @pl.loop(0, count)
    def _(p):
        own_copy(p, lambda c: c.start())

    line_barrier(f, n)
    gather = LineGather(f, n, count, own, slot, (ag_sr, ag_rr, ag_sl, ag_rl))

    def block(p, j):
        return parts.at[lax.rem(p, ring), :, pl.ds(j * wz, wz)]

    def stage_out(p, act):
        kind = lax.rem(p, 3)
        sl = lax.rem(p, 2)

        @pl.when(kind < 2)
        def _():
            act(pltpu.make_async_copy(stage.at[sl], ggu_hbm.at[kind, rows_of(p)], stage_sems.at[sl]))

        @pl.when(kind == 2)
        def _():
            act(pltpu.make_async_copy(stage.at[sl], gd_hbm.at[rows_of(p)], stage_sems.at[sl]))

    def finish(p):
        @pl.when(p >= 2)
        def _():
            stage_out(p - 2, lambda c: c.wait())
        sl = lax.rem(p, 2)
        mine = parts.at[lax.rem(p, ring), :, pl.ds(pl.multiple_of(f * wz, wz), wz)]
        stage[sl] = mine[...].astype(f32)

        @pl.when(f > 0)
        def _():
            stage[sl] += from_left[p, jnp.maximum(f - 1, 0)].astype(f32)

        @pl.when(f < n - 1)
        def _():
            stage[sl] += from_right[p, jnp.minimum(f, n - 2)].astype(f32)
        stage_out(p, lambda c: c.start())

    reduce = LineReduce(f, n, count, block, from_left, from_right, (rs_sr, rs_rr, rs_sl, rs_rl), finish)

    acc_o[...] = jnp.zeros_like(acc_o)
    acc_g[...] = jnp.zeros_like(acc_g)

    first = 3 + n - 1

    @pl.loop(0, first)
    def _(t):
        gather.tick(t)

    for c in loads:
        c.wait()

    def compute(c):
        for k in range(3):
            own_copy(3 * c + k, lambda cc: cc.wait())

        @pl.loop(0, tokens // rb)
        def _(i):
            rows = pl.ds(pl.multiple_of(i * rb, rb), rb)
            a = in2[rows, :]
            gate = dot_nt(a, w[3 * c])
            up = dot_nt(a, w[3 * c + 1])
            gh = dot_nt(cot[rows, :], w[3 * c + 2])
            sig = jax.nn.sigmoid(gate)
            silu = gate * sig
            h = (silu * up).astype(bf16)
            dg = (gh * up * sig * (1.0 + gate * (1.0 - sig))).astype(bf16)
            du = (gh * silu).astype(bf16)
            hid[rows, :] = h
            dga[rows, :] = dg
            dup[rows, :] = du
            acc_o[rows, :] = (acc_o[rows, :].astype(f32) + dot_nn(h, w[3 * c + 2])).astype(acc_o.dtype)
            acc_g[rows, :] = (acc_g[rows, :].astype(f32) + dot_nn(dg, w[3 * c]) + dot_nn(du, w[3 * c + 1])).astype(acc_g.dtype)

        for k, (small, big) in enumerate(((dga, in2), (dup, in2), (hid, cot))):
            for j in range(n):
                block(3 * c + k, j)[...] = dot_tn(small[...], big[:, pl.ds(j * wz, wz)]).astype(bf16)

    @pl.loop(0, nc)
    def _(c):
        compute(c)

        @pl.loop(0, 3)
        def _(k):
            gather.tick(3 * c + k + first)
            reduce.tick(3 * c + k)

    in2[...] = acc_o[...].astype(bf16)
    cot[...] = acc_g[...].astype(bf16)
    stores = [pltpu.make_async_copy(in2, out_hbm, load_sems.at[0]),
              pltpu.make_async_copy(cot, gin_hbm, load_sems.at[1])]
    for c in stores:
        c.start()

    @pl.loop(0, n - 1)
    def _(k):
        reduce.tick(count + k)

    @pl.loop(0, count)
    def _(p):
        gather.drain(p)
    for p in (count - 2, count - 1):
        stage_out(jnp.int32(p), lambda c: c.wait())
    for c in stores:
        c.wait()


def piece_rows(ff):
    r = 0
    for cand in range(16, 257, 16):
        if ff % cand == 0:
            r = cand
    return r


def mlp(in2, cot, wgu, wd, n, cid):
    tokens, width = in2.shape
    ff, wz = wd.shape
    r = piece_rows(ff)
    rb = min(256, tokens)
    nc = ff // r
    count = 3 * nc
    ring = min(count, 3 * ((n - 1 + 2) // 3) + 3)
    any_spec = pl.BlockSpec(memory_space=pl.ANY)
    acc_dtype = f32 if tokens * width * 8 <= 20 * 2**20 else bf16
    D = pltpu.SemaphoreType.DMA
    return pl.pallas_call(
        functools.partial(mlp_kernel, n, r, rb),
        out_shape=(
            jax.ShapeDtypeStruct((tokens, width), bf16),
            jax.ShapeDtypeStruct((tokens, width), bf16),
            jax.ShapeDtypeStruct((2, ff, wz), f32),
            jax.ShapeDtypeStruct((ff, wz), f32),
        ),
        in_specs=[any_spec] * 4,
        out_specs=[any_spec] * 4,
        scratch_shapes=[
            pltpu.VMEM((tokens, width), bf16),
            pltpu.VMEM((tokens, width), bf16),
            pltpu.VMEM((tokens, width), acc_dtype),
            pltpu.VMEM((tokens, width), acc_dtype),
            pltpu.VMEM((count, r, width), bf16),
            pltpu.VMEM((tokens, r), bf16),
            pltpu.VMEM((tokens, r), bf16),
            pltpu.VMEM((tokens, r), bf16),
            pltpu.VMEM((ring, r, width), bf16),
            pltpu.VMEM((count, n - 1, r, wz), bf16),
            pltpu.VMEM((count, n - 1, r, wz), bf16),
            pltpu.VMEM((2, r, wz), f32),
            D((2,)),
            D((count,)),
        ] + [D((count, n - 1))] * 8 + [D((2,))],
        compiler_params=pltpu.CompilerParams(
            collective_id=cid, has_side_effects=True, vmem_limit_bytes=64 * 1024 * 1024 - 65536),
        name="mlp",
    )(in2, cot, wgu, wd)


def gather_rows(rows):
    return lax.all_gather(rows, "seq", axis=0, tiled=True)


def scatter_rows(partial):
    return lax.psum_scatter(
        partial.astype(jnp.bfloat16), "seq", scatter_dimension=0, tiled=True
    ).astype(jnp.float32)


def scatter_weight(grad, axis):
    return lax.psum_scatter(
        grad.astype(jnp.bfloat16), "fsdp", scatter_dimension=axis, tiled=True
    ).astype(jnp.float32)


def local(
    block_input,
    cotangent,
    ln1_gain,
    ln1_bias,
    qkv_weight,
    qkv_bias,
    out_weight,
    ln2_gain,
    ln2_bias,
    gate_up_weight,
    down_weight,
):
    seq_here, tok_here, model_width = block_input.shape
    groups = lax.axis_size("seq")
    length = tok_here * groups
    heads_here = HEADS // groups
    cols_here = heads_here * HEAD_DIM
    ff_here = FF // groups
    small = jnp.concatenate(
        [
            ln1_gain[None],
            ln1_bias[None],
            ln2_gain[None],
            ln2_bias[None],
            qkv_bias,
        ],
        axis=0,
    )
    small_full = lax.all_gather(small, ("fsdp", "seq"), axis=1, tiled=True).astype(jnp.float32)
    gain_one, shift_one, gain_two, shift_two = [small_full[i] for i in range(4)]
    head_start = lax.axis_index("seq") * cols_here
    bias_here = lax.dynamic_slice_in_dim(small_full[4:], head_start, cols_here, 1)

    qkv_full = lax.all_gather(qkv_weight, "fsdp", axis=0, tiled=True)
    out_full = lax.all_gather(out_weight, "fsdp", axis=1, tiled=True)
    qkv_full = qkv_full.reshape(model_width, 3 * cols_here)

    block_float = block_input[0].astype(jnp.float32)
    cot_here = cotangent[0]
    cot_float = cot_here.astype(jnp.float32)
    norm_one, normed_one, inverse_one = layer_norm(block_float, gain_one, shift_one)
    in_one = gather_rows(norm_one.astype(jnp.bfloat16))
    cot_all = gather_rows(cot_here)

    projected = jnp.dot(in_one, qkv_full, preferred_element_type=jnp.float32) + bias_here.reshape(
        3 * cols_here
    )
    projected = projected.reshape(length, 3, heads_here, HEAD_DIM)
    cosine, sine_part = rotary_tables(jnp.arange(length, dtype=jnp.float32))
    queries = rotate(projected[:, 0], cosine, sine_part, 1.0).astype(jnp.bfloat16)
    key_rows = rotate(projected[:, 1], cosine, sine_part, 1.0).astype(jnp.bfloat16)
    value_rows = projected[:, 2].astype(jnp.bfloat16)
    head_out, head_total = attend(queries, key_rows, value_rows)
    mixed = head_out.reshape(length, cols_here)
    residual = block_float + scatter_rows(
        jnp.dot(mixed, out_full, preferred_element_type=jnp.float32)
    )
    norm_two, normed_two, inverse_two = layer_norm(residual, gain_two, shift_two)
    in_two = gather_rows(norm_two.astype(jnp.bfloat16))
    out_sum, grad_sum, grad_gate_up, grad_down = mlp(
        in_two,
        cot_all,
        jnp.transpose(gate_up_weight, (1, 2, 0)),
        down_weight,
        lax.axis_size("fsdp"),
        0,
    )
    grad_gate_up = jnp.transpose(grad_gate_up, (2, 0, 1))
    block_output = residual + scatter_rows(out_sum)
    grad_norm_two = scatter_rows(grad_sum)
    grad_gain_two = jnp.sum(grad_norm_two * normed_two, axis=0)
    grad_shift_two = jnp.sum(grad_norm_two, axis=0)
    grad_residual = cot_float + norm_back(grad_norm_two, normed_two, inverse_two, gain_two)
    grad_rows = gather_rows(grad_residual.astype(jnp.bfloat16))
    grad_mixed = jnp.einsum(
        "td,cd->tc", grad_rows, out_full, preferred_element_type=jnp.float32
    ).astype(jnp.bfloat16)
    grad_out = scatter_weight(
        jnp.einsum("tc,td->cd", mixed, grad_rows, preferred_element_type=jnp.float32), 1
    )
    grad_query, grad_keys, grad_values = attend_back(
        queries,
        key_rows,
        value_rows,
        head_out,
        head_total,
        grad_mixed.reshape(length, heads_here, HEAD_DIM),
    )
    grad_query = rotate(grad_query, cosine, sine_part, -1.0)
    grad_keys = rotate(grad_keys, cosine, sine_part, -1.0)
    grad_qkv = (
        jnp.stack([grad_query, grad_keys, grad_values], axis=1)
        .astype(jnp.bfloat16)
        .reshape(length, 3 * cols_here)
    )
    bias_grad = jnp.sum(grad_qkv.astype(jnp.float32), axis=0).reshape(3, cols_here)
    grad_norm_one = scatter_rows(
        jnp.einsum("tf,cf->tc", grad_qkv, qkv_full, preferred_element_type=jnp.float32)
    )
    grad_qkv_weight = scatter_weight(
        jnp.einsum("tc,tf->cf", in_one, grad_qkv, preferred_element_type=jnp.float32).reshape(
            model_width, 3, cols_here
        ),
        0,
    )
    grad_gain_one = jnp.sum(grad_norm_one * normed_one, axis=0)
    grad_shift_one = jnp.sum(grad_norm_one, axis=0)
    input_grad = grad_residual + norm_back(grad_norm_one, normed_one, inverse_one, gain_one)
    bias_wide = lax.dynamic_update_slice_in_dim(
        jnp.zeros((3, model_width), jnp.float32), bias_grad, head_start, 1
    )
    vectors = jnp.concatenate(
        [
            grad_gain_one[None],
            grad_shift_one[None],
            grad_gain_two[None],
            grad_shift_two[None],
            bias_wide,
        ],
        axis=0,
    )
    vectors = lax.psum_scatter(vectors, ("fsdp", "seq"), scatter_dimension=1, tiled=True)
    return (
        block_output.astype(jnp.bfloat16)[None],
        input_grad[None],
        vectors[0],
        vectors[1],
        grad_qkv_weight,
        vectors[4:],
        grad_out,
        vectors[2],
        vectors[3],
        grad_gate_up,
        grad_down,
    )


def solution(mesh):
    placed = (
        P("fsdp", "seq", None),
        P("fsdp", "seq", None),
        P(("fsdp", "seq")),
        P(("fsdp", "seq")),
        P("fsdp", None, "seq"),
        P(None, ("fsdp", "seq")),
        P("seq", "fsdp"),
        P(("fsdp", "seq")),
        P(("fsdp", "seq")),
        P("fsdp", None, "seq"),
        P("seq", "fsdp"),
    )
    return jax.shard_map(
        local,
        mesh=mesh,
        in_specs=placed,
        out_specs=(
            P("fsdp", "seq", None),
            P("fsdp", "seq", None),
            P(("fsdp", "seq")),
            P(("fsdp", "seq")),
            P("fsdp", None, "seq"),
            P(None, ("fsdp", "seq")),
            P("seq", "fsdp"),
            P(("fsdp", "seq")),
            P(("fsdp", "seq")),
            P("fsdp", None, "seq"),
            P("seq", "fsdp"),
        ),
        check_vma=False,
    )
```

time: 1940 us -> 1010 us (0.52)
  waiting for transfers between devices: 1310 us -> 551 us
  Pallas kernels: 0 us -> 237 us
  matrix products: 207 us -> 68.8 us
  blocking collectives: 170 us -> 45 us
  local copies, waits for them, and re-layouts: 162 us -> 44.5 us
    all_gather x8 -> x6, waiting for transfers between devices: 554 us -> 161 us  [the longest x4 146 us: gather_rows(): return lax.all_gather(rows, 'seq', axis=0, tiled=True)]
    reduce_scatter x8 -> x6, waiting for transfers between devices: 616 us -> 251 us  [the longest x4 191 us: scatter_rows(): lax.psum_scatter(partial.astype(jnp.bfloat16), 'seq', scatter_dimension=0...]
    pallas_call x0 -> x1, Pallas kernels: none -> 237 us  [mlp(): pl.pallas_call(functools.partial(mlp_kernel, n, r, rb), out_shape=(jax.Sh...]
    dot_general x12 -> x6, matrix products: 162 us -> 32.8 us  [the longest x1 7.44 us: local(): jnp.einsum('tc,tf->cf', in_one, grad_qkv, preferred_element_type=jnp.floa...]
    unnamed x2 -> x0, blocking collectives: 78.3 us -> none
    all_to_all x3 -> x0, waiting for transfers between devices: 66.9 us -> none  [the longest x1 40.8 us: sequence_layer(): lax.all_to_all(packed, 'seq', split_axis=3, concat_axis=1, tiled=True)]
    unnamed x18 -> x14, waiting for transfers between devices: 76.8 us -> 139 us
    convert_element_type x1 -> x2, local copies, waits for them, and re-layouts: 62.3 us -> 0.96 us  [the longest x1 0.87 us: local(): value_rows = projected[:, 2].astype(jnp.bfloat16)]
  transfers between devices with their start and end apart: 20 -> 13, of which waited for: 17 -> 11; matrix products, arithmetic and copies ran while one was open for 19% -> 12% of each run, Pallas kernels for 0% -> 0%
where the time goes in v1:
time: 1010 us; the launch traced here: 1000 us
  waiting for transfers between devices  551 us (55%)
  Pallas kernels  237 us (23%)
  matrix products  68.8 us (7%)
  blocking collectives  45 us (4%)
  local copies, waits for them, and re-layouts  44.5 us (4%)
  other arithmetic  33.7 us (3%)
  between operations  15 us (1%)
    pallas_call x1, Pallas kernels, mlp(): pl.pallas_call(functools.partial(mlp_kernel, n, r, rb), out_shape=(jax.Sh...  237 us
    reduce_scatter x4, waiting for transfers between devices, scatter_rows(): lax.psum_scatter(partial.astype(jnp.bfloat16), 'seq', scatter_dimension=0...  191 us
    all_gather x4, waiting for transfers between devices, gather_rows(): return lax.all_gather(rows, 'seq', axis=0, tiled=True)  146 us
    unnamed x14, waiting for transfers between devices  139 us
    reduce_scatter x2, waiting for transfers between devices, scatter_weight(): lax.psum_scatter(grad.astype(jnp.bfloat16), 'fsdp', scatter_dimension=axi...  59.3 us
    all_gather x1, blocking collectives, local(): lax.all_gather(small, ('fsdp', 'seq'), axis=1, tiled=True)  45 us
    dynamic_update_slice x4, local copies, waits for them, and re-layouts, attend_back(): lax.scan(one_block, (zeros, zeros), starts)  21.9 us
  transfers between devices with their start and end apart: 13, of which 11 were waited for; matrix products, arithmetic and copies ran while one was open for 12% of the time, Pallas kernels for 0%

profile of v1, /device:TPU:0, one launch (start us, length us, event | category | flops | bytes accessed | tf_op | source)
XLA Modules:
  0.0 1003.1 jit_solution(17754360520084802774)
XLA Ops:
  10.4 45.0 %all-gather.1 = bf16[32,64,7]{1,2,0:T(8,128)(2,1)S(1)} all-gather(bf16[1,64,7]{1,2,0:T(8,128)(2,1)S(1)} %bitcast.234), channel_id=1, replica_groups=mesh['fsdp'=4,'seq'=8] {'fsdp','seq'}, dimensions={0}, use_global_device_ids=true | all-gather | bytes 29568 | tf_op jit(solution)/shard_map/all_gather | solution.py:539
  61.1 15.3 %all-gather.11.cloned.1.call-done = bf16[2048,3,256]{0,2,1:T(8,128)(2,1)} async-done(((bf16[512,3,256]{0,2,1:T(8,128)(2,1)}), bf16[2048,3,256]{0,2,1:T(8,128)(2,1)}) %all-gather.11.cloned.1.call-update) | async-done | bytes 3145744 | tf_op jit(solution)/shard_map/all_gather | solution.py:544
  76.4 37.8 %all-gather.9.cloned.1.call-done = bf16[1024,2048]{1,0:T(8,128)(2,1)} async-done(((bf16[128,2048]{1,0:T(8,128)(2,1)}), bf16[1024,2048]{1,0:T(8,128)(2,1)}) %all-gather.9.cloned.1.call-update) | async-done | bytes 4194320 | tf_op jit(solution)/shard_map/all_gather | solution.py:495
  114.2 6.2 convolution_add_fusion
  121.8 22.6 %while.28 = (s32[]{:T(128)}, bf16[2,512,4,64]{1,3,2,0:T(8,128)(2,1)S(1)}, f32[2,4,512]{2,1,0:T(4,128)S(1)}, s32[2]{0:T(128)S(1)}, bf16[1024,4,64]{0,2,1:T(8,128)...) while((s32[]{:T(128)}, ...), condition=%wide.region_5.6_spmd.clone, body=%wide.region_2.5_spmd.clone.sunk | while | flops 560593408 | bytes 28905644 | solution.py:76
  145.3 4.7 convolution_convert_fusion
  150.7 50.6 %reduce-scatter.10.cloned.1.call-done = bf16[128,2048]{1,0:T(8,128)(2,1)} async-done(((bf16[1024,2048]{1,0:T(8,128)(2,1)}), bf16[128,2048]{1,0:T(8,128)(2,1)}) %reduce-scatter.10.cloned.1.call-update) | async-done | bytes 524304 | tf_op jit(solution)/shard_map/reduce_scatter | solution.py:499
  206.2 33.5 %all-gather.19.cloned.1.call-done = bf16[1,1024,2048]{2,1,0:T(8,128)(2,1)} async-done(((bf16[1,128,2048]{2,1,0:T(8,128)(2,1)}), bf16[1,1024,2048]{2,1,0:T(8,128)(2,1)}) %all-gather.19.cloned.1.call-update) | async-done | bytes 4194320 | tf_op jit(solution)/shard_map/all_gather | solution.py:495
  239.7 38.9 %all-gather.15.cloned.1.call-done.in2_hbm = bf16[1024,2048]{1,0:T(8,128)(2,1)} async-done(((bf16[128,2048]{1,0:T(8,128)(2,1)}), bf16[1024,2048]{1,0:T(8,128)(2,1)}) %all-gather.15.cloned.1.call-update) | async-done | bytes 4194320 | tf_op jit(solution)/shard_map/all_gather | solution.py:495
  278.6 236.5 %mlp.1 = (bf16[1024,2048]{1,0:T(8,128)(2,1)}, bf16[1024,2048]{1,0:T(8,128)(2,1)}, f32[2,704,512]{2,1,0:T(8,128)}, f32[704,512]{1,0:T(8,128)}) custom-call(bf16[1024,2048]{1,0:T(8,128)(2,1)} %all-gather.15.cloned.1.call-done.in2_hbm, bf16[1024,2048]{1,0:T(8,128)(2,1)} %bitcast.204, bf16[2,704,512]{2,1,0:T(8,128)(2,1)} %bitcast.214, bf16[704,512]{1,0:T(8,128)(2,1)} %wd_hbm.1), custom_call_target="tpu_custom_call" | custom-call | tf_op jit(solution)/shard_map/mlp/pallas_call | solution.py:462
  515.3 48.5 %reduce-scatter.14.cloned.1.call-done = bf16[128,2048]{1,0:T(8,128)(2,1)} async-done(((bf16[1024,2048]{1,0:T(8,128)(2,1)}), bf16[128,2048]{1,0:T(8,128)(2,1)}) %reduce-scatter.14.cloned.1.call-update) | async-done | bytes 524304 | tf_op jit(solution)/shard_map/reduce_scatter | solution.py:499
  569.3 35.5 %all-gather.17.cloned.1.call-done = bf16[1024,2048]{1,0:T(8,128)(2,1)} async-done(((bf16[128,2048]{1,0:T(8,128)(2,1)}), bf16[1024,2048]{1,0:T(8,128)(2,1)}) %all-gather.17.cloned.1.call-update) | async-done | bytes 4194320 | tf_op jit(solution)/shard_map/all_gather | solution.py:495
  609.4 4.9 multiply_reduce_fusion
  614.4 54.8 %while.29 = (s32[]{:T(128)}, f32[1024,4,64]{0,2,1:T(8,128)S(1)}, f32[1024,4,64]{0,2,1:T(8,128)}, f32[2,512,4,64]{1,0,3,2:T(2,128)}, s32[2]{0:T(128)S(1)}, /*inde...) while((s32[]{:T(128)}, f32[1024,4,64]{0,2,1:T(8,128)S(1)}, ...), condition=%wide.region_15.16_spmd.clone, body=%wide.region_14.15_spmd.clone.sunk | while | flops 1365115392 | bytes 50917632 | solution.py:131
  623.1 4.8 multiply_convert_fusion.2
  630.9 10.4 %dynamic_update_slice.27 = f32[2,512,4,64]{1,0,3,2:T(2,128)} dynamic-update-slice(f32[2,512,4,64]{1,0,3,2:T(2,128)} %get-tuple-element.431, f32[1,512,4,64]{1,0,3,2:T(1,128)S(1)} %copy.71, s32[]{:T(128)S(6)} %copy.88, s32[]{:T(128)} %constant.40.clone.1..sunk.1, s32[]{:T(128)} %constant.40.clone.1..sunk.1, s32[]{:T(128)} %constant.40.clone.1..sunk.1) | dynamic-update-slice | bytes 1048580 | tf_op jit(solution)/shard_map/while/body/jit(dynamic_update_index_in_dim)/dynamic_update_slice | solution.py:131
  651.0 4.8 multiply_convert_fusion.2
  658.8 10.4 %dynamic_update_slice.27 = f32[2,512,4,64]{1,0,3,2:T(2,128)} dynamic-update-slice(f32[2,512,4,64]{1,0,3,2:T(2,128)} %get-tuple-element.431, f32[1,512,4,64]{1,0,3,2:T(1,128)S(1)} %copy.71, s32[]{:T(128)S(6)} %copy.88, s32[]{:T(128)} %constant.40.clone.1..sunk.1, s32[]{:T(128)} %constant.40.clone.1..sunk.1, s32[]{:T(128)} %constant.40.clone.1..sunk.1) | dynamic-update-slice | bytes 1048580 | tf_op jit(solution)/shard_map/while/body/jit(dynamic_update_index_in_dim)/dynamic_update_slice | solution.py:131
  673.7 5.1 convolution_convert_fusion.1
  679.8 7.4 fusion.41
  689.5 40.6 %reduce-scatter.16.cloned.1.call-done = bf16[128,2048]{1,0:T(8,128)(2,1)} async-done(((bf16[1024,2048]{1,0:T(8,128)(2,1)}), bf16[128,2048]{1,0:T(8,128)(2,1)}) %reduce-scatter.16.cloned.1.call-update) | async-done | bytes 524304 | tf_op jit(solution)/shard_map/reduce_scatter | solution.py:499
  733.1 51.6 %reduce-scatter.12.cloned.1.call-done = bf16[128,2048]{1,0:T(8,128)(2,1)} async-done(((bf16[1024,2048]{1,0:T(8,128)(2,1)}), bf16[128,2048]{1,0:T(8,128)(2,1)}) %reduce-scatter.12.cloned.1.call-update) | async-done | bytes 524304 | tf_op jit(solution)/shard_map/reduce_scatter | solution.py:499
  788.0 59.2 %reduce-scatter.18.cloned.1.call-done = bf16[512,3,256]{2,0,1:T(8,128)(2,1)} async-done(((bf16[2048,3,256]{2,0,1:T(8,128)(2,1)}), bf16[512,3,256]{2,0,1:T(8,128)(2,1)}) %reduce-scatter.18.cloned.1.call-update) | async-done | bytes 786448 | tf_op jit(solution)/shard_map/reduce_scatter | solution.py:505
  849.7 136.9 %reduce-scatter.22.cloned.1.call-done = f32[64,7]{1,0:T(8,128)} async-done(((f32[2048,7]{1,0:T(8,128)}), f32[64,7]{1,0:T(8,128)}) %reduce-scatter.22.cloned.1.call-update) | async-done | bytes 1808
  (211 shorter events, 91.5 us)
Async XLA Ops:
  7.2 51.0 %copy-start.2 = (bf16[1,128,2048]{2,1,0:T(8,128)(2,1)S(1)}, bf16[1,128,2048]{2,1,0:T(8,128)(2,1)}, u32[]{:S(2)}) copy-start(bf16[1,128,2048]{2,1,0:T(8,128)(2,1)} %param.15) | copy-start | bytes 1572868
  7.2 69.3 %all-gather.11.cloned.1.call-start = ((), (), s32[]{:S(2)}) async-start(), calls=%async_computation.8 | async-start | bytes 3932160 | tf_op jit(solution)/shard_map/all_gather | solution.py:544
  9.6 104.6 %all-gather.9.cloned.1.call-start = ((), (), s32[]{:S(2)}) async-start(), calls=%async_computation.7 | async-start | bytes 4718592 | tf_op jit(solution)/shard_map/all_gather | solution.py:495
  58.2 145.8 %copy-start.19 = (f32[1,2048]{1,0:T(1,128)}, f32[1,2048]{1,0:T(1,128)S(1)}, u32[]{:S(2)}) copy-start(f32[1,2048]{1,0:T(1,128)S(1)} %get-tuple-element.253) | copy-start | bytes 24580
  59.4 85.9 %all-gather.13.cloned.1.call-start = ((), (), s32[]{:S(2)}) async-start(), calls=%async_computation.9 | async-start | bytes 1310720 | tf_op jit(solution)/shard_map/all_gather | solution.py:545
  60.1 141.2 %reduce-scatter.10.cloned.1.call-start = ((), (), s32[]{:S(2)}) async-start(), calls=%async_computation.10 | async-start | bytes 4718592 | tf_op jit(solution)/shard_map/reduce_scatter | solution.py:499
  61.1 60.5 %copy-start.16 = (f32[1024,16]{0,1:T(8,128)}, f32[1024,16]{0,1:T(8,128)S(1)}, u32[]{:S(2)}) copy-start(f32[1024,16]{0,1:T(8,128)S(1)} %get-tuple-element.261) | copy-start | bytes 196612
  150.1 89.6 %all-gather.19.cloned.1.call-start = ((), (), s32[]{:S(2)}) async-start(), calls=%async_computation.18 | async-start | bytes 4718592 | tf_op jit(solution)/shard_map/all_gather | solution.py:495
  150.6 128.0 %all-gather.15.cloned.1.call-start = ((), (), s32[]{:S(2)}) async-start(), calls=%async_computation.11 | async-start | bytes 4718592 | tf_op jit(solution)/shard_map/all_gather | solution.py:495
  206.1 357.7 %reduce-scatter.14.cloned.1.call-start = ((), (), s32[]{:S(2)}) async-start(), calls=%async_computation.13 | async-start | bytes 4718592 | tf_op jit(solution)/shard_map/reduce_scatter | solution.py:499
  515.2 52.8 %copy-start.14 = (bf16[2,512,4,64]{1,3,2,0:T(8,128)(2,1)S(1)}, bf16[2,512,4,64]{1,3,2,0:T(8,128)(2,1)}, u32[]{:S(2)}) copy-start(bf16[2,512,4,64]{1,3,2,0:T(8,128)(2,1)} %copy-done.13) | copy-start | bytes 1572868
  515.3 89.5 %copy-start.12 = (bf16[32,8,2,512]{3,1,2,0:T(8,128)(2,1)S(1)}, bf16[32,8,2,512]{3,1,2,0:T(8,128)(2,1)}, u32[]{:S(2)}) copy-start(bf16[32,8,2,512]{3,1,2,0:T(8,128)(2,1)} %copy-done.11) | copy-start | bytes 1572868
  515.3 89.5 %all-gather.17.cloned.1.call-start = ((), (), s32[]{:S(2)}) async-start(), calls=%async_computation.14 | async-start | bytes 4718592 | tf_op jit(solution)/shard_map/all_gather | solution.py:495
  568.0 119.5 %reduce-scatter.20.cloned.1.call-start = ((), (), s32[]{:S(2)}) async-start(), calls=%async_computation.17 | async-start | bytes 1310720 | tf_op jit(solution)/shard_map/reduce_scatter | solution.py:505
  609.2 120.9 %reduce-scatter.16.cloned.1.call-start = ((), (), s32[]{:S(2)}) async-start(), calls=%async_computation.15 | async-start | bytes 4718592 | tf_op jit(solution)/shard_map/reduce_scatter | solution.py:499
  678.8 105.9 %reduce-scatter.12.cloned.1.call-start = ((), (), s32[]{:S(2)}) async-start(), calls=%async_computation.12 | async-start | bytes 4718592 | tf_op jit(solution)/shard_map/reduce_scatter | solution.py:499
  679.5 167.8 %reduce-scatter.18.cloned.1.call-start = ((), (), s32[]{:S(2)}) async-start(), calls=%async_computation.16 | async-start | bytes 3932160 | tf_op jit(solution)/shard_map/reduce_scatter | solution.py:505
  679.8 50.3 %copy-start.22 = (f32[1,2048]{1,0:T(1,128)S(1)}, f32[1,2048]{1,0:T(1,128)}, u32[]{:S(2)}) copy-start(f32[1,2048]{1,0:T(1,128)} %copy-done.21) | copy-start | bytes 24580
  679.8 50.3 %copy-start.28 = (f32[128]{0:T(128)S(1)}, f32[128]{0:T(128)}, u32[]{:S(2)}) copy-start(f32[128]{0:T(128)} %copy-done.27) | copy-start | bytes 1540
  687.3 97.4 %copy-start.7 = (bf16[128,2048]{1,0:T(8,128)(2,1)S(1)}, bf16[128,2048]{1,0:T(8,128)(2,1)}, u32[]{:S(2)}) copy-start(bf16[128,2048]{1,0:T(8,128)(2,1)} %reduce-scatter.10.cloned.1.call-done) | copy-start | bytes 1572868
  687.3 97.4 %copy-start.9 = (bf16[1,128,2048]{2,1,0:T(8,128)(2,1)S(1)}, bf16[1,128,2048]{2,1,0:T(8,128)(2,1)}, u32[]{:S(2)}) copy-start(bf16[1,128,2048]{2,1,0:T(8,128)(2,1)} %param.16) | copy-start | bytes 1572868
  687.3 97.4 %copy-start.10 = (bf16[128,2048]{1,0:T(8,128)(2,1)S(1)}, bf16[128,2048]{1,0:T(8,128)(2,1)}, u32[]{:S(2)}) copy-start(bf16[128,2048]{1,0:T(8,128)(2,1)} %reduce-scatter.14.cloned.1.call-done) | copy-start | bytes 1572868
  687.3 299.3 %reduce-scatter.22.cloned.1.call-start = ((), (), s32[]{:S(2)}) async-start(), calls=%async_computation.19 | async-start | bytes 1081344
  788.0 207.1 %copy-start.15 = (f32[704,512]{1,0:T(8,128)S(1)}, f32[704,512]{1,0:T(8,128)}, u32[]{:S(2)}) copy-start(f32[704,512]{1,0:T(8,128)} %get-tuple-element.477) | copy-start | bytes 4325380
  (27 other events, 415.7 us)
Sparse Core Ops, SparseCore 0:
  10.1 66.2 all-gather.10
  78.9 35.2 all-gather.8
  115.8 27.9 all-gather.12
  150.2 51.1 reduce-scatter.9
  203.1 36.5 all-gather.18
  242.0 36.5 all-gather.14
  515.4 48.3 reduce-scatter.13
  568.1 36.5 all-gather.16
  609.3 27.2 reduce-scatter.19
  678.9 51.1 reduce-scatter.15
  733.5 51.1 reduce-scatter.11
  786.8 60.3 reduce-scatter.17
  850.1 136.4 reduce-scatter.21

commit v2 on v1

v2 whole, which is shorter than its diff:
```python
import functools

import jax
import jax.numpy as jnp
from jax import lax
from jax.experimental import pallas as pl
from jax.experimental.pallas import tpu as pltpu
from jax.sharding import PartitionSpec as P

HEAD_DIM = 64
ROTARY = 16

epsilon = 1e-05
masked_score = -1e30

MESH = pl.DeviceIdType.MESH
NT = (((1,), (1,)), ((), ()))
TN = (((0,), (0,)), ((), ()))
f32, bf16 = jnp.float32, jnp.bfloat16


def dot_nn(a, b):
    return jnp.dot(a, b, preferred_element_type=f32)


def dot_nt(a, b):
    return lax.dot_general(a, b, NT, preferred_element_type=f32)


def dot_tn(a, b):
    return lax.dot_general(a, b, TN, preferred_element_type=f32)


def remote(src, dst, send_sem, recv_sem, device):
    return pltpu.make_async_remote_copy(
        src_ref=src, dst_ref=dst, send_sem=send_sem, recv_sem=recv_sem,
        device_id=device, device_id_type=MESH)


def line_barrier(f, n):
    barrier = pltpu.get_barrier_semaphore()

    @pl.when(f > 0)
    def _():
        pl.semaphore_signal(barrier, inc=1, device_id={"fsdp": f - 1}, device_id_type=MESH)

    @pl.when(f < n - 1)
    def _():
        pl.semaphore_signal(barrier, inc=1, device_id={"fsdp": f + 1}, device_id_type=MESH)

    pl.semaphore_wait(barrier, (f > 0).astype(jnp.int32) + (f < n - 1).astype(jnp.int32))


def when(condition):
    if isinstance(condition, (bool, int)):
        return (lambda body: body()) if condition else (lambda body: None)
    return pl.when(condition)


class LineGather:
    def __init__(self, f, n, count, own, slot, sems):
        self.f, self.n, self.count, self.own, self.slot = f, n, count, own, slot
        self.send_r, self.recv_r, self.send_l, self.recv_l = sems

    def copy(self, src, p, h, source, rightward):
        f = self.f
        send, recv = (self.send_r, self.recv_r) if rightward else (self.send_l, self.recv_l)
        target = f + 1 if rightward else f - 1
        return remote(src, self.slot(p, source), send.at[p, h], recv.at[p, h], {"fsdp": target})

    def tick(self, t):
        f, n, count = self.f, self.n, self.count

        @when((t >= 0) & (t < count))
        def _():
            @pl.when(f < n - 1)
            def _():
                self.own(t, lambda src: self.copy(src, t, 0, f, True).start())

            @pl.when(f > 0)
            def _():
                self.own(t, lambda src: self.copy(src, t, 0, f, False).start())

        for h in range(1, n):
            self.arrive(t - h, h)

    def arrive(self, p, h):
        f, n = self.f, self.n

        @when((p >= 0) & (p < self.count))
        def _():
            @pl.when(f - h >= 0)
            def _():
                here = self.slot(p, f - h)
                self.copy(here, p, h - 1, f - h, True).wait_recv()
                if h < n - 1:
                    @pl.when(f < n - 1)
                    def _():
                        self.copy(here, p, h, f - h, True).start()

            @pl.when(f + h <= n - 1)
            def _():
                here = self.slot(p, f + h)
                self.copy(here, p, h - 1, f + h, False).wait_recv()
                if h < n - 1:
                    @pl.when(f > 0)
                    def _():
                        self.copy(here, p, h, f + h, False).start()

    def drain(self, p):
        f, n = self.f, self.n
        for h in range(0, n - 1):
            @pl.when((f - h >= 0) & (f < n - 1))
            def _(h=h):
                self.copy(self.slot(p, f - h), p, h, f - h, True).wait_send()

            @pl.when((f + h <= n - 1) & (f > 0))
            def _(h=h):
                self.copy(self.slot(p, f + h), p, h, f + h, False).wait_send()


class LineReduce:
    def __init__(self, f, n, count, block, from_left, from_right, sems, finish):
        self.f, self.n, self.count, self.block = f, n, count, block
        self.from_left, self.from_right, self.finish = from_left, from_right, finish
        self.send_r, self.recv_r, self.send_l, self.recv_l = sems

    def right(self, p, j):
        return remote(self.block(p, j), self.from_left.at[p, j - 1], self.send_r.at[p, j - 1],
                      self.recv_r.at[p, j - 1], {"fsdp": self.f + 1})

    def left(self, p, j):
        return remote(self.block(p, j), self.from_right.at[p, j], self.send_l.at[p, j],
                      self.recv_l.at[p, j], {"fsdp": self.f - 1})

    def tick(self, u):
        f, n, count = self.f, self.n, self.count
        p = u - f

        @pl.when((p >= 0) & (p < count))
        def _():
            for j in range(n - 1, 0, -1):
                @pl.when((f > 0) & (j >= f))
                def _(j=j):
                    self.right(p, j).wait_recv()

                @pl.when((f > 0) & (j > f))
                def _(j=j):
                    here = self.block(p, j)
                    here[...] = (here[...].astype(f32) + self.from_left[p, j - 1].astype(f32)).astype(bf16)

                @pl.when(j > f)
                def _(j=j):
                    self.right(p, j).start()

        q = u - (n - 1 - f)

        @pl.when((q >= 0) & (q < count))
        def _():
            for j in range(0, n - 1):
                @pl.when((f < n - 1) & (j <= f))
                def _(j=j):
                    self.left(q, j).wait_recv()

                @pl.when((f < n - 1) & (j < f))
                def _(j=j):
                    here = self.block(q, j)
                    here[...] = (here[...].astype(f32) + self.from_right[q, j].astype(f32)).astype(bf16)

                @pl.when(j < f)
                def _(j=j):
                    self.left(q, j).start()

        e = u - (n - 1)

        @pl.when((e >= 0) & (e < count))
        def _():
            for j in range(n):
                @pl.when(j > f)
                def _(j=j):
                    self.right(e, j).wait_send()

                @pl.when(j < f)
                def _(j=j):
                    self.left(e, j).wait_send()
            self.finish(e)


def mlp_kernel(n, r, rb, in2_hbm, cot_hbm, wgu_hbm, wd_hbm,
               out_hbm, gin_hbm, ggu_hbm, gd_hbm,
               in2, cot, acc_o, acc_g, w, hid, dga, dup, parts, from_left, from_right,
               stage, load_sems, own_sems, ag_sr, ag_rr, ag_sl, ag_rl, rs_sr, rs_rr, rs_sl, rs_rl,
               stage_sems):
    f = lax.axis_index("fsdp")
    tokens, width = in2.shape
    wz = width // n
    ff = wd_hbm.shape[0]
    nc = ff // r
    count = 3 * nc
    ring = parts.shape[0]
    loads = [pltpu.make_async_copy(in2_hbm, in2, load_sems.at[0]),
             pltpu.make_async_copy(cot_hbm, cot, load_sems.at[1])]
    for c in loads:
        c.start()

    def rows_of(p):
        return pl.ds(pl.multiple_of(p // 3 * r, r), r)

    def own(p, use):
        kind = lax.rem(p, 3)

        @pl.when(kind < 2)
        def _():
            use(wgu_hbm.at[kind, rows_of(p)])

        @pl.when(kind == 2)
        def _():
            use(wd_hbm.at[rows_of(p)])

    def slot(p, source):
        return w.at[p, :, pl.ds(pl.multiple_of(source * wz, wz), wz)]

    def own_copy(p, act):
        own(p, lambda src: act(pltpu.make_async_copy(src, slot(p, f), own_sems.at[p])))

    @pl.loop(0, count)
    def _(p):
        own_copy(p, lambda c: c.start())

    line_barrier(f, n)
    gather = LineGather(f, n, count, own, slot, (ag_sr, ag_rr, ag_sl, ag_rl))

    def block(p, j):
        return parts.at[lax.rem(p, ring), :, pl.ds(j * wz, wz)]

    def stage_out(p, act):
        kind = lax.rem(p, 3)
        sl = lax.rem(p, 2)

        @pl.when(kind < 2)
        def _():
            act(pltpu.make_async_copy(stage.at[sl], ggu_hbm.at[kind, rows_of(p)], stage_sems.at[sl]))

        @pl.when(kind == 2)
        def _():
            act(pltpu.make_async_copy(stage.at[sl], gd_hbm.at[rows_of(p)], stage_sems.at[sl]))

    def finish(p):
        @pl.when(p >= 2)
        def _():
            stage_out(p - 2, lambda c: c.wait())
        sl = lax.rem(p, 2)
        mine = parts.at[lax.rem(p, ring), :, pl.ds(pl.multiple_of(f * wz, wz), wz)]
        stage[sl] = mine[...].astype(f32)

        @pl.when(f > 0)
        def _():
            stage[sl] += from_left[p, jnp.maximum(f - 1, 0)].astype(f32)

        @pl.when(f < n - 1)
        def _():
            stage[sl] += from_right[p, jnp.minimum(f, n - 2)].astype(f32)
        stage_out(p, lambda c: c.start())

    reduce = LineReduce(f, n, count, block, from_left, from_right, (rs_sr, rs_rr, rs_sl, rs_rl), finish)

    acc_o[...] = jnp.zeros_like(acc_o)
    acc_g[...] = jnp.zeros_like(acc_g)

    first = 3 + n - 1

    @pl.loop(0, first)
    def _(t):
        gather.tick(t)

    for c in loads:
        c.wait()

    def compute(c):
        for k in range(3):
            own_copy(3 * c + k, lambda cc: cc.wait())

        @pl.loop(0, tokens // rb)
        def _(i):
            rows = pl.ds(pl.multiple_of(i * rb, rb), rb)
            a = in2[rows, :]
            gate = dot_nt(a, w[3 * c])
            up = dot_nt(a, w[3 * c + 1])
            gh = dot_nt(cot[rows, :], w[3 * c + 2])
            sig = jax.nn.sigmoid(gate)
            silu = gate * sig
            h = (silu * up).astype(bf16)
            dg = (gh * up * sig * (1.0 + gate * (1.0 - sig))).astype(bf16)
            du = (gh * silu).astype(bf16)
            hid[rows, :] = h
            dga[rows, :] = dg
            dup[rows, :] = du
            acc_o[rows, :] = (acc_o[rows, :].astype(f32) + dot_nn(h, w[3 * c + 2])).astype(acc_o.dtype)
            acc_g[rows, :] = (acc_g[rows, :].astype(f32) + dot_nn(dg, w[3 * c]) + dot_nn(du, w[3 * c + 1])).astype(acc_g.dtype)

        for k, (small, big) in enumerate(((dga, in2), (dup, in2), (hid, cot))):
            for j in range(n):
                block(3 * c + k, j)[...] = dot_tn(small[...], big[:, pl.ds(j * wz, wz)]).astype(bf16)

    @pl.loop(0, nc)
    def _(c):
        compute(c)

        @pl.loop(0, 3)
        def _(k):
            gather.tick(3 * c + k + first)
            reduce.tick(3 * c + k)

    in2[...] = acc_o[...].astype(bf16)
    cot[...] = acc_g[...].astype(bf16)
    stores = [pltpu.make_async_copy(in2, out_hbm, load_sems.at[0]),
              pltpu.make_async_copy(cot, gin_hbm, load_sems.at[1])]
    for c in stores:
        c.start()

    @pl.loop(0, n - 1)
    def _(k):
        reduce.tick(count + k)

    @pl.loop(0, count)
    def _(p):
        gather.drain(p)
    for p in (count - 2, count - 1):
        stage_out(jnp.int32(p), lambda c: c.wait())
    for c in stores:
        c.wait()


def piece_rows(ff):
    r = 0
    for cand in range(16, 257, 16):
        if ff % cand == 0:
            r = cand
    return r


def mlp(in2, cot, wgu, wd, n, cid):
    tokens, width = in2.shape
    ff, wz = wd.shape
    r = piece_rows(ff)
    rb = min(256, tokens)
    nc = ff // r
    count = 3 * nc
    ring = min(count, 3 * ((n - 1 + 2) // 3) + 3)
    any_spec = pl.BlockSpec(memory_space=pl.ANY)
    acc_dtype = f32 if tokens * width * 8 <= 20 * 2**20 else bf16
    D = pltpu.SemaphoreType.DMA
    return pl.pallas_call(
        functools.partial(mlp_kernel, n, r, rb),
        out_shape=(
            jax.ShapeDtypeStruct((tokens, width), bf16),
            jax.ShapeDtypeStruct((tokens, width), bf16),
            jax.ShapeDtypeStruct((2, ff, wz), f32),
            jax.ShapeDtypeStruct((ff, wz), f32),
        ),
        in_specs=[any_spec] * 4,
        out_specs=[any_spec] * 4,
        scratch_shapes=[
            pltpu.VMEM((tokens, width), bf16),
            pltpu.VMEM((tokens, width), bf16),
            pltpu.VMEM((tokens, width), acc_dtype),
            pltpu.VMEM((tokens, width), acc_dtype),
            pltpu.VMEM((count, r, width), bf16),
            pltpu.VMEM((tokens, r), bf16),
            pltpu.VMEM((tokens, r), bf16),
            pltpu.VMEM((tokens, r), bf16),
            pltpu.VMEM((ring, r, width), bf16),
            pltpu.VMEM((count, n - 1, r, wz), bf16),
            pltpu.VMEM((count, n - 1, r, wz), bf16),
            pltpu.VMEM((2, r, wz), f32),
            D((2,)),
            D((count,)),
        ] + [D((count, n - 1))] * 8 + [D((2,))],
        compiler_params=pltpu.CompilerParams(
            collective_id=cid, has_side_effects=True, vmem_limit_bytes=64 * 1024 * 1024 - 65536),
        name="mlp",
    )(in2, cot, wgu, wd)


LANES = 128
PER = LANES // HEAD_DIM


def xor(a, b, count):
    total = 0
    bit = 1
    while bit < count:
        x, y = (a // bit) % 2, (b // bit) % 2
        total = total + bit * (x + y - 2 * x * y)
        bit *= 2
    return total


def everyone_barrier(me, nf, ns):
    barrier = pltpu.get_barrier_semaphore()
    total = nf * ns

    @pl.loop(1, total)
    def _(k):
        t = lax.rem(me + k, total)
        pl.semaphore_signal(barrier, inc=1, device_id={"fsdp": t // ns, "seq": lax.rem(t, ns)},
                            device_id_type=MESH)
    pl.semaphore_wait(barrier, total - 1)


class RowGather:
    def __init__(self, s, m, tok, buf, sems):
        self.j, self.c, self.m, self.tok, self.buf = s // 2, s % 2, m, tok, buf
        self.send_o, self.recv_o, self.send_s, self.recv_s = sems

    def slot(self, chip, core):
        row = (chip * 2 + core) * self.tok
        return self.buf.at[pl.ds(pl.multiple_of(row, self.tok), self.tok)]

    def off(self, src, d, chip):
        return remote(src, self.slot(chip, self.c), self.send_o.at[d], self.recv_o.at[d],
                      {"seq": xor(self.j, d, self.m) * 2 + self.c})

    def sib(self, src, d, core):
        return remote(src, self.slot(xor(self.j, d, self.m), core), self.send_s.at[d], self.recv_s.at[d],
                      {"seq": self.j * 2 + 1 - self.c})

    def start(self, src):
        for d in range(1, self.m):
            self.off(src, d, self.j).start()
        self.sib(src, 0, self.c).start()

    def relay(self, d):
        chip = xor(self.j, d, self.m)
        here = self.slot(chip, self.c)
        self.off(here, d, chip).wait_recv()
        self.sib(here, d, self.c).start()

    def finish(self):
        for d in range(self.m):
            self.sib(self.slot(xor(self.j, d, self.m), 1 - self.c), d, 1 - self.c).wait_recv()

    def drain(self, src):
        for d in range(1, self.m):
            self.off(src, d, self.j).wait_send()
            chip = xor(self.j, d, self.m)
            self.sib(self.slot(chip, self.c), d, self.c).wait_send()
        self.sib(src, 0, self.c).wait_send()


class RowReduce:
    def __init__(self, s, m, from_sib, from_off, sems):
        self.j, self.c, self.m = s // 2, s % 2, m
        self.from_sib, self.from_off = from_sib, from_off
        self.send_s, self.recv_s, self.send_o, self.recv_o = sems

    def sib(self, src, d):
        return remote(src, self.from_sib.at[d], self.send_s.at[d], self.recv_s.at[d],
                      {"seq": self.j * 2 + 1 - self.c})

    def off(self, d):
        return remote(self.from_sib.at[d], self.from_off.at[d - 1], self.send_o.at[d], self.recv_o.at[d],
                      {"seq": xor(self.j, d, self.m) * 2 + self.c})

    def give(self, d, src):
        self.sib(src, d).start()

    def pass_on(self, d, own):
        here = self.from_sib.at[d]
        self.sib(here, d).wait_recv()
        here[...] = (own.astype(f32) + here[...].astype(f32)).astype(bf16)
        self.off(d).start()

    def total(self, own):
        here = self.from_sib.at[0]
        self.sib(here, 0).wait_recv()
        value = own.astype(f32) + here[...].astype(f32)
        for d in range(self.m - 1, 0, -1):
            self.off(d).wait_recv()
            value = value + self.from_off[d - 1].astype(f32)
        return value

    def drain(self, src_of):
        for d in range(self.m):
            self.sib(src_of(d), d).wait_send()
        for d in range(1, self.m):
            self.off(d).wait_send()


def normed_rows(x):
    center = x - jnp.mean(x, axis=-1, keepdims=True)
    inverse = lax.rsqrt(jnp.mean(center * center, axis=-1, keepdims=True) + epsilon)
    return center * inverse, inverse


def lane_of(shape):
    return lax.broadcasted_iota(jnp.int32, shape, len(shape) - 1)


def rotary_tiles(rows, first):
    half = ROTARY // 2
    lane = lane_of((rows, LANES))
    pos = (first + lax.broadcasted_iota(jnp.int32, (rows, LANES), 0)).astype(f32)
    within = lane % HEAD_DIM
    freq = jnp.zeros((rows, LANES), f32)
    for i in range(half):
        freq = jnp.where(within % half == i, float(10000.0 ** (-2.0 * i / ROTARY)), freq)
    angle = pos * freq
    turned = within < ROTARY
    cosine = jnp.where(turned, jnp.cos(angle), 1.0)
    sine = jnp.where(turned, jnp.sin(angle), 0.0)
    return cosine, sine


def turn(u, cosine, sine, direction):
    half = ROTARY // 2
    within = lane_of(u.shape) % HEAD_DIM
    ahead = pltpu.roll(u, LANES - half, 1)
    behind = pltpu.roll(u, half, 1)
    turned = jnp.where(within < half, -ahead, behind)
    return u * cosine + direction * turned * sine


def front_kernel(nf, ns,
                 x_hbm, cot_hbm, g1, b1, g2, b2, qb, wqkv_hbm, wo_hbm,
                 in1_hbm, cotall_hbm, in2_hbm, qkv_hbm, att_hbm, lse_hbm, res_hbm, wq_hbm, woall_hbm,
                 vec_hbm, cos_hbm, sin_hbm,
                 x, in1, tile, tiles, vecs, wq, wo, qkv, att, lse, cos, sin, part, keep, give,
                 from_sib, from_off, res, in2,
                 load_sems, own_sems, small_s, small_r,
                 ag_sr, ag_rr, ag_sl, ag_rl,
                 a_so, a_ro, a_ss, a_rs, c_so, c_ro, c_ss, c_rs, e_so, e_ro, e_ss, e_rs,
                 r_ss, r_rs, r_so, r_ro, out_sems):
    f, s = lax.axis_index("fsdp"), lax.axis_index("seq")
    total = nf * ns
    me = f * ns + s
    m = ns // 2
    j, c = s // 2, s % 2
    tok, width = x.shape
    length = in1.shape[0]
    cols = qkv.shape[2]
    wz = width // nf
    pairs = cols // LANES
    block_rows = 2 * tok
    load = pltpu.make_async_copy(x_hbm, x, load_sems.at[0])
    load.start()

    def own(p, use):
        use(wqkv_hbm.at[p] if p < 3 else wo_hbm)

    def slot(p, source):
        if p < 3:
            return wq.at[p, pl.ds(pl.multiple_of(source * wz, wz), wz)]
        return wo.at[:, pl.ds(pl.multiple_of(source * wz, wz), wz)]

    def own_copy(p):
        box = []
        own(p, lambda src: box.append(pltpu.make_async_copy(src, slot(p, f), own_sems.at[p])))
        return box[0]

    for p in range(4):
        own_copy(p).start()
    cot_rows = pl.ds(pl.multiple_of(s * tok, tok), tok)
    cot_own = pltpu.make_async_copy(cot_hbm, cotall_hbm.at[cot_rows], load_sems.at[1])

    w = g1.shape[1]
    spread = LANES // w
    here = lane_of((1, LANES)) // w == lax.rem(me, spread)
    tile[...] = jnp.zeros_like(tile)
    for row, piece in enumerate((g1[...], b1[...], g2[...], b2[...], qb[0:1, :], qb[1:2, :], qb[2:3, :])):
        wide = jnp.concatenate([piece.astype(f32)] * spread, axis=1)
        tile[row:row + 1, :] = jnp.where(here, wide, 0.0)

    everyone_barrier(me, nf, ns)
    gather = LineGather(f, nf, 4, own, slot, (ag_sr, ag_rr, ag_sl, ag_rl))
    gather.tick(0)

    def small(k):
        t = lax.rem(me + k, total)
        return remote(tile, tiles.at[k], small_s.at[k], small_r.at[k], {"fsdp": t // ns, "seq": lax.rem(t, ns)})

    @pl.loop(1, total)
    def _(k):
        small(k).start()
    cot_own.start()
    tiles[0] = tile[...]
    for q in range(length // block_rows):
        rows = pl.ds(q * block_rows, block_rows)
        cos[rows, :], sin[rows, :] = rotary_tiles(block_rows, q * block_rows)
    stores = [pltpu.make_async_copy(cos, cos_hbm, out_sems.at[0]), pltpu.make_async_copy(sin, sin_hbm, out_sems.at[1])]
    for st in stores:
        st.start()

    @pl.loop(1, total)
    def _(k):
        small(k).wait_recv()
    vecs[...] = jnp.zeros_like(vecs)

    @pl.loop(0, total)
    def _(k):
        source = lax.rem(me + total - k, total)
        lanes = pl.ds(pl.multiple_of(source // spread * LANES, LANES), LANES)
        vecs[:, lanes] += tiles[k]

    def store(ref, hbm, i):
        st = pltpu.make_async_copy(ref, hbm, out_sems.at[i])
        st.start()
        stores.append(st)

    store(vecs, vec_hbm, 2)
    load.wait()
    normed, _ = normed_rows(x[...].astype(f32))
    mine = pl.ds(pl.multiple_of(s * tok, tok), tok)
    in1[mine, :] = (normed * vecs[0:1, :] + vecs[1:2, :]).astype(bf16)
    rows_in = RowGather(s, m, tok, in1, (a_so, a_ro, a_ss, a_rs))
    rows_in.start(in1.at[mine])
    rows_cot = RowGather(s, m, tok, cotall_hbm, (c_so, c_ro, c_ss, c_rs))
    rows_cot.start(cot_hbm)
    gather.tick(1)
    for d in range(1, m):
        rows_in.relay(d)
        if d == 2:
            gather.tick(2)
    if m <= 2:
        gather.tick(2)
    rows_in.finish()
    store(in1, in1_hbm, 3)
    bias_at = pl.ds(pl.multiple_of(s * cols, LANES), cols)

    def project(k):
        own_copy(k).wait()

        @pl.loop(0, length // block_rows)
        def _(q):
            rows = pl.ds(pl.multiple_of(q * block_rows, block_rows), block_rows)
            value = dot_nn(in1[rows, :], wq[k]) + vecs[4 + k:5 + k, bias_at]
            for g in range(pairs):
                lanes = slice(g * LANES, (g + 1) * LANES)
                u = value[:, lanes]
                if k < 2:
                    u = turn(u, cos[rows, :], sin[rows, :], 1.0)
                qkv[k, rows, lanes] = u.astype(bf16)

    relays = list(range(1, m))
    last = 2
    for k in range(3):
        while last < k + nf - 1:
            last += 1
            gather.tick(last)
        project(k)
        if relays:
            rows_cot.relay(relays.pop(0))
    while last < 3 + nf - 1:
        last += 1
        gather.tick(last)
    own_copy(3).wait()
    while relays:
        rows_cot.relay(relays.pop(0))
    store(qkv, qkv_hbm, 4)
    store(wq, wq_hbm, 5)
    store(wo, woall_hbm, 6)

    def attend(b):
        rows = pl.ds(b * block_rows, block_rows)

        @pl.loop(0, pairs)
        def _(g):
            lanes = pl.ds(pl.multiple_of(g * LANES, LANES), LANES)
            q, kd, vd = qkv[0, rows, lanes], qkv[1, rows, lanes], qkv[2, rows, lanes]
            lane = lane_of((block_rows, LANES))
            seen = lane_of((block_rows, block_rows)) <= lax.broadcasted_iota(jnp.int32, (block_rows, block_rows), 0)
            out = jnp.zeros((block_rows, LANES), f32)
            logs = lse[rows, :]
            for h in range(PER):
                head = lane // HEAD_DIM == h
                qm = jnp.where(head, q.astype(f32) * HEAD_DIM ** -0.5, 0.0).astype(bf16)
                sd = jnp.where(seen, dot_nt(qm, kd), masked_score)
                top = jnp.max(sd, axis=1, keepdims=True)
                if b > 0:
                    before = pl.ds(0, b * block_rows)
                    sl = dot_nt(qm, qkv[1, before, lanes])
                    top = jnp.maximum(top, jnp.max(sl, axis=1, keepdims=True))
                ed = jnp.exp(sd - top)
                tot = jnp.sum(ed, axis=1, keepdims=True)
                if b > 0:
                    el = jnp.exp(sl - top)
                    tot = tot + jnp.sum(el, axis=1, keepdims=True)
                inv = 1.0 / tot
                value = dot_nn((ed * inv).astype(bf16), vd)
                if b > 0:
                    value = value + dot_nn((el * inv).astype(bf16), qkv[2, before, lanes])
                out = jnp.where(head, value, out)
                logs = jnp.where(lane == g * PER + h, top + jnp.log(tot), logs)
            att[rows, lanes] = out.astype(bf16)
            lse[rows, :] = logs

    lse[...] = jnp.zeros_like(lse)
    sums = RowReduce(s, m, from_sib, from_off, (r_ss, r_rs, r_so, r_ro))

    @pl.loop(0, m)
    def _(step):
        d = m - 1 - step
        chip = xor(j, d, m)
        for b in range(m):
            @pl.when(chip == b)
            def _(b=b):
                attend(b)
        rows = pl.ds(pl.multiple_of(chip * block_rows, block_rows), block_rows)
        part[...] = dot_nn(att[rows, :], wo[...])
        give[d] = part[pl.ds(pl.multiple_of((1 - c) * tok, tok), tok), :].astype(bf16)
        keep[d] = part[pl.ds(pl.multiple_of(c * tok, tok), tok), :]
        sums.give(d, give.at[d])

        @pl.when(step > 0)
        def _():
            sums.pass_on(d + 1, keep[d + 1])
    store(att, att_hbm, 7)
    store(lse, lse_hbm, 8)
    rows_cot.finish()
    res[...] = x[...].astype(f32) + sums.total(keep[0])
    store(res, res_hbm, 9)
    normed, _ = normed_rows(res[...])
    in2[...] = (normed * vecs[2:3, :] + vecs[3:4, :]).astype(bf16)
    rows_two = RowGather(s, m, tok, in2_hbm, (e_so, e_ro, e_ss, e_rs))
    rows_two.start(in2)
    in2_own = pltpu.make_async_copy(in2, in2_hbm.at[mine], load_sems.at[2])
    in2_own.start()
    for d in range(1, m):
        rows_two.relay(d)
    rows_two.finish()

    @pl.loop(1, total)
    def _(k):
        small(k).wait_send()
    for p in range(4):
        gather.drain(p)
    rows_in.drain(in1.at[mine])
    rows_cot.drain(cot_hbm)
    rows_two.drain(in2)
    sums.drain(lambda d: give.at[d])
    cot_own.wait()
    in2_own.wait()
    for st in stores:
        st.wait()


def front(x, cot, g1, b1, g2, b2, qb, wqkv, wo, nf, ns, cid):
    tok, width = x.shape
    cols, wz = wo.shape
    length = tok * ns
    m = ns // 2
    w = g1.shape[1]
    D, V = pltpu.SemaphoreType.DMA, pltpu.VMEM
    A = pl.BlockSpec(memory_space=pl.ANY)
    M = pl.BlockSpec(memory_space=pltpu.VMEM)
    S = jax.ShapeDtypeStruct
    return pl.pallas_call(
        functools.partial(front_kernel, nf, ns),
        out_shape=(
            S((length, width), bf16), S((length, width), bf16), S((length, width), bf16),
            S((3, length, cols), bf16), S((length, cols), bf16), S((length, LANES), f32),
            S((tok, width), f32), S((3, width, cols), bf16), S((cols, width), bf16),
            S((8, width), f32), S((length, LANES), f32), S((length, LANES), f32),
        ),
        in_specs=[A, A, M, M, M, M, M, A, A],
        out_specs=[A] * 12,
        scratch_shapes=[
            V((tok, width), bf16), V((length, width), bf16), V((8, LANES), f32), V((nf * ns, 8, LANES), f32),
            V((8, width), f32), V((3, width, cols), bf16), V((cols, width), bf16), V((3, length, cols), bf16),
            V((length, cols), bf16), V((length, LANES), f32), V((length, LANES), f32), V((length, LANES), f32),
            V((2 * tok, width), f32), V((m, tok, width), f32), V((m, tok, width), bf16),
            V((m, tok, width), bf16), V((m - 1, tok, width), bf16), V((tok, width), f32), V((tok, width), bf16),
            D((3,)), D((4,)), D((nf * ns,)), D((nf * ns,)),
        ] + [D((4, nf - 1))] * 4 + [D((m,))] * 16 + [D((10,))],
        compiler_params=pltpu.CompilerParams(
            collective_id=cid, has_side_effects=True, vmem_limit_bytes=64 * 1024 * 1024 - 65536),
        name="front",
    )(x, cot, g1, b1, g2, b2, qb, wqkv, wo)


def back_kernel(nf, ns,
                gsum_hbm, osum_hbm, res_hbm, cot_hbm, x_hbm, vec_hbm, qkv_hbm, att_hbm, lse_hbm, in1_hbm, wq_hbm, wo_hbm,
                cos_hbm, sin_hbm,
                out_hbm, ig_hbm, gqkv_hbm, gout_hbm, o_g1, o_b1, o_g2, o_b2, o_qb,
                gkeep, okeep, res, cot, vec, qkv, att, lse, in1, wq, wo, cos, sin,
                grows, ga, gq, dk, dv, parts, from_left, from_right, stage, stage_t,
                g_sib, g_off, o_sib, o_off, i_sib, i_off, part, gres, sums, tiles,
                load_sems, keep_sems, in1_sems, small_s, small_r,
                rs_sr, rs_rr, rs_sl, rs_rl,
                w_so, w_ro, w_ss, w_rs,
                g_ss, g_rs, g_so, g_ro, o_ss, o_rs, o_so, o_ro, i_ss, i_rs, i_so, i_ro,
                stage_sems, out_sems):
    f, s = lax.axis_index("fsdp"), lax.axis_index("seq")
    total = nf * ns
    me = f * ns + s
    m = ns // 2
    j, c = s // 2, s % 2
    tok, width = cot.shape
    length, cols = att.shape
    wz = width // nf
    pairs = cols // LANES
    block_rows = 2 * tok
    count = 4 * pairs
    span = 768 if length <= 1024 else 256
    mine = pl.ds(pl.multiple_of(s * tok, tok), tok)

    def rows_at(ref, chip, core):
        return ref.at[pl.ds(pl.multiple_of((chip * 2 + core) * tok, tok), tok)]

    keeps = []
    for d in range(m - 1, -1, -1):
        for i, (hbm, ref) in enumerate(((gsum_hbm, gkeep), (osum_hbm, okeep))):
            keeps.append(pltpu.make_async_copy(rows_at(hbm, xor(j, d, m), c), ref.at[d], keep_sems.at[2 * d + i]))
            keeps[-1].start()
    plain = [(res_hbm, res), (cot_hbm, cot), (vec_hbm, vec), (wo_hbm, wo), (att_hbm, att), (qkv_hbm, qkv),
             (lse_hbm, lse), (wq_hbm, wq), (cos_hbm, cos), (sin_hbm, sin)]
    loads = [pltpu.make_async_copy(a, b, load_sems.at[i]) for i, (a, b) in enumerate(plain)]
    for load in loads:
        load.start()

    def in1_load(k):
        return pltpu.make_async_copy(in1_hbm.at[:, pl.ds(k * wz, wz)], in1.at[k % 2], in1_sems.at[k % 2])
    in1_load(0).start()

    everyone_barrier(me, nf, ns)
    two = RowReduce(s, m, g_sib, g_off, (g_ss, g_rs, g_so, g_ro))
    out = RowReduce(s, m, o_sib, o_off, (o_ss, o_rs, o_so, o_ro))

    def two_src(d):
        return rows_at(gsum_hbm, xor(j, d, m), 1 - c)

    def out_src(d):
        return rows_at(osum_hbm, xor(j, d, m), 1 - c)

    for d in range(m - 1, -1, -1):
        two.give(d, two_src(d))
    for d in range(m - 1, -1, -1):
        out.give(d, out_src(d))
    for keep in keeps:
        keep.wait()
    for d in range(m - 1, 0, -1):
        two.pass_on(d, gkeep[d])
    for load in loads[:3]:
        load.wait()
    sums[...] = jnp.zeros_like(sums)
    normed, inverse = normed_rows(res[...])
    grad = two.total(gkeep[0])
    sums[2:3, :] = jnp.sum(grad * normed, axis=0, keepdims=True)
    sums[3:4, :] = jnp.sum(grad, axis=0, keepdims=True)

    def norm_grad(grad, normed, inverse, gain):
        scaled = grad * gain
        return inverse * (scaled - jnp.mean(scaled, axis=-1, keepdims=True)
                          - normed * jnp.mean(scaled * normed, axis=-1, keepdims=True))

    gres[...] = cot[...].astype(f32) + norm_grad(grad, normed, inverse, vec[2:3, :])
    grows[mine, :] = gres[...].astype(bf16)
    x_load = pltpu.make_async_copy(x_hbm, cot, load_sems.at[len(plain)])
    x_load.start()
    rows_w = RowGather(s, m, tok, grows, (w_so, w_ro, w_ss, w_rs))
    rows_w.start(grows.at[mine])
    for d in range(m - 1, 0, -1):
        out.pass_on(d, okeep[d])
    for d in range(1, m):
        rows_w.relay(d)
    rows_w.finish()
    for load in loads[3:]:
        load.wait()

    def block(p, k):
        return parts.at[p, :, pl.ds(k * wz, wz)]

    def staged(p, act):
        sl = lax.rem(p, 2)

        @pl.when(p < pairs)
        def _():
            act(pltpu.make_async_copy(
                stage.at[sl], gout_hbm.at[pl.ds(pl.multiple_of(p * LANES, LANES), LANES)], stage_sems.at[sl]))

        @pl.when(p >= pairs)
        def _():
            q = p - pairs
            lanes = pl.ds(pl.multiple_of(q // 3 * LANES, LANES), LANES)
            act(pltpu.make_async_copy(stage_t.at[sl], gqkv_hbm.at[lax.rem(q, 3), :, lanes], stage_sems.at[sl]))

    def finish(p):
        @pl.when(p >= 2)
        def _():
            staged(p - 2, lambda cc: cc.wait())
        sl = lax.rem(p, 2)
        stage[sl] = parts[p, :, pl.ds(pl.multiple_of(f * wz, wz), wz)].astype(f32)

        @pl.when(f > 0)
        def _():
            stage[sl] += from_left[p, jnp.maximum(f - 1, 0)].astype(f32)

        @pl.when(f < nf - 1)
        def _():
            stage[sl] += from_right[p, jnp.minimum(f, nf - 2)].astype(f32)

        @pl.when(p >= pairs)
        def _():
            stage_t[sl] = stage[sl].T
        staged(p, lambda cc: cc.start())

    reduce = LineReduce(f, nf, count, block, from_left, from_right, (rs_sr, rs_rr, rs_sl, rs_rl), finish)

    for k in range(nf):
        lanes = slice(k * wz, (k + 1) * wz)
        value = dot_tn(att[...], grows[:, lanes]).astype(bf16)
        for g in range(pairs):
            parts[g, :, lanes] = value[g * LANES:(g + 1) * LANES, :]
    for p in range(pairs):
        reduce.tick(jnp.int32(p))

    @pl.loop(0, m)
    def _(b):
        rows = pl.ds(pl.multiple_of(b * block_rows, block_rows), block_rows)
        ga[rows, :] = dot_nt(grows[rows, :], wo[...]).astype(bf16)

    @pl.loop(0, pairs)
    def _(g):
        lanes = pl.ds(pl.multiple_of(g * LANES, LANES), LANES)
        dk[...] = jnp.zeros_like(dk)
        dv[...] = jnp.zeros_like(dv)
        lane = lane_of((block_rows, LANES))
        seen = lane_of((block_rows, block_rows)) <= lax.broadcasted_iota(jnp.int32, (block_rows, block_rows), 0)
        for b in range(m):
            rows = pl.ds(b * block_rows, block_rows)
            q = qkv[0, rows, lanes].astype(f32) * HEAD_DIM ** -0.5
            go = ga[rows, lanes].astype(f32)
            both = go * att[rows, lanes].astype(f32)
            logs = lse[rows, :]
            grad_q = jnp.zeros((block_rows, LANES), f32)
            for h in range(PER):
                head = lane // HEAD_DIM == h
                qm = jnp.where(head, q, 0.0).astype(bf16)
                gm = jnp.where(head, go, 0.0).astype(bf16)
                delta = jnp.sum(jnp.where(head, both, 0.0), axis=1, keepdims=True)
                log = jnp.sum(jnp.where(lane == g * PER + h, logs, 0.0), axis=1, keepdims=True)
                acc = jnp.zeros((block_rows, LANES), f32)
                spans = [(k, min(span, b * block_rows - k)) for k in range(0, b * block_rows, span)]
                for first, size in spans + [(b * block_rows, block_rows)]:
                    at = pl.ds(first, size)
                    key, val = qkv[1, at, lanes], qkv[2, at, lanes]
                    pr = jnp.exp(dot_nt(qm, key) - log)
                    if first == b * block_rows:
                        pr = jnp.where(seen, pr, 0.0)
                    gp = dot_nt(gm, val)
                    gs = (pr * (gp - delta)).astype(bf16)
                    dv[at, :] += dot_tn(pr.astype(bf16), gm)
                    dk[at, :] += dot_tn(gs, qm)
                    acc = acc + dot_nn(gs, key)
                grad_q = jnp.where(head, acc * HEAD_DIM ** -0.5, grad_q)
            gq[0, rows, lanes] = turn(grad_q, cos[rows, :], sin[rows, :], -1.0).astype(bf16)
        gq[1, :, lanes] = turn(dk[...], cos[...], sin[...], -1.0).astype(bf16)
        gq[2, :, lanes] = dv[...].astype(bf16)
        three = jnp.concatenate([gq[0, :, lanes], gq[1, :, lanes], gq[2, :, lanes]], axis=1)
        at = pl.ds(pl.multiple_of(s * cols + g * LANES, LANES), LANES)
        for k in range(3):
            sums[4 + k:5 + k, at] = jnp.sum(gq[k, :, lanes].astype(f32), axis=0, keepdims=True)

        @pl.when(g > 0)
        def _():
            for k in range(3):
                reduce.tick(pairs + 3 * (g - 1) + k)
        for k in range(nf):
            in1_load(k).wait()
            in1_load((k + 1) % nf).start()
            value = dot_tn(three, in1[k % 2]).astype(bf16)
            for i in range(3):
                parts[pairs + 3 * g + i, :, k * wz:(k + 1) * wz] = value[i * LANES:(i + 1) * LANES, :]
    in1_load(0).wait()

    okeep[0] = (res[...] + out.total(okeep[0])).astype(bf16)
    stores = [pltpu.make_async_copy(okeep.at[0], out_hbm, out_sems.at[0])]
    stores[0].start()
    out.drain(out_src)
    one = RowReduce(s, m, i_sib, i_off, (i_ss, i_rs, i_so, i_ro))
    late = list(range(pairs + 3 * (pairs - 1), count + nf - 1))
    for d in range(m - 1, -1, -1):
        if late:
            reduce.tick(jnp.int32(late.pop(0)))
        rows = pl.ds(pl.multiple_of(xor(j, d, m) * block_rows, block_rows), block_rows)
        value = dot_nt(gq[0, rows, :], wq[0])
        for k in (1, 2):
            value = value + dot_nt(gq[k, rows, :], wq[k])
        part[...] = value.astype(bf16)
        if d == 0:
            stores.pop().wait()
        okeep[d] = part[pl.ds(pl.multiple_of((1 - c) * tok, tok), tok), :]
        gkeep[d] = part[pl.ds(pl.multiple_of(c * tok, tok), tok), :]
        one.give(d, okeep.at[d])
        if d < m - 1:
            one.pass_on(d + 1, gkeep[d + 1])
    grad = one.total(gkeep[0])
    x_load.wait()
    normed, inverse = normed_rows(cot[...].astype(f32))
    sums[0:1, :] = jnp.sum(grad * normed, axis=0, keepdims=True)
    sums[1:2, :] = jnp.sum(grad, axis=0, keepdims=True)
    res[...] = gres[...] + norm_grad(grad, normed, inverse, vec[0:1, :])
    stores.append(pltpu.make_async_copy(res, ig_hbm, out_sems.at[1]))
    stores[0].start()

    w = o_g1.shape[1]
    spread = LANES // w

    def tile_of(t):
        return sums.at[:, pl.ds(pl.multiple_of(t // spread * LANES, LANES), LANES)]

    def small(k):
        t = lax.rem(me + k, total)
        return remote(tile_of(t), tiles.at[k], small_s.at[k], small_r.at[k],
                      {"fsdp": t // ns, "seq": lax.rem(t, ns)})

    @pl.loop(1, total)
    def _(k):
        small(k).start()
    for t in late:
        reduce.tick(jnp.int32(t))
    tiles[0] = tile_of(me)[...]

    @pl.loop(1, total)
    def _(k):
        small(k).wait_recv()
        tiles[0] += tiles[k]
    for k in range(spread):
        @pl.when(lax.rem(me, spread) == k)
        def _(k=k):
            lanes = slice(k * w, (k + 1) * w)
            for i, ref in enumerate((o_g1, o_b1, o_g2, o_b2)):
                ref[...] = tiles[0, i:i + 1, lanes]
            o_qb[...] = tiles[0, 4:7, lanes]

    @pl.loop(1, total)
    def _(k):
        small(k).wait_send()
    two.drain(two_src)
    one.drain(lambda d: okeep.at[d])
    rows_w.drain(grows.at[mine])
    for p in (count - 2, count - 1):
        staged(jnp.int32(p), lambda cc: cc.wait())
    for st in stores:
        st.wait()


def back(gsum, osum, res, cot, x, vec, qkv, att, lse, in1, wq, wo, cos, sin, nf, ns, cid):
    tok, width = x.shape
    length, cols = att.shape
    wz = width // nf
    m = ns // 2
    w = width // (nf * ns)
    pairs = cols // LANES
    count = 4 * pairs
    D, V = pltpu.SemaphoreType.DMA, pltpu.VMEM
    A = pl.BlockSpec(memory_space=pl.ANY)
    M = pl.BlockSpec(memory_space=pltpu.VMEM)
    S = jax.ShapeDtypeStruct
    rows_v = V((m, tok, width), bf16)
    offs_v = V((m - 1, tok, width), bf16)
    return pl.pallas_call(
        functools.partial(back_kernel, nf, ns),
        out_shape=(
            S((tok, width), bf16), S((tok, width), f32), S((3, wz, cols), f32), S((cols, wz), f32),
            S((1, w), f32), S((1, w), f32), S((1, w), f32), S((1, w), f32), S((3, w), f32),
        ),
        in_specs=[A] * 14,
        out_specs=[A] * 4 + [M] * 5,
        scratch_shapes=[
            rows_v, rows_v, V((tok, width), f32), V((tok, width), bf16), V((8, width), f32),
            V((3, length, cols), bf16), V((length, cols), bf16), V((length, LANES), f32), V((2, length, wz), bf16),
            V((3, width, cols), bf16), V((cols, width), bf16), V((length, LANES), f32), V((length, LANES), f32),
            V((length, width), bf16), V((length, cols), bf16), V((3, length, cols), bf16),
            V((length, LANES), f32), V((length, LANES), f32),
            V((count, LANES, width), bf16), V((count, nf - 1, LANES, wz), bf16), V((count, nf - 1, LANES, wz), bf16),
            V((2, LANES, wz), f32), V((2, wz, LANES), f32),
            rows_v, offs_v, rows_v, offs_v, rows_v, offs_v,
            V((2 * tok, width), bf16), V((tok, width), f32),
            V((8, width), f32), V((nf * ns, 8, LANES), f32),
            D((11,)), D((2 * m,)), D((2,)), D((nf * ns,)), D((nf * ns,)),
        ] + [D((count, nf - 1))] * 4 + [D((m,))] * 16 + [D((2,)), D((2,))],
        compiler_params=pltpu.CompilerParams(
            collective_id=cid, has_side_effects=True, vmem_limit_bytes=64 * 1024 * 1024 - 65536),
        name="back",
    )(gsum, osum, res, cot, x, vec, qkv, att, lse, in1, wq, wo, cos, sin)


def local(
    block_input,
    cotangent,
    ln1_gain,
    ln1_bias,
    qkv_weight,
    qkv_bias,
    out_weight,
    ln2_gain,
    ln2_bias,
    gate_up_weight,
    down_weight,
):
    fsdp, seq = lax.axis_size("fsdp"), lax.axis_size("seq")
    (in_one, cot_all, in_two, qkv, mixed, logs, residual, qkv_full, out_full, vectors, cosine, sine) = front(
        block_input[0],
        cotangent[0],
        ln1_gain[None],
        ln1_bias[None],
        ln2_gain[None],
        ln2_bias[None],
        qkv_bias,
        jnp.transpose(qkv_weight, (1, 0, 2)),
        out_weight,
        fsdp,
        seq,
        1,
    )
    out_sum, grad_sum, grad_gate_up, grad_down = mlp(
        in_two, cot_all, jnp.transpose(gate_up_weight, (1, 2, 0)), down_weight, fsdp, 0
    )
    block_output, input_grad, grad_qkv, grad_out, gain_one, bias_one, gain_two, bias_two, grad_bias = back(
        grad_sum,
        out_sum,
        residual,
        cotangent[0],
        block_input[0],
        vectors,
        qkv,
        mixed,
        logs,
        in_one,
        qkv_full,
        out_full,
        cosine,
        sine,
        fsdp,
        seq,
        2,
    )
    return (
        block_output[None],
        input_grad[None],
        gain_one[0],
        bias_one[0],
        jnp.transpose(grad_qkv, (1, 0, 2)),
        grad_bias,
        grad_out,
        gain_two[0],
        bias_two[0],
        jnp.transpose(grad_gate_up, (2, 0, 1)),
        grad_down,
    )


def solution(mesh):
    placed = (
        P("fsdp", "seq", None),
        P("fsdp", "seq", None),
        P(("fsdp", "seq")),
        P(("fsdp", "seq")),
        P("fsdp", None, "seq"),
        P(None, ("fsdp", "seq")),
        P("seq", "fsdp"),
        P(("fsdp", "seq")),
        P(("fsdp", "seq")),
        P("fsdp", None, "seq"),
        P("seq", "fsdp"),
    )
    return jax.shard_map(
        local,
        mesh=mesh,
        in_specs=placed,
        out_specs=(
            P("fsdp", "seq", None),
            P("fsdp", "seq", None),
            P(("fsdp", "seq")),
            P(("fsdp", "seq")),
            P("fsdp", None, "seq"),
            P(None, ("fsdp", "seq")),
            P("seq", "fsdp"),
            P(("fsdp", "seq")),
            P(("fsdp", "seq")),
            P("fsdp", None, "seq"),
            P("seq", "fsdp"),
        ),
        check_vma=False,
    )
```

time: 1010 us -> 570 us (0.56)
  waiting for transfers between devices: 551 us -> 0 us
  Pallas kernels: 237 us -> 549 us
  matrix products: 68.8 us -> 0 us
  blocking collectives: 45 us -> 0 us
  other arithmetic: 33.7 us -> 0 us
  local copies, waits for them, and re-layouts: 44.5 us -> 12.5 us
  between operations: 15 us -> 1.16 us
    pallas_call x0 -> x2, Pallas kernels: none -> 312 us  [the longest x1 166 us: back(): pl.pallas_call(functools.partial(back_kernel, nf, ns), out_shape=(S((tok,...]
    reduce_scatter x6 -> x0, waiting for transfers between devices: 251 us -> none  [the longest x4 191 us: scatter_rows(): lax.psum_scatter(partial.astype(jnp.bfloat16), 'seq', scatter_dimension=0...]
    all_gather x6 -> x0, waiting for transfers between devices: 161 us -> none  [the longest x4 146 us: gather_rows(): return lax.all_gather(rows, 'seq', axis=0, tiled=True)]
    unnamed x14 -> x0, waiting for transfers between devices: 139 us -> none
    dot_general x20 -> x0, matrix products: 68.8 us -> none  [the longest x2 9.52 us: one_block(): jnp.einsum('qhd,khd->hqk', grad_block, value_rows, preferred_element_type...]
    all_gather x1 -> x0, blocking collectives: 45 us -> none  [local(): lax.all_gather(small, ('fsdp', 'seq'), axis=1, tiled=True)]
    dynamic_update_slice x5 -> x0, local copies, waits for them, and re-layouts: 21.9 us -> none  [the longest x4 21.9 us: attend_back(): lax.scan(one_block, (zeros, zeros), starts)]
    reduce_sum x9 -> x0, other arithmetic: 14.6 us -> none  [the longest x2 4.67 us: one_block(): jnp.sum(jnp.exp(scores - row_max), axis=-1, keepdims=True)]
  transfers between devices with their start and end apart: 13 -> 0, of which waited for: 11 -> 0; matrix products, arithmetic and copies ran while one was open for 12% -> 0% of each run, Pallas kernels for 0% -> 0%
where the time goes in v2:
time: 570 us; the launch traced here: 563 us
  Pallas kernels  549 us (96%)
  local copies, waits for them, and re-layouts  12.5 us (2%)
    pallas_call x1, Pallas kernels, mlp(): pl.pallas_call(functools.partial(mlp_kernel, n, r, rb), out_shape=(jax.Sh...  237 us
    pallas_call x1, Pallas kernels, back(): pl.pallas_call(functools.partial(back_kernel, nf, ns), out_shape=(S((tok,...  166 us
    pallas_call x1, Pallas kernels, front(): pl.pallas_call(functools.partial(front_kernel, nf, ns), out_shape=(S((len...  146 us
    unnamed x29, local copies, waits for them, and re-layouts  12.5 us

profile of v2, /device:TPU:0, one launch (start us, length us, event | category | flops | bytes accessed | tf_op | source)
XLA Modules:
  0.0 562.9 jit_solution(6115323820409238384)
XLA Ops:
  0.6 145.8 %front.1 = (bf16[1024,2048]{1,0:T(8,128)(2,1)}, bf16[1024,2048]{1,0:T(8,128)(2,1)}, bf16[1024,2048]{1,0:T(8,128)(2,1)}, bf16[3,1024,256]{2,1,0:T(8,128)(2,1)}, b...) custom-call(bf16[128,2048]{1,0:T(8,128)(2,1)} %bitcast.17, ...), custom_call_target="tpu_custom_call" | custom-call | tf_op jit(solution)/shard_map/front/pallas_call | solution.py:757
  146.4 237.2 %mlp.1 = (bf16[1024,2048]{1,0:T(8,128)(2,1)}, bf16[1024,2048]{1,0:T(8,128)(2,1)}, f32[2,704,512]{2,1,0:T(8,128)}, f32[704,512]{1,0:T(8,128)}) custom-call(bf16[1024,2048]{1,0:T(8,128)(2,1)} %get-tuple-element.36.in2_hbm, bf16[1024,2048]{1,0:T(8,128)(2,1)} %get-tuple-element.37.cot_hbm, bf16[2,704,512]{2,1,0:T(8,128)(2,1)} %bitcast.22, bf16[704,512]{1,0:T(8,128)(2,1)} %wd_hbm.1), custom_call_target="tpu_custom_call" | custom-call | tf_op jit(solution)/shard_map/mlp/pallas_call | solution.py:353
  383.6 166.2 %back.1 = (bf16[128,2048]{1,0:T(8,128)(2,1)}, f32[128,2048]{1,0:T(8,128)}, f32[3,512,256]{2,1,0:T(8,128)}, f32[256,512]{1,0:T(8,128)}, f32[1,64]{1,0:T(1,128)}, ...) custom-call(bf16[1024,2048]{1,0:T(8,128)(2,1)} %get-tuple-element.38.gsum_hbm, ...), custom_call_target="tpu_custom_call" | custom-call | tf_op jit(solution)/shard_map/back/pallas_call | solution.py:1062
  549.9 0.0 copy-start.8
  549.9 0.0 copy-start.7
  549.9 0.0 copy-start.1
  549.9 2.0 copy.33
  551.9 0.0 copy-start
  551.9 2.4 copy.34
  554.4 0.0 copy-done.8
  554.4 0.5 copy.35
  554.9 0.0 copy-done.7
  554.9 0.5 copy.36
  555.4 0.0 copy-done.1
  555.4 1.1 copy.37
  556.6 0.0 copy-done.4
  556.6 0.6 copy.38
  557.2 0.8 copy.39
  558.0 0.5 copy.40
  558.5 0.5 copy.41
  559.0 0.0 copy-done
  559.0 1.6 copy.42
  560.6 0.8 copy-done.2
  561.4 1.1 copy.43
  (8 shorter events, 0.0 us)
Async XLA Ops:
  549.9 4.5 copy-start.8
  549.9 5.0 copy-start.7
  549.9 5.5 copy-start.1
  551.9 4.6 copy-start.4
  551.9 5.2 copy-start.3
  551.9 6.0 %copy-start.6 = (f32[1,64]{1,0:T(1,128)S(1)}, f32[1,64]{1,0:T(1,128)}, u32[]{:S(2)}) copy-start(f32[1,64]{1,0:T(1,128)} %get-tuple-element.57) | copy-start | bytes 772
  551.9 6.5 %copy-start.5 = (f32[1,64]{1,0:T(1,128)S(1)}, f32[1,64]{1,0:T(1,128)}, u32[]{:S(2)}) copy-start(f32[1,64]{1,0:T(1,128)} %get-tuple-element.58) | copy-start | bytes 772
  551.9 7.0 %copy-start = (f32[2,704,512]{2,1,0:T(8,128)S(1)}, f32[2,704,512]{2,1,0:T(8,128)}, u32[]{:S(2)}) copy-start(f32[2,704,512]{2,1,0:T(8,128)} %get-tuple-element.59) | copy-start | bytes 8650756
  559.0 2.4 copy-start.2

commit v3 on v2

--- a/solution.py
+++ b/solution.py
@@ -68,10 +68,10 @@
         target = f + 1 if rightward else f - 1
         return remote(src, self.slot(p, source), send.at[p, h], recv.at[p, h], {"fsdp": target})
 
-    def tick(self, t):
-        f, n, count = self.f, self.n, self.count
-
-        @when((t >= 0) & (t < count))
+    def send_own(self, t):
+        f, n = self.f, self.n
+
+        @when((t >= 0) & (t < self.count))
         def _():
             @pl.when(f < n - 1)
             def _():
@@ -81,8 +81,13 @@
             def _():
                 self.own(t, lambda src: self.copy(src, t, 0, f, False).start())
 
-        for h in range(1, n):
+    def arrivals(self, t):
+        for h in range(1, self.n):
             self.arrive(t - h, h)
+
+    def tick(self, t):
+        self.send_own(t)
+        self.arrivals(t)
 
     def arrive(self, p, h):
         f, n = self.f, self.n
@@ -186,20 +191,24 @@
             self.finish(e)
 
 
-def mlp_kernel(n, r, rb, in2_hbm, cot_hbm, wgu_hbm, wd_hbm,
-               out_hbm, gin_hbm, ggu_hbm, gd_hbm,
-               in2, cot, acc_o, acc_g, w, hid, dga, dup, parts, from_left, from_right,
+def mlp_kernel(n, r, rb, left, in2_hbm, cot_hbm, w0_hbm, wgu_hbm, wd_hbm,
+               out_hbm, gin_hbm, ggu_hbm, gd_hbm, *more):
+    rest_hbm, more = (more[0], more[1:]) if left else (None, more)
+    (in2, cot, acc_o, acc_g, w, hid, dga, dup, parts, from_left, from_right,
                stage, load_sems, own_sems, ag_sr, ag_rr, ag_sl, ag_rl, rs_sr, rs_rr, rs_sl, rs_rl,
-               stage_sems):
+               stage_sems, rest_sems) = more
     f = lax.axis_index("fsdp")
     tokens, width = in2.shape
     wz = width // n
     ff = wd_hbm.shape[0]
     nc = ff // r
     count = 3 * nc
+    summed = count - 3 * left
+    ahead = max(n - 1, 3)
     ring = parts.shape[0]
     loads = [pltpu.make_async_copy(in2_hbm, in2, load_sems.at[0]),
-             pltpu.make_async_copy(cot_hbm, cot, load_sems.at[1])]
+             pltpu.make_async_copy(cot_hbm, cot, load_sems.at[1]),
+             pltpu.make_async_copy(w0_hbm, w.at[pl.ds(0, 3)], load_sems.at[2])]
     for c in loads:
         c.start()
 
@@ -223,12 +232,13 @@
     def own_copy(p, act):
         own(p, lambda src: act(pltpu.make_async_copy(src, slot(p, f), own_sems.at[p])))
 
-    @pl.loop(0, count)
+    @pl.loop(3, count)
     def _(p):
         own_copy(p, lambda c: c.start())
 
     line_barrier(f, n)
-    gather = LineGather(f, n, count, own, slot, (ag_sr, ag_rr, ag_sl, ag_rl))
+    gather = LineGather(f, n, count - 3, lambda p, use: own(p + 3, use), lambda p, source: slot(p + 3, source),
+                        (ag_sr, ag_rr, ag_sl, ag_rl))
 
     def block(p, j):
         return parts.at[lax.rem(p, ring), :, pl.ds(j * wz, wz)]
@@ -262,23 +272,22 @@
             stage[sl] += from_right[p, jnp.minimum(f, n - 2)].astype(f32)
         stage_out(p, lambda c: c.start())
 
-    reduce = LineReduce(f, n, count, block, from_left, from_right, (rs_sr, rs_rr, rs_sl, rs_rl), finish)
+    reduce = LineReduce(f, n, summed, block, from_left, from_right, (rs_sr, rs_rr, rs_sl, rs_rl), finish)
 
     acc_o[...] = jnp.zeros_like(acc_o)
     acc_g[...] = jnp.zeros_like(acc_g)
 
-    first = 3 + n - 1
-
-    @pl.loop(0, first)
-    def _(t):
-        gather.tick(t)
+    for t in range(3):
+        gather.send_own(t)
 
     for c in loads:
         c.wait()
 
     def compute(c):
-        for k in range(3):
-            own_copy(3 * c + k, lambda cc: cc.wait())
+        @pl.when(c > 0)
+        def _():
+            for k in range(3):
+                own_copy(3 * c + k, lambda cc: cc.wait())
 
         @pl.loop(0, tokens // rb)
         def _(i):
@@ -298,6 +307,10 @@
             acc_o[rows, :] = (acc_o[rows, :].astype(f32) + dot_nn(h, w[3 * c + 2])).astype(acc_o.dtype)
             acc_g[rows, :] = (acc_g[rows, :].astype(f32) + dot_nn(dg, w[3 * c]) + dot_nn(du, w[3 * c + 1])).astype(acc_g.dtype)
 
+        @pl.when(c == 0)
+        def _():
+            gather.arrivals(1)
+
         for k, (small, big) in enumerate(((dga, in2), (dup, in2), (hid, cot))):
             for j in range(n):
                 block(3 * c + k, j)[...] = dot_tn(small[...], big[:, pl.ds(j * wz, wz)]).astype(bf16)
@@ -306,26 +319,39 @@
     def _(c):
         compute(c)
 
-        @pl.loop(0, 3)
-        def _(k):
-            gather.tick(3 * c + k + first)
-            reduce.tick(3 * c + k)
+        @pl.when(c == 0)
+        def _():
+            gather.arrivals(2)
+
+        @pl.when(c == 0)
+        def _():
+            for t in range(3, ahead):
+                gather.tick(t)
+
+        @pl.when(c < nc - left)
+        def _():
+            @pl.loop(0, 3)
+            def _(k):
+                reduce.tick(3 * c + k)
+                gather.tick(3 * c + k + ahead)
 
     in2[...] = acc_o[...].astype(bf16)
     cot[...] = acc_g[...].astype(bf16)
     stores = [pltpu.make_async_copy(in2, out_hbm, load_sems.at[0]),
               pltpu.make_async_copy(cot, gin_hbm, load_sems.at[1])]
+    for k in range(3 * left):
+        stores.append(pltpu.make_async_copy(parts.at[(count - 3 + k) % ring], rest_hbm.at[k], rest_sems.at[k]))
     for c in stores:
         c.start()
 
     @pl.loop(0, n - 1)
     def _(k):
-        reduce.tick(count + k)
-
-    @pl.loop(0, count)
+        reduce.tick(summed + k)
+
+    @pl.loop(0, count - 3)
     def _(p):
         gather.drain(p)
-    for p in (count - 2, count - 1):
+    for p in (summed - 2, summed - 1):
         stage_out(jnp.int32(p), lambda c: c.wait())
     for c in stores:
         c.wait()
@@ -339,7 +365,7 @@
     return r
 
 
-def mlp(in2, cot, wgu, wd, n, cid):
+def mlp(in2, cot, w0, wgu, wd, n, left, cid):
     tokens, width = in2.shape
     ff, wz = wd.shape
     r = piece_rows(ff)
@@ -351,15 +377,15 @@
     acc_dtype = f32 if tokens * width * 8 <= 20 * 2**20 else bf16
     D = pltpu.SemaphoreType.DMA
     return pl.pallas_call(
-        functools.partial(mlp_kernel, n, r, rb),
+        functools.partial(mlp_kernel, n, r, rb, left),
         out_shape=(
             jax.ShapeDtypeStruct((tokens, width), bf16),
             jax.ShapeDtypeStruct((tokens, width), bf16),
             jax.ShapeDtypeStruct((2, ff, wz), f32),
             jax.ShapeDtypeStruct((ff, wz), f32),
-        ),
-        in_specs=[any_spec] * 4,
-        out_specs=[any_spec] * 4,
+        ) + (jax.ShapeDtypeStruct((3, r, width), bf16),) * left,
+        in_specs=[any_spec] * 5,
+        out_specs=[any_spec] * (4 + left),
         scratch_shapes=[
             pltpu.VMEM((tokens, width), bf16),
             pltpu.VMEM((tokens, width), bf16),
@@ -370,16 +396,16 @@
             pltpu.VMEM((tokens, r), bf16),
             pltpu.VMEM((tokens, r), bf16),
             pltpu.VMEM((ring, r, width), bf16),
-            pltpu.VMEM((count, n - 1, r, wz), bf16),
-            pltpu.VMEM((count, n - 1, r, wz), bf16),
+            pltpu.VMEM((count - 3 * left, n - 1, r, wz), bf16),
+            pltpu.VMEM((count - 3 * left, n - 1, r, wz), bf16),
             pltpu.VMEM((2, r, wz), f32),
-            D((2,)),
+            D((3,)),
             D((count,)),
-        ] + [D((count, n - 1))] * 8 + [D((2,))],
+        ] + [D((count - 3, n - 1))] * 4 + [D((count - 3 * left, n - 1))] * 4 + [D((2,)), D((3,))],
         compiler_params=pltpu.CompilerParams(
             collective_id=cid, has_side_effects=True, vmem_limit_bytes=64 * 1024 * 1024 - 65536),
         name="mlp",
-    )(in2, cot, wgu, wd)
+    )(in2, cot, w0, wgu, wd)
 
 
 LANES = 128
@@ -412,28 +438,44 @@
     def __init__(self, s, m, tok, buf, sems):
         self.j, self.c, self.m, self.tok, self.buf = s // 2, s % 2, m, tok, buf
         self.send_o, self.recv_o, self.send_s, self.recv_s = sems
-
-    def slot(self, chip, core):
+        self.square = m == 4
+
+    def slot(self, chip, core, part=None):
         row = (chip * 2 + core) * self.tok
-        return self.buf.at[pl.ds(pl.multiple_of(row, self.tok), self.tok)]
+        if part is None:
+            return self.buf.at[pl.ds(pl.multiple_of(row, self.tok), self.tok)]
+        half = self.tok // 2
+        return self.buf.at[pl.ds(pl.multiple_of(row + part * half, half), half)]
 
     def off(self, src, d, chip):
         return remote(src, self.slot(chip, self.c), self.send_o.at[d], self.recv_o.at[d],
                       {"seq": xor(self.j, d, self.m) * 2 + self.c})
 
+    def half(self, part, source, to):
+        here = self.slot(xor(self.j, source, 4), self.c, part)
+        index = 0 if part else 3
+        return remote(here, here, self.send_o.at[index], self.recv_o.at[index],
+                      {"seq": xor(self.j, to, 4) * 2 + self.c})
+
     def sib(self, src, d, core):
         return remote(src, self.slot(xor(self.j, d, self.m), core), self.send_s.at[d], self.recv_s.at[d],
                       {"seq": self.j * 2 + 1 - self.c})
 
     def start(self, src):
-        for d in range(1, self.m):
+        for d in range(1, 3 if self.square else self.m):
             self.off(src, d, self.j).start()
         self.sib(src, 0, self.c).start()
 
     def relay(self, d):
         chip = xor(self.j, d, self.m)
         here = self.slot(chip, self.c)
-        self.off(here, d, chip).wait_recv()
+        if self.square and d == 3:
+            self.half(0, 3, 2).wait_recv()
+            self.half(1, 3, 1).wait_recv()
+        else:
+            self.off(here, d, chip).wait_recv()
+            if self.square:
+                self.half(d - 1, d, 3 - d).start()
         self.sib(here, d, self.c).start()
 
     def finish(self):
@@ -442,8 +484,11 @@
 
     def drain(self, src):
         for d in range(1, self.m):
-            self.off(src, d, self.j).wait_send()
             chip = xor(self.j, d, self.m)
+            if not self.square or d < 3:
+                self.off(src, d, self.j).wait_send()
+                if self.square:
+                    self.half(d - 1, d, 3 - d).wait_send()
             self.sib(self.slot(chip, self.c), d, self.c).wait_send()
         self.sib(src, 0, self.c).wait_send()
 
@@ -453,6 +498,8 @@
         self.j, self.c, self.m = s // 2, s % 2, m
         self.from_sib, self.from_off = from_sib, from_off
         self.send_s, self.recv_s, self.send_o, self.recv_o = sems
+        self.square = m == 4
+        self.tok = from_sib.shape[1]
 
     def sib(self, src, d):
         return remote(src, self.from_sib.at[d], self.send_s.at[d], self.recv_s.at[d],
@@ -461,6 +508,14 @@
     def off(self, d):
         return remote(self.from_sib.at[d], self.from_off.at[d - 1], self.send_o.at[d], self.recv_o.at[d],
                       {"seq": xor(self.j, d, self.m) * 2 + self.c})
+
+    def half(self, d, part):
+        at = pl.ds(part * (self.tok // 2), self.tok // 2)
+        last = d // 3
+        to = d * (1 - last) + (part + 1) * last
+        index = 2 * d + part
+        return remote(self.from_sib.at[d, at], self.from_off.at[d - 1, at], self.send_o.at[index], self.recv_o.at[index],
+                      {"seq": xor(self.j, to, 4) * 2 + self.c})
 
     def give(self, d, src):
         self.sib(src, d).start()
@@ -469,12 +524,29 @@
         here = self.from_sib.at[d]
         self.sib(here, d).wait_recv()
         here[...] = (own.astype(f32) + here[...].astype(f32)).astype(bf16)
-        self.off(d).start()
+        if not self.square:
+            self.off(d).start()
+            return
+        for part in range(2):
+            @when((d == 3) | (part == d - 1))
+            def _(part=part):
+                self.half(d, part).start()
 
     def total(self, own):
         here = self.from_sib.at[0]
         self.sib(here, 0).wait_recv()
         value = own.astype(f32) + here[...].astype(f32)
+        if self.square:
+            for part, d in ((0, 2), (1, 1)):
+                at = pl.ds(part * (self.tok // 2), self.tok // 2)
+                self.half(3, part).wait_recv()
+                self.from_sib[d, at] = (self.from_sib[d, at].astype(f32) + self.from_off[2, at].astype(f32)).astype(bf16)
+                self.half(d, part).start()
+            for d in (1, 2):
+                self.half(d, 0).wait_recv()
+                self.half(d, 1).wait_recv()
+                value = value + self.from_off[d - 1].astype(f32)
+            return value
         for d in range(self.m - 1, 0, -1):
             self.off(d).wait_recv()
             value = value + self.from_off[d - 1].astype(f32)
@@ -484,7 +556,11 @@
         for d in range(self.m):
             self.sib(src_of(d), d).wait_send()
         for d in range(1, self.m):
-            self.off(d).wait_send()
+            if self.square:
+                self.half(d, 0).wait_send()
+                self.half(d, 1).wait_send()
+            else:
+                self.off(d).wait_send()
 
 
 def normed_rows(x):
@@ -522,13 +598,13 @@
 
 
 def front_kernel(nf, ns,
-                 x_hbm, cot_hbm, g1, b1, g2, b2, qb, wqkv_hbm, wo_hbm,
+                 x_hbm, cot_hbm, g1, b1, g2, b2, qb, wqkv_hbm, wo_hbm, wgu_hbm, wd_hbm,
                  in1_hbm, cotall_hbm, in2_hbm, qkv_hbm, att_hbm, lse_hbm, res_hbm, wq_hbm, woall_hbm,
-                 vec_hbm, cos_hbm, sin_hbm,
+                 vec_hbm, cos_hbm, sin_hbm, w0_hbm,
                  x, in1, tile, tiles, vecs, wq, wo, qkv, att, lse, cos, sin, part, keep, give,
-                 from_sib, from_off, res, in2,
+                 from_sib, from_off, res, in2, w0,
                  load_sems, own_sems, small_s, small_r,
-                 ag_sr, ag_rr, ag_sl, ag_rl,
+                 ag_sr, ag_rr, ag_sl, ag_rl, m_sr, m_rr, m_sl, m_rl,
                  a_so, a_ro, a_ss, a_rs, c_so, c_ro, c_ss, c_rs, e_so, e_ro, e_ss, e_rs,
                  r_ss, r_rs, r_so, r_ro, out_sems):
     f, s = lax.axis_index("fsdp"), lax.axis_index("seq")
@@ -560,6 +636,25 @@
 
     for p in range(4):
         own_copy(p).start()
+
+    r = w0.shape[1]
+
+    def mlp_own(p, use):
+        @pl.when(p < 2)
+        def _():
+            use(wgu_hbm.at[p, pl.ds(0, r)])
+
+        @pl.when(p == 2)
+        def _():
+            use(wd_hbm.at[pl.ds(0, r)])
+
+    def mlp_slot(p, source):
+        return w0.at[p, :, pl.ds(pl.multiple_of(source * wz, wz), wz)]
+
+    mlp_copies = [pltpu.make_async_copy(wgu_hbm.at[p, pl.ds(0, r)] if p < 2 else wd_hbm.at[pl.ds(0, r)],
+                                        mlp_slot(p, f), own_sems.at[4 + p]) for p in range(3)]
+    for copy in mlp_copies:
+        copy.start()
     cot_rows = pl.ds(pl.multiple_of(s * tok, tok), tok)
     cot_own = pltpu.make_async_copy(cot_hbm, cotall_hbm.at[cot_rows], load_sems.at[1])
 
@@ -573,6 +668,7 @@
 
     everyone_barrier(me, nf, ns)
     gather = LineGather(f, nf, 4, own, slot, (ag_sr, ag_rr, ag_sl, ag_rl))
+    second = LineGather(f, nf, 3, mlp_own, mlp_slot, (m_sr, m_rr, m_sl, m_rl))
     gather.tick(0)
 
     def small(k):
@@ -654,6 +750,7 @@
         last += 1
         gather.tick(last)
     own_copy(3).wait()
+    second.tick(jnp.int32(0))
     while relays:
         rows_cot.relay(relays.pop(0))
     store(qkv, qkv_hbm, 4)
@@ -711,9 +808,14 @@
         keep[d] = part[pl.ds(pl.multiple_of(c * tok, tok), tok), :]
         sums.give(d, give.at[d])
 
-        @pl.when(step > 0)
+        @pl.when((step > 0))
         def _():
             sums.pass_on(d + 1, keep[d + 1])
+
+        @pl.when(step % 2 == 1)
+        def _():
+            second.tick((step + 1) // 2)
+    ticks = list(range(m // 2 + 1, 3 + nf - 1))
     store(att, att_hbm, 7)
     store(lse, lse_hbm, 8)
     rows_cot.finish()
@@ -725,15 +827,26 @@
     rows_two.start(in2)
     in2_own = pltpu.make_async_copy(in2, in2_hbm.at[mine], load_sems.at[2])
     in2_own.start()
+    if ticks:
+        second.tick(jnp.int32(ticks.pop(0)))
     for d in range(1, m):
         rows_two.relay(d)
+        if ticks and d < m - 1:
+            second.tick(jnp.int32(ticks.pop(0)))
     rows_two.finish()
+    for t in ticks:
+        second.tick(jnp.int32(t))
+    for copy in mlp_copies:
+        copy.wait()
+    store(w0, w0_hbm, 10)
 
     @pl.loop(1, total)
     def _(k):
         small(k).wait_send()
     for p in range(4):
         gather.drain(p)
+    for p in range(3):
+        second.drain(p)
     rows_in.drain(in1.at[mine])
     rows_cot.drain(cot_hbm)
     rows_two.drain(in2)
@@ -744,7 +857,8 @@
         st.wait()
 
 
-def front(x, cot, g1, b1, g2, b2, qb, wqkv, wo, nf, ns, cid):
+def front(x, cot, g1, b1, g2, b2, qb, wqkv, wo, wgu, wd, nf, ns, cid):
+    r = piece_rows(wd.shape[0])
     tok, width = x.shape
     cols, wz = wo.shape
     length = tok * ns
@@ -760,36 +874,43 @@
             S((length, width), bf16), S((length, width), bf16), S((length, width), bf16),
             S((3, length, cols), bf16), S((length, cols), bf16), S((length, LANES), f32),
             S((tok, width), f32), S((3, width, cols), bf16), S((cols, width), bf16),
-            S((8, width), f32), S((length, LANES), f32), S((length, LANES), f32),
+            S((8, width), f32), S((length, LANES), f32), S((length, LANES), f32), S((3, r, width), bf16),
         ),
-        in_specs=[A, A, M, M, M, M, M, A, A],
-        out_specs=[A] * 12,
+        in_specs=[A, A, M, M, M, M, M, A, A, A, A],
+        out_specs=[A] * 13,
         scratch_shapes=[
             V((tok, width), bf16), V((length, width), bf16), V((8, LANES), f32), V((nf * ns, 8, LANES), f32),
             V((8, width), f32), V((3, width, cols), bf16), V((cols, width), bf16), V((3, length, cols), bf16),
             V((length, cols), bf16), V((length, LANES), f32), V((length, LANES), f32), V((length, LANES), f32),
             V((2 * tok, width), f32), V((m, tok, width), f32), V((m, tok, width), bf16),
             V((m, tok, width), bf16), V((m - 1, tok, width), bf16), V((tok, width), f32), V((tok, width), bf16),
-            D((3,)), D((4,)), D((nf * ns,)), D((nf * ns,)),
-        ] + [D((4, nf - 1))] * 4 + [D((m,))] * 16 + [D((10,))],
+            V((3, r, width), bf16),
+            D((3,)), D((7,)), D((nf * ns,)), D((nf * ns,)),
+        ] + [D((4, nf - 1))] * 4 + [D((3, nf - 1))] * 4 + [D((m,))] * 14 + [D((2 * m,))] * 2 + [D((11,))],
         compiler_params=pltpu.CompilerParams(
             collective_id=cid, has_side_effects=True, vmem_limit_bytes=64 * 1024 * 1024 - 65536),
         name="front",
-    )(x, cot, g1, b1, g2, b2, qb, wqkv, wo)
-
-
-def back_kernel(nf, ns,
+    )(x, cot, g1, b1, g2, b2, qb, wqkv, wo, wgu, wd)
+
+
+def back_kernel(nf, ns, left,
                 gsum_hbm, osum_hbm, res_hbm, cot_hbm, x_hbm, vec_hbm, qkv_hbm, att_hbm, lse_hbm, in1_hbm, wq_hbm, wo_hbm,
-                cos_hbm, sin_hbm,
-                out_hbm, ig_hbm, gqkv_hbm, gout_hbm, o_g1, o_b1, o_g2, o_b2, o_qb,
-                gkeep, okeep, res, cot, vec, qkv, att, lse, in1, wq, wo, cos, sin,
+                cos_hbm, sin_hbm, *more):
+    if left:
+        (rest_hbm, _, _, out_hbm, ig_hbm, gqkv_hbm, gout_hbm, o_g1, o_b1, o_g2, o_b2, o_qb, ggu_hbm, gd_hbm) = more[:14]
+        (rest, rest_left, rest_right, rest_stage, rest_sems, q_sr, q_rr, q_sl, q_rl) = more[-9:]
+        more = more[14:-9]
+    else:
+        (out_hbm, ig_hbm, gqkv_hbm, gout_hbm, o_g1, o_b1, o_g2, o_b2, o_qb) = more[:9]
+        more = more[9:]
+    (gkeep, okeep, res, cot, vec, qkv, att, lse, in1, wq, wo, cos, sin,
                 grows, ga, gq, dk, dv, parts, from_left, from_right, stage, stage_t,
                 g_sib, g_off, o_sib, o_off, i_sib, i_off, part, gres, sums, tiles,
                 load_sems, keep_sems, in1_sems, small_s, small_r,
                 rs_sr, rs_rr, rs_sl, rs_rl,
                 w_so, w_ro, w_ss, w_rs,
                 g_ss, g_rs, g_so, g_ro, o_ss, o_rs, o_so, o_ro, i_ss, i_rs, i_so, i_ro,
-                stage_sems, out_sems):
+     stage_sems, out_sems) = more
     f, s = lax.axis_index("fsdp"), lax.axis_index("seq")
     total = nf * ns
     me = f * ns + s
@@ -821,11 +942,49 @@
     def in1_load(k):
         return pltpu.make_async_copy(in1_hbm.at[:, pl.ds(k * wz, wz)], in1.at[k % 2], in1_sems.at[k % 2])
     in1_load(0).start()
+    if left:
+        rest_load = pltpu.make_async_copy(rest_hbm, rest, rest_sems.at[0])
+        rest_load.start()
 
     everyone_barrier(me, nf, ns)
     two = RowReduce(s, m, g_sib, g_off, (g_ss, g_rs, g_so, g_ro))
     out = RowReduce(s, m, o_sib, o_off, (o_ss, o_rs, o_so, o_ro))
 
+    waiting = []
+    if left:
+        r = rest.shape[1]
+        last_rows = pl.ds(gd_hbm.shape[0] - r, r)
+
+        def rest_out(p, act):
+            @pl.when(p < 2)
+            def _():
+                act(pltpu.make_async_copy(rest_stage.at[p], ggu_hbm.at[p, last_rows], rest_sems.at[p]))
+
+            @pl.when(p == 2)
+            def _():
+                act(pltpu.make_async_copy(rest_stage.at[p], gd_hbm.at[last_rows], rest_sems.at[p]))
+
+        def rest_finish(p):
+            rest_stage[p] = rest[p, :, pl.ds(pl.multiple_of(f * wz, wz), wz)].astype(f32)
+
+            @pl.when(f > 0)
+            def _():
+                rest_stage[p] += rest_left[p, jnp.maximum(f - 1, 0)].astype(f32)
+
+            @pl.when(f < nf - 1)
+            def _():
+                rest_stage[p] += rest_right[p, jnp.minimum(f, nf - 2)].astype(f32)
+            rest_out(p, lambda cc: cc.start())
+
+        rest_sum = LineReduce(f, nf, 3, lambda p, k: rest.at[p, :, pl.ds(k * wz, wz)], rest_left, rest_right,
+                              (q_sr, q_rr, q_sl, q_rl), rest_finish)
+        waiting = list(range(3 + nf - 1))
+
+    def rest_tick(how_many=1):
+        for _ in range(how_many):
+            if waiting:
+                rest_sum.tick(jnp.int32(waiting.pop(0)))
+
     def two_src(d):
         return rows_at(gsum_hbm, xor(j, d, m), 1 - c)
 
@@ -834,12 +993,16 @@
 
     for d in range(m - 1, -1, -1):
         two.give(d, two_src(d))
-    for d in range(m - 1, -1, -1):
-        out.give(d, out_src(d))
+    if left:
+        rest_load.wait()
+    rest_tick()
     for keep in keeps:
         keep.wait()
     for d in range(m - 1, 0, -1):
         two.pass_on(d, gkeep[d])
+    for d in range(m - 1, -1, -1):
+        out.give(d, out_src(d))
+    rest_tick()
     for load in loads[:3]:
         load.wait()
     sums[...] = jnp.zeros_like(sums)
@@ -859,11 +1022,13 @@
     x_load.start()
     rows_w = RowGather(s, m, tok, grows, (w_so, w_ro, w_ss, w_rs))
     rows_w.start(grows.at[mine])
+    rest_tick()
+    for d in range(1, m):
+        rows_w.relay(d)
+        rest_tick()
+    rows_w.finish()
     for d in range(m - 1, 0, -1):
         out.pass_on(d, okeep[d])
-    for d in range(1, m):
-        rows_w.relay(d)
-    rows_w.finish()
     for load in loads[3:]:
         load.wait()
 
@@ -911,6 +1076,7 @@
         value = dot_tn(att[...], grows[:, lanes]).astype(bf16)
         for g in range(pairs):
             parts[g, :, lanes] = value[g * LANES:(g + 1) * LANES, :]
+    rest_tick(len(waiting))
     for p in range(pairs):
         reduce.tick(jnp.int32(p))
 
@@ -1043,9 +1209,13 @@
         staged(jnp.int32(p), lambda cc: cc.wait())
     for st in stores:
         st.wait()
-
-
-def back(gsum, osum, res, cot, x, vec, qkv, att, lse, in1, wq, wo, cos, sin, nf, ns, cid):
+    if left:
+        for p in range(3):
+            rest_out(jnp.int32(p), lambda cc: cc.wait())
+
+
+def back(gsum, osum, res, cot, x, vec, qkv, att, lse, in1, wq, wo, cos, sin, rest, ggu, gd, nf, ns, cid):
+    left = 0 if rest is None else 1
     tok, width = x.shape
     length, cols = att.shape
     wz = width // nf
@@ -1057,16 +1227,24 @@
     A = pl.BlockSpec(memory_space=pl.ANY)
     M = pl.BlockSpec(memory_space=pltpu.VMEM)
     S = jax.ShapeDtypeStruct
+    extra_in, extra_out, extra_scratch = (), (), []
+    if left:
+        r = rest.shape[1]
+        extra_in = (rest, ggu, gd)
+        extra_out = (S(ggu.shape, f32), S(gd.shape, f32))
+        extra_scratch = [V((3, r, width), bf16), V((3, nf - 1, r, wz), bf16), V((3, nf - 1, r, wz), bf16),
+                         V((3, r, wz), f32), D((3,))] + [D((3, nf - 1))] * 4
     rows_v = V((m, tok, width), bf16)
     offs_v = V((m - 1, tok, width), bf16)
     return pl.pallas_call(
-        functools.partial(back_kernel, nf, ns),
+        functools.partial(back_kernel, nf, ns, left),
         out_shape=(
             S((tok, width), bf16), S((tok, width), f32), S((3, wz, cols), f32), S((cols, wz), f32),
             S((1, w), f32), S((1, w), f32), S((1, w), f32), S((1, w), f32), S((3, w), f32),
-        ),
-        in_specs=[A] * 14,
-        out_specs=[A] * 4 + [M] * 5,
+        ) + extra_out,
+        in_specs=[A] * (14 + 3 * left),
+        out_specs=[A] * 4 + [M] * 5 + [A] * (2 * left),
+        input_output_aliases={15: 9, 16: 10} if left else {},
         scratch_shapes=[
             rows_v, rows_v, V((tok, width), f32), V((tok, width), bf16), V((8, width), f32),
             V((3, length, cols), bf16), V((length, cols), bf16), V((length, LANES), f32), V((2, length, wz), bf16),
@@ -1079,11 +1257,12 @@
             V((2 * tok, width), bf16), V((tok, width), f32),
             V((8, width), f32), V((nf * ns, 8, LANES), f32),
             D((11,)), D((2 * m,)), D((2,)), D((nf * ns,)), D((nf * ns,)),
-        ] + [D((count, nf - 1))] * 4 + [D((m,))] * 16 + [D((2,)), D((2,))],
+        ] + [D((count, nf - 1))] * 4 + [D((m,))] * 4 + [D((m,)), D((m,)), D((2 * m,)), D((2 * m,))] * 3 + [D((2,)), D((2,))]
+        + extra_scratch,
         compiler_params=pltpu.CompilerParams(
             collective_id=cid, has_side_effects=True, vmem_limit_bytes=64 * 1024 * 1024 - 65536),
         name="back",
-    )(gsum, osum, res, cot, x, vec, qkv, att, lse, in1, wq, wo, cos, sin)
+    )(gsum, osum, res, cot, x, vec, qkv, att, lse, in1, wq, wo, cos, sin, *extra_in)
 
 
 def local(
@@ -1100,7 +1279,9 @@
     down_weight,
 ):
     fsdp, seq = lax.axis_size("fsdp"), lax.axis_size("seq")
-    (in_one, cot_all, in_two, qkv, mixed, logs, residual, qkv_full, out_full, vectors, cosine, sine) = front(
+    gate_up = jnp.transpose(gate_up_weight, (1, 2, 0))
+    left = 1 if seq * block_input.shape[1] <= 1024 else 0
+    (in_one, cot_all, in_two, qkv, mixed, logs, residual, qkv_full, out_full, vectors, cosine, sine, first) = front(
         block_input[0],
         cotangent[0],
         ln1_gain[None],
@@ -1110,14 +1291,16 @@
         qkv_bias,
         jnp.transpose(qkv_weight, (1, 0, 2)),
         out_weight,
+        gate_up,
+        down_weight,
         fsdp,
         seq,
         1,
     )
-    out_sum, grad_sum, grad_gate_up, grad_down = mlp(
-        in_two, cot_all, jnp.transpose(gate_up_weight, (1, 2, 0)), down_weight, fsdp, 0
+    out_sum, grad_sum, grad_gate_up, grad_down, *rest = mlp(
+        in_two, cot_all, first, gate_up, down_weight, fsdp, left, 0
     )
-    block_output, input_grad, grad_qkv, grad_out, gain_one, bias_one, gain_two, bias_two, grad_bias = back(
+    block_output, input_grad, grad_qkv, grad_out, gain_one, bias_one, gain_two, bias_two, grad_bias, *grads = back(
         grad_sum,
         out_sum,
         residual,
@@ -1132,10 +1315,15 @@
         out_full,
         cosine,
         sine,
+        rest[0] if left else None,
+        grad_gate_up,
+        grad_down,
         fsdp,
         seq,
         2,
     )
+    if left:
+        grad_gate_up, grad_down = grads
     return (
         block_output[None],
         input_grad[None],

time: 570 us -> 474 us (0.83)
  Pallas kernels: 549 us -> 452 us
    pallas_call x2, Pallas kernels: 403 us -> 314 us  [the longest x1 164 us: mlp(): pl.pallas_call(functools.partial(mlp_kernel, n, r, rb, left), out_shape=(...]
    pallas_call x1, Pallas kernels: 146 us -> 138 us  [front(): pl.pallas_call(functools.partial(front_kernel, nf, ns), out_shape=(S((len...]
where the time goes in v3:
time: 474 us; the launch traced here: 466 us
  Pallas kernels  452 us (95%)
  local copies, waits for them, and re-layouts  12.5 us (3%)
    pallas_call x1, Pallas kernels, mlp(): pl.pallas_call(functools.partial(mlp_kernel, n, r, rb, left), out_shape=(...  164 us
    pallas_call x1, Pallas kernels, back(): pl.pallas_call(functools.partial(back_kernel, nf, ns, left), out_shape=(S...  150 us
    pallas_call x1, Pallas kernels, front(): pl.pallas_call(functools.partial(front_kernel, nf, ns), out_shape=(S((len...  138 us
    unnamed x29, local copies, waits for them, and re-layouts  12.5 us

profile of v3, /device:TPU:0, one launch (start us, length us, event | category | flops | bytes accessed | tf_op | source)
XLA Modules:
  0.0 466.0 jit_solution(11207202134210254471)
XLA Ops:
  0.6 138.3 %front.1 = (bf16[1024,2048]{1,0:T(8,128)(2,1)}, bf16[1024,2048]{1,0:T(8,128)(2,1)}, bf16[1024,2048]{1,0:T(8,128)(2,1)}, bf16[3,1024,256]{2,1,0:T(8,128)(2,1)}, b...) custom-call(bf16[128,2048]{1,0:T(8,128)(2,1)} %bitcast.19, ...), custom_call_target="tpu_custom_call" | custom-call | tf_op jit(solution)/shard_map/front/pallas_call | solution.py:871
  139.0 163.6 %mlp.1 = (bf16[1024,2048]{1,0:T(8,128)(2,1)}, bf16[1024,2048]{1,0:T(8,128)(2,1)}, f32[2,704,512]{2,1,0:T(8,128)}, f32[704,512]{1,0:T(8,128)}, bf16[3,176,2048]{2,1,0:T(8,128)(2,1)}) custom-call(bf16[1024,2048]{1,0:T(8,128)(2,1)} %get-tuple-element.40.in2_hbm, bf16[1024,2048]{1,0:T(8,128)(2,1)} %get-tuple-element.41.cot_hbm, ...), custom_call_target="tpu_custom_call" | custom-call | tf_op jit(solution)/shard_map/mlp/pallas_call | solution.py:379
  302.6 150.4 %back.1 = (bf16[128,2048]{1,0:T(8,128)(2,1)}, f32[128,2048]{1,0:T(8,128)}, f32[3,512,256]{2,1,0:T(8,128)}, f32[256,512]{1,0:T(8,128)}, f32[1,64]{1,0:T(1,128)}, ...) custom-call(bf16[1024,2048]{1,0:T(8,128)(2,1)} %get-tuple-element.43, ...), custom_call_target="tpu_custom_call", output_to_operand_aliasing={{9}: (15, {}), {10}: (16, {})} | custom-call | tf_op jit(solution)/shard_map/back/pallas_call | solution.py:1239
  453.0 0.0 copy-start.8
  453.0 0.0 copy-start.7
  453.0 0.0 copy-start.2
  453.0 2.0 copy.37
  455.0 0.0 copy-start
  455.0 2.4 copy.38
  457.5 0.0 copy-done.8
  457.5 0.5 copy.39
  458.0 0.0 copy-done.7
  458.0 0.5 copy.40
  458.5 0.0 copy-done.2
  458.5 1.1 copy.41
  459.6 0.0 copy-done.4
  459.7 0.6 copy.42
  460.2 0.0 copy-done.3
  460.2 0.8 copy.43
  461.0 0.5 copy.44
  461.5 0.5 copy.45
  462.1 1.6 copy.46
  463.6 0.8 copy-done.1
  464.5 1.1 copy.47
  (8 shorter events, 0.0 us)
Async XLA Ops:
  453.0 4.5 copy-start.8
  453.0 5.0 %copy-start.7 = (f32[1,64]{1,0:T(1,128)S(1)}, f32[1,64]{1,0:T(1,128)}, u32[]{:S(2)}) copy-start(f32[1,64]{1,0:T(1,128)} %get-tuple-element.61) | copy-start | bytes 772
  453.0 5.5 %copy-start.2 = (f32[3,512,256]{2,1,0:T(8,128)S(1)}, f32[3,512,256]{2,1,0:T(8,128)}, u32[]{:S(2)}) copy-start(f32[3,512,256]{2,1,0:T(8,128)} %get-tuple-element.62) | copy-start | bytes 4718596
  455.0 4.6 copy-start.4
  455.0 5.2 %copy-start.3 = (f32[256,512]{1,0:T(8,128)S(1)}, f32[256,512]{1,0:T(8,128)}, u32[]{:S(2)}) copy-start(f32[256,512]{1,0:T(8,128)} %get-tuple-element.86) | copy-start | bytes 1572868
  455.0 6.0 %copy-start.6 = (f32[1,64]{1,0:T(1,128)S(1)}, f32[1,64]{1,0:T(1,128)}, u32[]{:S(2)}) copy-start(f32[1,64]{1,0:T(1,128)} %get-tuple-element.65) | copy-start | bytes 772
  455.0 6.5 %copy-start.5 = (f32[1,64]{1,0:T(1,128)S(1)}, f32[1,64]{1,0:T(1,128)}, u32[]{:S(2)}) copy-start(f32[1,64]{1,0:T(1,128)} %get-tuple-element.66) | copy-start | bytes 772
  455.0 7.0 %copy-start = (f32[2,704,512]{2,1,0:T(8,128)S(1)}, f32[2,704,512]{2,1,0:T(8,128)}, u32[]{:S(2)}) copy-start(f32[2,704,512]{2,1,0:T(8,128)} %get-tuple-element.67) | copy-start | bytes 8650756
  462.1 2.4 copy-start.1

commit v4 on v3

--- a/solution.py
+++ b/solution.py
@@ -82,7 +82,7 @@
                 self.own(t, lambda src: self.copy(src, t, 0, f, False).start())
 
     def arrivals(self, t):
-        for h in range(1, self.n):
+        for h in range(self.n - 1, 0, -1):
             self.arrive(t - h, h)
 
     def tick(self, t):
@@ -144,49 +144,54 @@
 
         @pl.when((p >= 0) & (p < count))
         def _():
-            for j in range(n - 1, 0, -1):
+            @pl.loop(0, n - 1)
+            def _(i):
+                j = n - 1 - i
+
                 @pl.when((f > 0) & (j >= f))
-                def _(j=j):
+                def _():
                     self.right(p, j).wait_recv()
 
                 @pl.when((f > 0) & (j > f))
-                def _(j=j):
+                def _():
                     here = self.block(p, j)
                     here[...] = (here[...].astype(f32) + self.from_left[p, j - 1].astype(f32)).astype(bf16)
 
                 @pl.when(j > f)
-                def _(j=j):
+                def _():
                     self.right(p, j).start()
 
         q = u - (n - 1 - f)
 
         @pl.when((q >= 0) & (q < count))
         def _():
-            for j in range(0, n - 1):
+            @pl.loop(0, n - 1)
+            def _(j):
                 @pl.when((f < n - 1) & (j <= f))
-                def _(j=j):
+                def _():
                     self.left(q, j).wait_recv()
 
                 @pl.when((f < n - 1) & (j < f))
-                def _(j=j):
+                def _():
                     here = self.block(q, j)
                     here[...] = (here[...].astype(f32) + self.from_right[q, j].astype(f32)).astype(bf16)
 
                 @pl.when(j < f)
-                def _(j=j):
+                def _():
                     self.left(q, j).start()
 
         e = u - (n - 1)
 
         @pl.when((e >= 0) & (e < count))
         def _():
-            for j in range(n):
+            @pl.loop(0, n)
+            def _(j):
                 @pl.when(j > f)
-                def _(j=j):
+                def _():
                     self.right(e, j).wait_send()
 
                 @pl.when(j < f)
-                def _(j=j):
+                def _():
                     self.left(e, j).wait_send()
             self.finish(e)
 
@@ -241,7 +246,7 @@
                         (ag_sr, ag_rr, ag_sl, ag_rl))
 
     def block(p, j):
-        return parts.at[lax.rem(p, ring), :, pl.ds(j * wz, wz)]
+        return parts.at[lax.rem(p, ring), :, pl.ds(pl.multiple_of(j * wz, wz), wz)]
 
     def stage_out(p, act):
         kind = lax.rem(p, 3)
@@ -307,46 +312,40 @@
             acc_o[rows, :] = (acc_o[rows, :].astype(f32) + dot_nn(h, w[3 * c + 2])).astype(acc_o.dtype)
             acc_g[rows, :] = (acc_g[rows, :].astype(f32) + dot_nn(dg, w[3 * c]) + dot_nn(du, w[3 * c + 1])).astype(acc_g.dtype)
 
+    @pl.loop(0, nc)
+    def _(c):
+        compute(c)
+
         @pl.when(c == 0)
         def _():
             gather.arrivals(1)
-
         for k, (small, big) in enumerate(((dga, in2), (dup, in2), (hid, cot))):
             for j in range(n):
                 block(3 * c + k, j)[...] = dot_tn(small[...], big[:, pl.ds(j * wz, wz)]).astype(bf16)
-
-    @pl.loop(0, nc)
-    def _(c):
-        compute(c)
-
-        @pl.when(c == 0)
-        def _():
-            gather.arrivals(2)
-
-        @pl.when(c == 0)
-        def _():
-            for t in range(3, ahead):
-                gather.tick(t)
-
-        @pl.when(c < nc - left)
-        def _():
-            @pl.loop(0, 3)
-            def _(k):
-                reduce.tick(3 * c + k)
-                gather.tick(3 * c + k + ahead)
+            reduce.tick(3 * c + k)
+            if k == 0:
+                @pl.when(c == 0)
+                def _():
+                    for t in range(2, ahead):
+                        if t < 3:
+                            gather.arrivals(t)
+                        else:
+                            gather.tick(t)
+            gather.tick(3 * c + k + ahead)
 
     in2[...] = acc_o[...].astype(bf16)
     cot[...] = acc_g[...].astype(bf16)
     stores = [pltpu.make_async_copy(in2, out_hbm, load_sems.at[0]),
               pltpu.make_async_copy(cot, gin_hbm, load_sems.at[1])]
     for k in range(3 * left):
-        stores.append(pltpu.make_async_copy(parts.at[(count - 3 + k) % ring], rest_hbm.at[k], rest_sems.at[k]))
+        stores.append(pltpu.make_async_copy(parts.at[(summed + k) % ring], rest_hbm.at[k], rest_sems.at[k]))
     for c in stores:
         c.start()
 
-    @pl.loop(0, n - 1)
-    def _(k):
-        reduce.tick(summed + k)
+    if left == 0:
+        @pl.loop(count, summed + n - 1)
+        def _(u):
+            reduce.tick(u)
 
     @pl.loop(0, count - 3)
     def _(p):
@@ -372,7 +371,7 @@
     rb = min(256, tokens)
     nc = ff // r
     count = 3 * nc
-    ring = min(count, 3 * ((n - 1 + 2) // 3) + 3)
+    ring = min(count, 3 * max((n - 1 + 2) // 3, left) + 3)
     any_spec = pl.BlockSpec(memory_space=pl.ANY)
     acc_dtype = f32 if tokens * width * 8 <= 20 * 2**20 else bf16
     D = pltpu.SemaphoreType.DMA
@@ -383,9 +382,9 @@
             jax.ShapeDtypeStruct((tokens, width), bf16),
             jax.ShapeDtypeStruct((2, ff, wz), f32),
             jax.ShapeDtypeStruct((ff, wz), f32),
-        ) + (jax.ShapeDtypeStruct((3, r, width), bf16),) * left,
+        ) + (jax.ShapeDtypeStruct((3 * left, r, width), bf16),) * min(left, 1),
         in_specs=[any_spec] * 5,
-        out_specs=[any_spec] * (4 + left),
+        out_specs=[any_spec] * (4 + min(left, 1)),
         scratch_shapes=[
             pltpu.VMEM((tokens, width), bf16),
             pltpu.VMEM((tokens, width), bf16),
@@ -401,7 +400,7 @@
             pltpu.VMEM((2, r, wz), f32),
             D((3,)),
             D((count,)),
-        ] + [D((count - 3, n - 1))] * 4 + [D((count - 3 * left, n - 1))] * 4 + [D((2,)), D((3,))],
+        ] + [D((count - 3, n - 1))] * 4 + [D((count - 3 * left, n - 1))] * 4 + [D((2,)), D((max(3 * left, 1),))],
         compiler_params=pltpu.CompilerParams(
             collective_id=cid, has_side_effects=True, vmem_limit_bytes=64 * 1024 * 1024 - 65536),
         name="mlp",
@@ -451,9 +450,14 @@
         return remote(src, self.slot(chip, self.c), self.send_o.at[d], self.recv_o.at[d],
                       {"seq": xor(self.j, d, self.m) * 2 + self.c})
 
-    def half(self, part, source, to):
+    def part_of(self, src, d, part):
+        half = self.tok // 2
+        return remote(src.at[pl.ds(part * half, half)], self.slot(self.j, self.c, part),
+                      self.send_o.at[2 * d + part], self.recv_o.at[2 * d + part],
+                      {"seq": xor(self.j, d, 4) * 2 + self.c})
+
+    def half(self, part, source, to, index):
         here = self.slot(xor(self.j, source, 4), self.c, part)
-        index = 0 if part else 3
         return remote(here, here, self.send_o.at[index], self.recv_o.at[index],
                       {"seq": xor(self.j, to, 4) * 2 + self.c})
 
@@ -462,34 +466,46 @@
                       {"seq": self.j * 2 + 1 - self.c})
 
     def start(self, src):
-        for d in range(1, 3 if self.square else self.m):
-            self.off(src, d, self.j).start()
+        if self.square:
+            for d, part in ((1, 0), (2, 1), (1, 1), (2, 0)):
+                self.part_of(src, d, part).start()
+        else:
+            for d in range(1, self.m):
+                self.off(src, d, self.j).start()
         self.sib(src, 0, self.c).start()
 
     def relay(self, d):
         chip = xor(self.j, d, self.m)
         here = self.slot(chip, self.c)
-        if self.square and d == 3:
-            self.half(0, 3, 2).wait_recv()
-            self.half(1, 3, 1).wait_recv()
+        if not self.square:
+            self.off(here, d, chip).wait_recv()
+        elif d == 3:
+            self.half(0, 3, 2, 6).wait_recv()
+            self.half(1, 3, 1, 7).wait_recv()
         else:
-            self.off(here, d, chip).wait_recv()
-            if self.square:
-                self.half(d - 1, d, 3 - d).start()
+            if d == 1:
+                for n in (1, 2):
+                    self.half(n - 1, n, n, 3 * n - 1).wait_recv()
+                    self.half(n - 1, n, 3 - n, 5 + n).start()
+            self.half(2 - d, d, d, d + 2).wait_recv()
         self.sib(here, d, self.c).start()
+
+    def arrived(self, d):
+        self.sib(self.slot(xor(self.j, d, self.m), 1 - self.c), d, 1 - self.c).wait_recv()
 
     def finish(self):
         for d in range(self.m):
-            self.sib(self.slot(xor(self.j, d, self.m), 1 - self.c), d, 1 - self.c).wait_recv()
+            self.arrived(d)
 
     def drain(self, src):
         for d in range(1, self.m):
-            chip = xor(self.j, d, self.m)
-            if not self.square or d < 3:
+            if not self.square:
                 self.off(src, d, self.j).wait_send()
-                if self.square:
-                    self.half(d - 1, d, 3 - d).wait_send()
-            self.sib(self.slot(chip, self.c), d, self.c).wait_send()
+            elif d < 3:
+                for part in range(2):
+                    self.part_of(src, d, part).wait_send()
+                self.half(d - 1, d, 3 - d, 5 + d).wait_send()
+            self.sib(self.slot(xor(self.j, d, self.m), self.c), d, self.c).wait_send()
         self.sib(src, 0, self.c).wait_send()
 
 
@@ -532,25 +548,30 @@
             def _(part=part):
                 self.half(d, part).start()
 
-    def total(self, own):
-        here = self.from_sib.at[0]
-        self.sib(here, 0).wait_recv()
-        value = own.astype(f32) + here[...].astype(f32)
+    def forward(self):
         if self.square:
             for part, d in ((0, 2), (1, 1)):
                 at = pl.ds(part * (self.tok // 2), self.tok // 2)
                 self.half(3, part).wait_recv()
                 self.from_sib[d, at] = (self.from_sib[d, at].astype(f32) + self.from_off[2, at].astype(f32)).astype(bf16)
                 self.half(d, part).start()
-            for d in (1, 2):
+
+    def collect(self, own):
+        here = self.from_sib.at[0]
+        self.sib(here, 0).wait_recv()
+        value = own.astype(f32) + here[...].astype(f32)
+        for d in (1, 2) if self.square else range(self.m - 1, 0, -1):
+            if self.square:
                 self.half(d, 0).wait_recv()
                 self.half(d, 1).wait_recv()
-                value = value + self.from_off[d - 1].astype(f32)
-            return value
-        for d in range(self.m - 1, 0, -1):
-            self.off(d).wait_recv()
+            else:
+                self.off(d).wait_recv()
             value = value + self.from_off[d - 1].astype(f32)
         return value
+
+    def total(self, own):
+        self.forward()
+        return self.collect(own)
 
     def drain(self, src_of):
         for d in range(self.m):
@@ -601,7 +622,7 @@
                  x_hbm, cot_hbm, g1, b1, g2, b2, qb, wqkv_hbm, wo_hbm, wgu_hbm, wd_hbm,
                  in1_hbm, cotall_hbm, in2_hbm, qkv_hbm, att_hbm, lse_hbm, res_hbm, wq_hbm, woall_hbm,
                  vec_hbm, cos_hbm, sin_hbm, w0_hbm,
-                 x, in1, tile, tiles, vecs, wq, wo, qkv, att, lse, cos, sin, part, keep, give,
+                 xall, in1, tile, tiles, vecs, wq, wo, qkv, att, lse, cos, sin, part, keep, give,
                  from_sib, from_off, res, in2, w0,
                  load_sems, own_sems, small_s, small_r,
                  ag_sr, ag_rr, ag_sl, ag_rl, m_sr, m_rr, m_sl, m_rl,
@@ -612,21 +633,21 @@
     me = f * ns + s
     m = ns // 2
     j, c = s // 2, s % 2
-    tok, width = x.shape
+    tok, width = x_hbm.shape
     length = in1.shape[0]
     cols = qkv.shape[2]
     wz = width // nf
     pairs = cols // LANES
     block_rows = 2 * tok
-    load = pltpu.make_async_copy(x_hbm, x, load_sems.at[0])
-    load.start()
+
+    last_piece = 3 * pairs
 
     def own(p, use):
-        use(wqkv_hbm.at[p] if p < 3 else wo_hbm)
+        use(wqkv_hbm.at[p % 3, :, pl.ds(p // 3 * LANES, LANES)] if p < last_piece else wo_hbm)
 
     def slot(p, source):
-        if p < 3:
-            return wq.at[p, pl.ds(pl.multiple_of(source * wz, wz), wz)]
+        if p < last_piece:
+            return wq.at[p % 3, pl.ds(pl.multiple_of(source * wz, wz), wz), pl.ds(p // 3 * LANES, LANES)]
         return wo.at[:, pl.ds(pl.multiple_of(source * wz, wz), wz)]
 
     def own_copy(p):
@@ -634,7 +655,7 @@
         own(p, lambda src: box.append(pltpu.make_async_copy(src, slot(p, f), own_sems.at[p])))
         return box[0]
 
-    for p in range(4):
+    for p in range(last_piece + 1):
         own_copy(p).start()
 
     r = w0.shape[1]
@@ -652,7 +673,7 @@
         return w0.at[p, :, pl.ds(pl.multiple_of(source * wz, wz), wz)]
 
     mlp_copies = [pltpu.make_async_copy(wgu_hbm.at[p, pl.ds(0, r)] if p < 2 else wd_hbm.at[pl.ds(0, r)],
-                                        mlp_slot(p, f), own_sems.at[4 + p]) for p in range(3)]
+                                        mlp_slot(p, f), own_sems.at[last_piece + 1 + p]) for p in range(3)]
     for copy in mlp_copies:
         copy.start()
     cot_rows = pl.ds(pl.multiple_of(s * tok, tok), tok)
@@ -667,9 +688,9 @@
         tile[row:row + 1, :] = jnp.where(here, wide, 0.0)
 
     everyone_barrier(me, nf, ns)
-    gather = LineGather(f, nf, 4, own, slot, (ag_sr, ag_rr, ag_sl, ag_rl))
+    gather = LineGather(f, nf, last_piece + 1, own, slot, (ag_sr, ag_rr, ag_sl, ag_rl))
     second = LineGather(f, nf, 3, mlp_own, mlp_slot, (m_sr, m_rr, m_sl, m_rl))
-    gather.tick(0)
+    mine = pl.ds(pl.multiple_of(s * tok, tok), tok)
 
     def small(k):
         t = lax.rem(me + k, total)
@@ -678,90 +699,98 @@
     @pl.loop(1, total)
     def _(k):
         small(k).start()
+    for t in range(3):
+        gather.send_own(t)
+    rows_x = RowGather(s, m, tok, xall, (a_so, a_ro, a_ss, a_rs))
+    rows_x.start(x_hbm)
+    x_own = pltpu.make_async_copy(x_hbm, xall.at[mine], load_sems.at[3])
+    x_own.start()
     cot_own.start()
     tiles[0] = tile[...]
-    for q in range(length // block_rows):
-        rows = pl.ds(q * block_rows, block_rows)
-        cos[rows, :], sin[rows, :] = rotary_tiles(block_rows, q * block_rows)
-    stores = [pltpu.make_async_copy(cos, cos_hbm, out_sems.at[0]), pltpu.make_async_copy(sin, sin_hbm, out_sems.at[1])]
-    for st in stores:
+    vecs[...] = jnp.zeros_like(vecs)
+    stores = []
+
+    def store(ref, hbm, i):
+        st = pltpu.make_async_copy(ref, hbm, out_sems.at[i])
         st.start()
+        stores.append(st)
+
+    state = [2]
+
+    def ticks_to(t):
+        while state[0] < t:
+            state[0] += 1
+            gather.tick(state[0])
+
+    gather.arrivals(1)
 
     @pl.loop(1, total)
     def _(k):
         small(k).wait_recv()
-    vecs[...] = jnp.zeros_like(vecs)
 
     @pl.loop(0, total)
     def _(k):
         source = lax.rem(me + total - k, total)
         lanes = pl.ds(pl.multiple_of(source // spread * LANES, LANES), LANES)
         vecs[:, lanes] += tiles[k]
-
-    def store(ref, hbm, i):
-        st = pltpu.make_async_copy(ref, hbm, out_sems.at[i])
-        st.start()
-        stores.append(st)
-
     store(vecs, vec_hbm, 2)
-    load.wait()
-    normed, _ = normed_rows(x[...].astype(f32))
-    mine = pl.ds(pl.multiple_of(s * tok, tok), tok)
-    in1[mine, :] = (normed * vecs[0:1, :] + vecs[1:2, :]).astype(bf16)
-    rows_in = RowGather(s, m, tok, in1, (a_so, a_ro, a_ss, a_rs))
-    rows_in.start(in1.at[mine])
+    gather.arrivals(2)
+
+    @pl.loop(0, length // block_rows)
+    def _(q):
+        rows = pl.ds(pl.multiple_of(q * block_rows, block_rows), block_rows)
+        cos[rows, :], sin[rows, :] = rotary_tiles(block_rows, q * block_rows)
+    store(cos, cos_hbm, 0)
+    store(sin, sin_hbm, 1)
     rows_cot = RowGather(s, m, tok, cotall_hbm, (c_so, c_ro, c_ss, c_rs))
-    rows_cot.start(cot_hbm)
-    gather.tick(1)
-    for d in range(1, m):
-        rows_in.relay(d)
-        if d == 2:
-            gather.tick(2)
-    if m <= 2:
-        gather.tick(2)
-    rows_in.finish()
+
+    def norm_chip(d):
+        @pl.loop(0, 2)
+        def _(core):
+            rows = pl.ds(pl.multiple_of((xor(j, d, m) * 2 + core) * tok, tok), tok)
+            normed, _ = normed_rows(xall[rows, :].astype(f32))
+            in1[rows, :] = (normed * vecs[0:1, :] + vecs[1:2, :]).astype(bf16)
+
+    x_own.wait()
+    for d in range(m):
+        if d > 0:
+            rows_x.relay(d)
+        if d == min(2, m - 1):
+            rows_cot.start(cot_hbm)
+            ticks_to(min(3, nf + 1))
+        if d > 2:
+            rows_x.arrived(d - 1)
+            norm_chip(d - 1)
+            ticks_to(min(1 + d, nf + 1))
+        elif d > 0:
+            rows_x.arrived(d - 1)
+            norm_chip(d - 1)
+    rows_x.arrived(m - 1)
+    norm_chip(m - 1)
     store(in1, in1_hbm, 3)
-    bias_at = pl.ds(pl.multiple_of(s * cols, LANES), cols)
-
-    def project(k):
-        own_copy(k).wait()
+
+    def project(g):
+        lanes = slice(g * LANES, (g + 1) * LANES)
+        bias_at = pl.ds(pl.multiple_of(s * cols + g * LANES, LANES), LANES)
+        for k in range(3):
+            own_copy(3 * g + k).wait()
 
         @pl.loop(0, length // block_rows)
         def _(q):
             rows = pl.ds(pl.multiple_of(q * block_rows, block_rows), block_rows)
-            value = dot_nn(in1[rows, :], wq[k]) + vecs[4 + k:5 + k, bias_at]
-            for g in range(pairs):
-                lanes = slice(g * LANES, (g + 1) * LANES)
-                u = value[:, lanes]
+            for k in range(3):
+                u = dot_nn(in1[rows, :], wq[k, :, lanes]) + vecs[4 + k:5 + k, bias_at]
                 if k < 2:
                     u = turn(u, cos[rows, :], sin[rows, :], 1.0)
                 qkv[k, rows, lanes] = u.astype(bf16)
 
-    relays = list(range(1, m))
-    last = 2
-    for k in range(3):
-        while last < k + nf - 1:
-            last += 1
-            gather.tick(last)
-        project(k)
-        if relays:
-            rows_cot.relay(relays.pop(0))
-    while last < 3 + nf - 1:
-        last += 1
-        gather.tick(last)
-    own_copy(3).wait()
-    second.tick(jnp.int32(0))
-    while relays:
-        rows_cot.relay(relays.pop(0))
-    store(qkv, qkv_hbm, 4)
-    store(wq, wq_hbm, 5)
-    store(wo, woall_hbm, 6)
-
-    def attend(b):
+    ticks_to(2 + nf - 1)
+    project(0)
+
+    def attend(b, g):
         rows = pl.ds(b * block_rows, block_rows)
 
-        @pl.loop(0, pairs)
-        def _(g):
+        if True:
             lanes = pl.ds(pl.multiple_of(g * LANES, LANES), LANES)
             q, kd, vd = qkv[0, rows, lanes], qkv[1, rows, lanes], qkv[2, rows, lanes]
             lane = lane_of((block_rows, LANES))
@@ -794,32 +823,62 @@
     lse[...] = jnp.zeros_like(lse)
     sums = RowReduce(s, m, from_sib, from_off, (r_ss, r_rs, r_so, r_ro))
 
-    @pl.loop(0, m)
-    def _(step):
+    @pl.loop(0, (pairs + 1) * m)
+    def _(turn_here):
+        g, step = turn_here // m, lax.rem(turn_here, m)
         d = m - 1 - step
         chip = xor(j, d, m)
+
+        for later in range(1, pairs):
+            @pl.when((g == later) & (step == 0))
+            def _(later=later):
+                project(later)
         for b in range(m):
-            @pl.when(chip == b)
+            @pl.when((g < pairs) & (chip == b))
             def _(b=b):
-                attend(b)
-        rows = pl.ds(pl.multiple_of(chip * block_rows, block_rows), block_rows)
-        part[...] = dot_nn(att[rows, :], wo[...])
-        give[d] = part[pl.ds(pl.multiple_of((1 - c) * tok, tok), tok), :].astype(bf16)
-        keep[d] = part[pl.ds(pl.multiple_of(c * tok, tok), tok), :]
-        sums.give(d, give.at[d])
-
-        @pl.when((step > 0))
-        def _():
-            sums.pass_on(d + 1, keep[d + 1])
-
-        @pl.when(step % 2 == 1)
-        def _():
-            second.tick((step + 1) // 2)
-    ticks = list(range(m // 2 + 1, 3 + nf - 1))
+                attend(b, g)
+
+        for later in range(1, pairs):
+            for t in range(3 * later + nf - 1, 3 * later + nf + 2):
+                @pl.when((g == later - 1) & (step == min(t - 3 * later - nf + 1, m - 1)))
+                def _(t=t):
+                    gather.tick(t)
+                    if t == last_piece + nf - 2:
+                        for p in range(3):
+                            second.send_own(jnp.int32(p))
+        for k in range(1, m):
+            @pl.when((g == (0 if k < m - 1 else pairs - 1)) & (step == k))
+            def _(k=k):
+                rows_cot.relay(k)
+
+        @pl.when((g == pairs) & (step == 0))
+        def _():
+            gather.tick(last_piece + nf - 1)
+            own_copy(last_piece).wait()
+            if pairs == 1:
+                for p in range(3):
+                    second.send_own(jnp.int32(p))
+
+        @pl.when(g == pairs)
+        def _():
+            rows = pl.ds(pl.multiple_of(chip * block_rows, block_rows), block_rows)
+            part[...] = dot_nn(att[rows, :], wo[...])
+            give[d] = part[pl.ds(pl.multiple_of((1 - c) * tok, tok), tok), :].astype(bf16)
+            keep[d] = part[pl.ds(pl.multiple_of(c * tok, tok), tok), :]
+            sums.give(d, give.at[d])
+
+            @pl.when(step > 0)
+            def _():
+                sums.pass_on(d + 1, keep[d + 1])
+    second.arrivals(jnp.int32(1))
+    ticks = list(range(2, 3 + nf - 1))
+    store(qkv, qkv_hbm, 4)
+    store(wq, wq_hbm, 5)
+    store(wo, woall_hbm, 6)
     store(att, att_hbm, 7)
     store(lse, lse_hbm, 8)
     rows_cot.finish()
-    res[...] = x[...].astype(f32) + sums.total(keep[0])
+    res[...] = xall[mine, :].astype(f32) + sums.total(keep[0])
     store(res, res_hbm, 9)
     normed, _ = normed_rows(res[...])
     in2[...] = (normed * vecs[2:3, :] + vecs[3:4, :]).astype(bf16)
@@ -828,14 +887,14 @@
     in2_own = pltpu.make_async_copy(in2, in2_hbm.at[mine], load_sems.at[2])
     in2_own.start()
     if ticks:
-        second.tick(jnp.int32(ticks.pop(0)))
+        second.arrivals(jnp.int32(ticks.pop(0)))
     for d in range(1, m):
         rows_two.relay(d)
         if ticks and d < m - 1:
-            second.tick(jnp.int32(ticks.pop(0)))
+            second.arrivals(jnp.int32(ticks.pop(0)))
     rows_two.finish()
     for t in ticks:
-        second.tick(jnp.int32(t))
+        second.arrivals(jnp.int32(t))
     for copy in mlp_copies:
         copy.wait()
     store(w0, w0_hbm, 10)
@@ -843,11 +902,11 @@
     @pl.loop(1, total)
     def _(k):
         small(k).wait_send()
-    for p in range(4):
+    for p in range(last_piece + 1):
         gather.drain(p)
     for p in range(3):
         second.drain(p)
-    rows_in.drain(in1.at[mine])
+    rows_x.drain(x_hbm)
     rows_cot.drain(cot_hbm)
     rows_two.drain(in2)
     sums.drain(lambda d: give.at[d])
@@ -864,6 +923,7 @@
     length = tok * ns
     m = ns // 2
     w = g1.shape[1]
+    pairs = cols // LANES
     D, V = pltpu.SemaphoreType.DMA, pltpu.VMEM
     A = pl.BlockSpec(memory_space=pl.ANY)
     M = pl.BlockSpec(memory_space=pltpu.VMEM)
@@ -879,14 +939,14 @@
         in_specs=[A, A, M, M, M, M, M, A, A, A, A],
         out_specs=[A] * 13,
         scratch_shapes=[
-            V((tok, width), bf16), V((length, width), bf16), V((8, LANES), f32), V((nf * ns, 8, LANES), f32),
+            V((length, width), bf16), V((length, width), bf16), V((8, LANES), f32), V((nf * ns, 8, LANES), f32),
             V((8, width), f32), V((3, width, cols), bf16), V((cols, width), bf16), V((3, length, cols), bf16),
             V((length, cols), bf16), V((length, LANES), f32), V((length, LANES), f32), V((length, LANES), f32),
             V((2 * tok, width), f32), V((m, tok, width), f32), V((m, tok, width), bf16),
             V((m, tok, width), bf16), V((m - 1, tok, width), bf16), V((tok, width), f32), V((tok, width), bf16),
             V((3, r, width), bf16),
-            D((3,)), D((7,)), D((nf * ns,)), D((nf * ns,)),
-        ] + [D((4, nf - 1))] * 4 + [D((3, nf - 1))] * 4 + [D((m,))] * 14 + [D((2 * m,))] * 2 + [D((11,))],
+            D((4,)), D((3 * pairs + 4,)), D((nf * ns,)), D((nf * ns,)),
+        ] + [D((3 * pairs + 1, nf - 1))] * 4 + [D((3, nf - 1))] * 4 + ([D((2 * m,))] * 2 + [D((m,))] * 2) * 3 + [D((m,))] * 2 + [D((2 * m,))] * 2 + [D((11,))],
         compiler_params=pltpu.CompilerParams(
             collective_id=cid, has_side_effects=True, vmem_limit_bytes=64 * 1024 * 1024 - 65536),
         name="front",
@@ -903,9 +963,9 @@
     else:
         (out_hbm, ig_hbm, gqkv_hbm, gout_hbm, o_g1, o_b1, o_g2, o_b2, o_qb) = more[:9]
         more = more[9:]
-    (gkeep, okeep, res, cot, vec, qkv, att, lse, in1, wq, wo, cos, sin,
+    (keep, res, cot, vec, qkv, att, lse, in1, wq, wo, cos, sin,
                 grows, ga, gq, dk, dv, parts, from_left, from_right, stage, stage_t,
-                g_sib, g_off, o_sib, o_off, i_sib, i_off, part, gres, sums, tiles,
+                g_sib, g_off, o_sib, o_off, i_sib, i_off, gres, sums, tiles,
                 load_sems, keep_sems, in1_sems, small_s, small_r,
                 rs_sr, rs_rr, rs_sl, rs_rl,
                 w_so, w_ro, w_ss, w_rs,
@@ -928,11 +988,11 @@
     def rows_at(ref, chip, core):
         return ref.at[pl.ds(pl.multiple_of((chip * 2 + core) * tok, tok), tok)]
 
-    keeps = []
+    def keep_load(hbm, d, at):
+        return pltpu.make_async_copy(rows_at(hbm, xor(j, d, m), c), keep.at[d], keep_sems.at[2 * d + at])
+
     for d in range(m - 1, -1, -1):
-        for i, (hbm, ref) in enumerate(((gsum_hbm, gkeep), (osum_hbm, okeep))):
-            keeps.append(pltpu.make_async_copy(rows_at(hbm, xor(j, d, m), c), ref.at[d], keep_sems.at[2 * d + i]))
-            keeps[-1].start()
+        keep_load(gsum_hbm, d, 0).start()
     plain = [(res_hbm, res), (cot_hbm, cot), (vec_hbm, vec), (wo_hbm, wo), (att_hbm, att), (qkv_hbm, qkv),
              (lse_hbm, lse), (wq_hbm, wq), (cos_hbm, cos), (sin_hbm, sin)]
     loads = [pltpu.make_async_copy(a, b, load_sems.at[i]) for i, (a, b) in enumerate(plain)]
@@ -953,32 +1013,39 @@
     waiting = []
     if left:
         r = rest.shape[1]
-        last_rows = pl.ds(gd_hbm.shape[0] - r, r)
+        first_row = gd_hbm.shape[0] - left * r
 
         def rest_out(p, act):
-            @pl.when(p < 2)
+            kind, sl = lax.rem(p, 3), lax.rem(p, 2)
+            at = pl.ds(pl.multiple_of(first_row + p // 3 * r, 16), r)
+
+            @pl.when(kind < 2)
             def _():
-                act(pltpu.make_async_copy(rest_stage.at[p], ggu_hbm.at[p, last_rows], rest_sems.at[p]))
-
-            @pl.when(p == 2)
+                act(pltpu.make_async_copy(rest_stage.at[sl], ggu_hbm.at[kind, at], rest_sems.at[sl]))
+
+            @pl.when(kind == 2)
             def _():
-                act(pltpu.make_async_copy(rest_stage.at[p], gd_hbm.at[last_rows], rest_sems.at[p]))
+                act(pltpu.make_async_copy(rest_stage.at[sl], gd_hbm.at[at], rest_sems.at[sl]))
 
         def rest_finish(p):
-            rest_stage[p] = rest[p, :, pl.ds(pl.multiple_of(f * wz, wz), wz)].astype(f32)
+            @pl.when(p >= 2)
+            def _():
+                rest_out(p - 2, lambda cc: cc.wait())
+            sl = lax.rem(p, 2)
+            rest_stage[sl] = rest[p, :, pl.ds(pl.multiple_of(f * wz, wz), wz)].astype(f32)
 
             @pl.when(f > 0)
             def _():
-                rest_stage[p] += rest_left[p, jnp.maximum(f - 1, 0)].astype(f32)
+                rest_stage[sl] += rest_left[p, jnp.maximum(f - 1, 0)].astype(f32)
 
             @pl.when(f < nf - 1)
             def _():
-                rest_stage[p] += rest_right[p, jnp.minimum(f, nf - 2)].astype(f32)
+                rest_stage[sl] += rest_right[p, jnp.minimum(f, nf - 2)].astype(f32)
             rest_out(p, lambda cc: cc.start())
 
-        rest_sum = LineReduce(f, nf, 3, lambda p, k: rest.at[p, :, pl.ds(k * wz, wz)], rest_left, rest_right,
+        rest_sum = LineReduce(f, nf, 3 * left, lambda p, k: rest.at[p, :, pl.ds(pl.multiple_of(k * wz, wz), wz)], rest_left, rest_right,
                               (q_sr, q_rr, q_sl, q_rl), rest_finish)
-        waiting = list(range(3 + nf - 1))
+        waiting = list(range(3 * left + nf - 1))
 
     def rest_tick(how_many=1):
         for _ in range(how_many):
@@ -996,10 +1063,11 @@
     if left:
         rest_load.wait()
     rest_tick()
-    for keep in keeps:
-        keep.wait()
+    for d in range(m - 1, -1, -1):
+        keep_load(gsum_hbm, d, 0).wait()
     for d in range(m - 1, 0, -1):
-        two.pass_on(d, gkeep[d])
+        two.pass_on(d, keep[d])
+    two.forward()
     for d in range(m - 1, -1, -1):
         out.give(d, out_src(d))
     rest_tick()
@@ -1007,7 +1075,9 @@
         load.wait()
     sums[...] = jnp.zeros_like(sums)
     normed, inverse = normed_rows(res[...])
-    grad = two.total(gkeep[0])
+    grad = two.collect(keep[0])
+    for d in range(m - 1, -1, -1):
+        keep_load(osum_hbm, d, 1).start()
     sums[2:3, :] = jnp.sum(grad * normed, axis=0, keepdims=True)
     sums[3:4, :] = jnp.sum(grad, axis=0, keepdims=True)
 
@@ -1023,17 +1093,11 @@
     rows_w = RowGather(s, m, tok, grows, (w_so, w_ro, w_ss, w_rs))
     rows_w.start(grows.at[mine])
     rest_tick()
-    for d in range(1, m):
-        rows_w.relay(d)
-        rest_tick()
-    rows_w.finish()
-    for d in range(m - 1, 0, -1):
-        out.pass_on(d, okeep[d])
     for load in loads[3:]:
         load.wait()
 
     def block(p, k):
-        return parts.at[p, :, pl.ds(k * wz, wz)]
+        return parts.at[p, :, pl.ds(pl.multiple_of(k * wz, wz), wz)]
 
     def staged(p, act):
         sl = lax.rem(p, 2)
@@ -1071,103 +1135,148 @@
 
     reduce = LineReduce(f, nf, count, block, from_left, from_right, (rs_sr, rs_rr, rs_sl, rs_rl), finish)
 
-    for k in range(nf):
-        lanes = slice(k * wz, (k + 1) * wz)
-        value = dot_tn(att[...], grows[:, lanes]).astype(bf16)
-        for g in range(pairs):
-            parts[g, :, lanes] = value[g * LANES:(g + 1) * LANES, :]
-    rest_tick(len(waiting))
-    for p in range(pairs):
-        reduce.tick(jnp.int32(p))
-
-    @pl.loop(0, m)
-    def _(b):
-        rows = pl.ds(pl.multiple_of(b * block_rows, block_rows), block_rows)
-        ga[rows, :] = dot_nt(grows[rows, :], wo[...]).astype(bf16)
-
-    @pl.loop(0, pairs)
-    def _(g):
+    def attend_back(b, g):
         lanes = pl.ds(pl.multiple_of(g * LANES, LANES), LANES)
-        dk[...] = jnp.zeros_like(dk)
-        dv[...] = jnp.zeros_like(dv)
         lane = lane_of((block_rows, LANES))
         seen = lane_of((block_rows, block_rows)) <= lax.broadcasted_iota(jnp.int32, (block_rows, block_rows), 0)
-        for b in range(m):
-            rows = pl.ds(b * block_rows, block_rows)
-            q = qkv[0, rows, lanes].astype(f32) * HEAD_DIM ** -0.5
-            go = ga[rows, lanes].astype(f32)
-            both = go * att[rows, lanes].astype(f32)
-            logs = lse[rows, :]
-            grad_q = jnp.zeros((block_rows, LANES), f32)
-            for h in range(PER):
-                head = lane // HEAD_DIM == h
-                qm = jnp.where(head, q, 0.0).astype(bf16)
-                gm = jnp.where(head, go, 0.0).astype(bf16)
-                delta = jnp.sum(jnp.where(head, both, 0.0), axis=1, keepdims=True)
-                log = jnp.sum(jnp.where(lane == g * PER + h, logs, 0.0), axis=1, keepdims=True)
-                acc = jnp.zeros((block_rows, LANES), f32)
-                spans = [(k, min(span, b * block_rows - k)) for k in range(0, b * block_rows, span)]
-                for first, size in spans + [(b * block_rows, block_rows)]:
-                    at = pl.ds(first, size)
-                    key, val = qkv[1, at, lanes], qkv[2, at, lanes]
-                    pr = jnp.exp(dot_nt(qm, key) - log)
-                    if first == b * block_rows:
-                        pr = jnp.where(seen, pr, 0.0)
-                    gp = dot_nt(gm, val)
-                    gs = (pr * (gp - delta)).astype(bf16)
-                    dv[at, :] += dot_tn(pr.astype(bf16), gm)
-                    dk[at, :] += dot_tn(gs, qm)
-                    acc = acc + dot_nn(gs, key)
-                grad_q = jnp.where(head, acc * HEAD_DIM ** -0.5, grad_q)
-            gq[0, rows, lanes] = turn(grad_q, cos[rows, :], sin[rows, :], -1.0).astype(bf16)
-        gq[1, :, lanes] = turn(dk[...], cos[...], sin[...], -1.0).astype(bf16)
-        gq[2, :, lanes] = dv[...].astype(bf16)
-        three = jnp.concatenate([gq[0, :, lanes], gq[1, :, lanes], gq[2, :, lanes]], axis=1)
+        rows = pl.ds(b * block_rows, block_rows)
+        q = qkv[0, rows, lanes].astype(f32) * HEAD_DIM ** -0.5
+        go = ga[rows, lanes].astype(f32)
+        both = go * att[rows, lanes].astype(f32)
+        logs = lse[rows, :]
+        grad_q = jnp.zeros((block_rows, LANES), f32)
+        for h in range(PER):
+            head = lane // HEAD_DIM == h
+            qm = jnp.where(head, q, 0.0).astype(bf16)
+            gm = jnp.where(head, go, 0.0).astype(bf16)
+            delta = jnp.sum(jnp.where(head, both, 0.0), axis=1, keepdims=True)
+            log = jnp.sum(jnp.where(lane == g * PER + h, logs, 0.0), axis=1, keepdims=True)
+            acc = jnp.zeros((block_rows, LANES), f32)
+            spans = [(k, min(span, b * block_rows - k)) for k in range(0, b * block_rows, span)]
+            for first, size in spans + [(b * block_rows, block_rows)]:
+                at = pl.ds(first, size)
+                key, val = qkv[1, at, lanes], qkv[2, at, lanes]
+                pr = jnp.exp(dot_nt(qm, key) - log)
+                if first == b * block_rows:
+                    pr = jnp.where(seen, pr, 0.0)
+                gp = dot_nt(gm, val)
+                gs = (pr * (gp - delta)).astype(bf16)
+                dv[at, :] += dot_tn(pr.astype(bf16), gm)
+                dk[at, :] += dot_tn(gs, qm)
+                acc = acc + dot_nn(gs, key)
+            grad_q = jnp.where(head, acc * HEAD_DIM ** -0.5, grad_q)
+        gq[0, rows, lanes] = turn(grad_q, cos[rows, :], sin[rows, :], -1.0).astype(bf16)
+
+    def weight_pieces(g):
+        lanes = pl.ds(pl.multiple_of(g * LANES, LANES), LANES)
+
+        @pl.loop(0, m)
+        def _(b):
+            rows = pl.ds(pl.multiple_of(b * block_rows, block_rows), block_rows)
+            gq[1, rows, lanes] = turn(dk[rows, :], cos[rows, :], sin[rows, :], -1.0).astype(bf16)
+            gq[2, rows, lanes] = dv[rows, :].astype(bf16)
+        at_once = 3 if length <= 1024 else 1
+        wide = [[gq[i, :, lanes] for i in range(3)]] if at_once == 3 else [[gq[i, :, lanes]] for i in range(3)]
         at = pl.ds(pl.multiple_of(s * cols + g * LANES, LANES), LANES)
         for k in range(3):
             sums[4 + k:5 + k, at] = jnp.sum(gq[k, :, lanes].astype(f32), axis=0, keepdims=True)
-
-        @pl.when(g > 0)
-        def _():
-            for k in range(3):
-                reduce.tick(pairs + 3 * (g - 1) + k)
         for k in range(nf):
             in1_load(k).wait()
             in1_load((k + 1) % nf).start()
-            value = dot_tn(three, in1[k % 2]).astype(bf16)
-            for i in range(3):
-                parts[pairs + 3 * g + i, :, k * wz:(k + 1) * wz] = value[i * LANES:(i + 1) * LANES, :]
+            for n, some in enumerate(wide):
+                value = dot_tn(jnp.concatenate(some, axis=1), in1[k % 2]).astype(bf16)
+                for i in range(at_once):
+                    parts[pairs + 3 * g + n + i, :, k * wz:(k + 1) * wz] = value[i * LANES:(i + 1) * LANES, :]
+
+    @pl.loop(0, pairs * m)
+    def _(turn_here):
+        g, step = turn_here // m, lax.rem(turn_here, m)
+        chip = xor(j, step, m)
+        rows = pl.ds(pl.multiple_of(chip * block_rows, block_rows), block_rows)
+
+        @pl.when(step == 0)
+        def _():
+            dk[...] = jnp.zeros_like(dk)
+            dv[...] = jnp.zeros_like(dv)
+        for d in range(m):
+            @pl.when((g == 0) & (step == d))
+            def _(d=d):
+                if d > 0:
+                    rows_w.relay(d)
+                rows_w.arrived(d)
+                if d > 0:
+                    rest_tick()
+
+        @pl.when(g == 0)
+        def _():
+            ga[rows, :] = dot_nt(grows[rows, :], wo[...]).astype(bf16)
+
+        @pl.when((g == 0) & (step == m - 1))
+        def _():
+            for d in range(m - 1, -1, -1):
+                keep_load(osum_hbm, d, 1).wait()
+            for d in range(m - 1, 0, -1):
+                out.pass_on(d, keep[d])
+            for k in range(nf):
+                lanes = slice(k * wz, (k + 1) * wz)
+                value = dot_tn(att[...], grows[:, lanes]).astype(bf16)
+                for i in range(pairs):
+                    parts[i, :, lanes] = value[i * LANES:(i + 1) * LANES, :]
+            rest_tick(len(waiting))
+            reduce.tick(jnp.int32(0))
+        for b in range(m):
+            @pl.when(chip == b)
+            def _(b=b):
+                attend_back(b, g)
+
+        @pl.when((g > 0) & (step % (m // 2) == m // 2 - 1))
+        def _():
+            reduce.tick(pairs + 3 * (g - 1) + 1 + (step + 1) // (m // 2) - 1)
+
+        @pl.when((g == pairs - 1) & (step == m - 1))
+        def _():
+            out.forward()
+
+        @pl.when(step == m - 1)
+        def _():
+            @pl.when(g == 0)
+            def _():
+                for p in range(1, pairs):
+                    reduce.tick(jnp.int32(p))
+            weight_pieces(g)
+            reduce.tick(pairs + 3 * g)
     in1_load(0).wait()
 
-    okeep[0] = (res[...] + out.total(okeep[0])).astype(bf16)
-    stores = [pltpu.make_async_copy(okeep.at[0], out_hbm, out_sems.at[0])]
+    keep[0] = (res[...] + out.collect(keep[0])).astype(bf16)
+    stores = [pltpu.make_async_copy(keep.at[0], out_hbm, out_sems.at[0])]
     stores[0].start()
     out.drain(out_src)
     one = RowReduce(s, m, i_sib, i_off, (i_ss, i_rs, i_so, i_ro))
-    late = list(range(pairs + 3 * (pairs - 1), count + nf - 1))
+    rows_w.drain(grows.at[mine])
+
+    def half_of(d, core):
+        return grows.at[pl.ds(pl.multiple_of((2 * d + core) * tok, tok), tok)]
+
+    late = list(range(pairs + 3 * (pairs - 1) + 1, count + nf - 1))
     for d in range(m - 1, -1, -1):
-        if late:
-            reduce.tick(jnp.int32(late.pop(0)))
         rows = pl.ds(pl.multiple_of(xor(j, d, m) * block_rows, block_rows), block_rows)
         value = dot_nt(gq[0, rows, :], wq[0])
         for k in (1, 2):
             value = value + dot_nt(gq[k, rows, :], wq[k])
-        part[...] = value.astype(bf16)
-        if d == 0:
-            stores.pop().wait()
-        okeep[d] = part[pl.ds(pl.multiple_of((1 - c) * tok, tok), tok), :]
-        gkeep[d] = part[pl.ds(pl.multiple_of(c * tok, tok), tok), :]
-        one.give(d, okeep.at[d])
+        grows[d * block_rows:(d + 1) * block_rows, :] = value.astype(bf16)
+        one.give(d, half_of(d, 1 - c))
         if d < m - 1:
-            one.pass_on(d + 1, gkeep[d + 1])
-    grad = one.total(gkeep[0])
+            one.pass_on(d + 1, half_of(d + 1, c)[...])
+        if late and d % 2 == 1:
+            reduce.tick(jnp.int32(late.pop(0)))
+    grad = one.total(half_of(0, c)[...])
     x_load.wait()
     normed, inverse = normed_rows(cot[...].astype(f32))
     sums[0:1, :] = jnp.sum(grad * normed, axis=0, keepdims=True)
     sums[1:2, :] = jnp.sum(grad, axis=0, keepdims=True)
     res[...] = gres[...] + norm_grad(grad, normed, inverse, vec[0:1, :])
     stores.append(pltpu.make_async_copy(res, ig_hbm, out_sems.at[1]))
-    stores[0].start()
+    stores[1].start()
 
     w = o_g1.shape[1]
     spread = LANES // w
@@ -1183,8 +1292,9 @@
     @pl.loop(1, total)
     def _(k):
         small(k).start()
-    for t in late:
-        reduce.tick(jnp.int32(t))
+    @pl.loop(late[0], late[-1] + 1)
+    def _(t):
+        reduce.tick(t)
     tiles[0] = tile_of(me)[...]
 
     @pl.loop(1, total)
@@ -1203,19 +1313,18 @@
     def _(k):
         small(k).wait_send()
     two.drain(two_src)
-    one.drain(lambda d: okeep.at[d])
-    rows_w.drain(grows.at[mine])
+    one.drain(lambda d: half_of(d, 1 - c))
     for p in (count - 2, count - 1):
         staged(jnp.int32(p), lambda cc: cc.wait())
     for st in stores:
         st.wait()
     if left:
-        for p in range(3):
+        for p in (3 * left - 2, 3 * left - 1):
             rest_out(jnp.int32(p), lambda cc: cc.wait())
 
 
 def back(gsum, osum, res, cot, x, vec, qkv, att, lse, in1, wq, wo, cos, sin, rest, ggu, gd, nf, ns, cid):
-    left = 0 if rest is None else 1
+    left = 0 if rest is None else rest.shape[0] // 3
     tok, width = x.shape
     length, cols = att.shape
     wz = width // nf
@@ -1232,8 +1341,8 @@
         r = rest.shape[1]
         extra_in = (rest, ggu, gd)
         extra_out = (S(ggu.shape, f32), S(gd.shape, f32))
-        extra_scratch = [V((3, r, width), bf16), V((3, nf - 1, r, wz), bf16), V((3, nf - 1, r, wz), bf16),
-                         V((3, r, wz), f32), D((3,))] + [D((3, nf - 1))] * 4
+        extra_scratch = [V((3 * left, r, width), bf16), V((3 * left, nf - 1, r, wz), bf16),
+                         V((3 * left, nf - 1, r, wz), bf16), V((2, r, wz), f32), D((2,))] + [D((3 * left, nf - 1))] * 4
     rows_v = V((m, tok, width), bf16)
     offs_v = V((m - 1, tok, width), bf16)
     return pl.pallas_call(
@@ -1242,11 +1351,11 @@
             S((tok, width), bf16), S((tok, width), f32), S((3, wz, cols), f32), S((cols, wz), f32),
             S((1, w), f32), S((1, w), f32), S((1, w), f32), S((1, w), f32), S((3, w), f32),
         ) + extra_out,
-        in_specs=[A] * (14 + 3 * left),
-        out_specs=[A] * 4 + [M] * 5 + [A] * (2 * left),
+        in_specs=[A] * (14 + len(extra_in)),
+        out_specs=[A] * 4 + [M] * 5 + [A] * len(extra_out),
         input_output_aliases={15: 9, 16: 10} if left else {},
         scratch_shapes=[
-            rows_v, rows_v, V((tok, width), f32), V((tok, width), bf16), V((8, width), f32),
+            rows_v, V((tok, width), f32), V((tok, width), bf16), V((8, width), f32),
             V((3, length, cols), bf16), V((length, cols), bf16), V((length, LANES), f32), V((2, length, wz), bf16),
             V((3, width, cols), bf16), V((cols, width), bf16), V((length, LANES), f32), V((length, LANES), f32),
             V((length, width), bf16), V((length, cols), bf16), V((3, length, cols), bf16),
@@ -1254,10 +1363,10 @@
             V((count, LANES, width), bf16), V((count, nf - 1, LANES, wz), bf16), V((count, nf - 1, LANES, wz), bf16),
             V((2, LANES, wz), f32), V((2, wz, LANES), f32),
             rows_v, offs_v, rows_v, offs_v, rows_v, offs_v,
-            V((2 * tok, width), bf16), V((tok, width), f32),
+            V((tok, width), f32),
             V((8, width), f32), V((nf * ns, 8, LANES), f32),
             D((11,)), D((2 * m,)), D((2,)), D((nf * ns,)), D((nf * ns,)),
-        ] + [D((count, nf - 1))] * 4 + [D((m,))] * 4 + [D((m,)), D((m,)), D((2 * m,)), D((2 * m,))] * 3 + [D((2,)), D((2,))]
+        ] + [D((count, nf - 1))] * 4 + [D((2 * m,))] * 2 + [D((m,))] * 2 + [D((m,)), D((m,)), D((2 * m,)), D((2 * m,))] * 3 + [D((2,)), D((2,))]
         + extra_scratch,
         compiler_params=pltpu.CompilerParams(
             collective_id=cid, has_side_effects=True, vmem_limit_bytes=64 * 1024 * 1024 - 65536),

time: 474 us -> 457 us (0.964)
  Pallas kernels: 452 us -> 435 us
    pallas_call x1, Pallas kernels: 138 us -> 132 us  [front(): pl.pallas_call(functools.partial(front_kernel, nf, ns), out_shape=(S((len...]
    pallas_call x1, Pallas kernels: 150 us -> 145 us  [back(): pl.pallas_call(functools.partial(back_kernel, nf, ns, left), out_shape=(S...]
    pallas_call x1, Pallas kernels: 164 us -> 159 us  [mlp(): pl.pallas_call(functools.partial(mlp_kernel, n, r, rb, left), out_shape=(...]
where the time goes in v4:
time: 457 us; the launch traced here: 449 us
  Pallas kernels  435 us (95%)
  local copies, waits for them, and re-layouts  12.5 us (3%)
    pallas_call x1, Pallas kernels, mlp(): pl.pallas_call(functools.partial(mlp_kernel, n, r, rb, left), out_shape=(...  159 us
    pallas_call x1, Pallas kernels, back(): pl.pallas_call(functools.partial(back_kernel, nf, ns, left), out_shape=(S...  145 us
    pallas_call x1, Pallas kernels, front(): pl.pallas_call(functools.partial(front_kernel, nf, ns), out_shape=(S((len...  132 us
    unnamed x29, local copies, waits for them, and re-layouts  12.5 us

profile of v4, /device:TPU:0, one launch (start us, length us, event | category | flops | bytes accessed | tf_op | source)
XLA Modules:
  0.0 449.1 jit_solution(6713138410376867980)
XLA Ops:
  0.6 132.0 %front.1 = (bf16[1024,2048]{1,0:T(8,128)(2,1)}, bf16[1024,2048]{1,0:T(8,128)(2,1)}, bf16[1024,2048]{1,0:T(8,128)(2,1)}, bf16[3,1024,256]{2,1,0:T(8,128)(2,1)}, b...) custom-call(bf16[128,2048]{1,0:T(8,128)(2,1)} %bitcast.19, ...), custom_call_target="tpu_custom_call" | custom-call | tf_op jit(solution)/shard_map/front/pallas_call | solution.py:931
  132.7 158.6 %mlp.1 = (bf16[1024,2048]{1,0:T(8,128)(2,1)}, bf16[1024,2048]{1,0:T(8,128)(2,1)}, f32[2,704,512]{2,1,0:T(8,128)}, f32[704,512]{1,0:T(8,128)}, bf16[3,176,2048]{2,1,0:T(8,128)(2,1)}) custom-call(bf16[1024,2048]{1,0:T(8,128)(2,1)} %get-tuple-element.40.in2_hbm, bf16[1024,2048]{1,0:T(8,128)(2,1)} %get-tuple-element.41.cot_hbm, ...), custom_call_target="tpu_custom_call" | custom-call | tf_op jit(solution)/shard_map/mlp/pallas_call | solution.py:378
  291.3 144.8 %back.1 = (bf16[128,2048]{1,0:T(8,128)(2,1)}, f32[128,2048]{1,0:T(8,128)}, f32[3,512,256]{2,1,0:T(8,128)}, f32[256,512]{1,0:T(8,128)}, f32[1,64]{1,0:T(1,128)}, ...) custom-call(bf16[1024,2048]{1,0:T(8,128)(2,1)} %get-tuple-element.43, ...), custom_call_target="tpu_custom_call", output_to_operand_aliasing={{9}: (15, {}), {10}: (16, {})} | custom-call | tf_op jit(solution)/shard_map/back/pallas_call | solution.py:1348
  436.0 0.0 copy-start.8
  436.0 0.0 copy-start.7
  436.1 0.0 copy-start.2
  436.1 2.0 copy.37
  438.1 0.0 copy-start
  438.1 2.4 copy.38
  440.5 0.0 copy-done.8
  440.5 0.5 copy.39
  441.0 0.0 copy-done.7
  441.1 0.5 copy.40
  441.6 0.0 copy-done.2
  441.6 1.1 copy.41
  442.7 0.0 copy-done.4
  442.7 0.6 copy.42
  443.3 0.8 copy.43
  444.1 0.0 copy-done.6
  444.1 0.5 copy.44
  444.6 0.5 copy.45
  445.1 1.6 copy.46
  446.7 0.8 copy-done.1
  447.5 1.1 copy.47
  (8 shorter events, 0.0 us)
Async XLA Ops:
  436.0 4.5 %copy-start.8 = (f32[1,64]{1,0:T(1,128)S(1)}, f32[1,64]{1,0:T(1,128)}, u32[]{:S(2)}) copy-start(f32[1,64]{1,0:T(1,128)} %get-tuple-element.60) | copy-start | bytes 772
  436.0 5.0 %copy-start.7 = (f32[1,64]{1,0:T(1,128)S(1)}, f32[1,64]{1,0:T(1,128)}, u32[]{:S(2)}) copy-start(f32[1,64]{1,0:T(1,128)} %get-tuple-element.61) | copy-start | bytes 772
  436.1 5.5 %copy-start.2 = (f32[3,512,256]{2,1,0:T(8,128)S(1)}, f32[3,512,256]{2,1,0:T(8,128)}, u32[]{:S(2)}) copy-start(f32[3,512,256]{2,1,0:T(8,128)} %get-tuple-element.62) | copy-start | bytes 4718596
  438.1 4.6 %copy-start.4 = (f32[3,64]{1,0:T(4,128)S(1)}, f32[3,64]{1,0:T(4,128)}, u32[]{:S(2)}) copy-start(f32[3,64]{1,0:T(4,128)} %get-tuple-element.85) | copy-start | bytes 2308
  438.1 5.2 %copy-start.3 = (f32[256,512]{1,0:T(8,128)S(1)}, f32[256,512]{1,0:T(8,128)}, u32[]{:S(2)}) copy-start(f32[256,512]{1,0:T(8,128)} %get-tuple-element.86) | copy-start | bytes 1572868
  438.1 6.0 %copy-start.6 = (f32[1,64]{1,0:T(1,128)S(1)}, f32[1,64]{1,0:T(1,128)}, u32[]{:S(2)}) copy-start(f32[1,64]{1,0:T(1,128)} %get-tuple-element.65) | copy-start | bytes 772
  438.1 6.5 %copy-start.5 = (f32[1,64]{1,0:T(1,128)S(1)}, f32[1,64]{1,0:T(1,128)}, u32[]{:S(2)}) copy-start(f32[1,64]{1,0:T(1,128)} %get-tuple-element.66) | copy-start | bytes 772
  438.1 7.0 %copy-start = (f32[2,704,512]{2,1,0:T(8,128)S(1)}, f32[2,704,512]{2,1,0:T(8,128)}, u32[]{:S(2)}) copy-start(f32[2,704,512]{2,1,0:T(8,128)} %get-tuple-element.67) | copy-start | bytes 8650756
  445.1 2.4 copy-start.1

commit v5 on v4

--- a/solution.py
+++ b/solution.py
@@ -196,7 +196,7 @@
             self.finish(e)
 
 
-def mlp_kernel(n, r, rb, left, in2_hbm, cot_hbm, w0_hbm, wgu_hbm, wd_hbm,
+def mlp_kernel(n, r, rb, head, left, in2_hbm, cot_hbm, w0_hbm, wgu_hbm, wd_hbm,
                out_hbm, gin_hbm, ggu_hbm, gd_hbm, *more):
     rest_hbm, more = (more[0], more[1:]) if left else (None, more)
     (in2, cot, acc_o, acc_g, w, hid, dga, dup, parts, from_left, from_right,
@@ -208,12 +208,12 @@
     ff = wd_hbm.shape[0]
     nc = ff // r
     count = 3 * nc
-    summed = count - 3 * left
+    summed = count - left
     ahead = max(n - 1, 3)
     ring = parts.shape[0]
     loads = [pltpu.make_async_copy(in2_hbm, in2, load_sems.at[0]),
              pltpu.make_async_copy(cot_hbm, cot, load_sems.at[1]),
-             pltpu.make_async_copy(w0_hbm, w.at[pl.ds(0, 3)], load_sems.at[2])]
+             pltpu.make_async_copy(w0_hbm, w.at[pl.ds(0, head)], load_sems.at[2])]
     for c in loads:
         c.start()
 
@@ -237,12 +237,12 @@
     def own_copy(p, act):
         own(p, lambda src: act(pltpu.make_async_copy(src, slot(p, f), own_sems.at[p])))
 
-    @pl.loop(3, count)
+    @pl.loop(head, count)
     def _(p):
         own_copy(p, lambda c: c.start())
 
     line_barrier(f, n)
-    gather = LineGather(f, n, count - 3, lambda p, use: own(p + 3, use), lambda p, source: slot(p + 3, source),
+    gather = LineGather(f, n, count - head, lambda p, use: own(p + head, use), lambda p, source: slot(p + head, source),
                         (ag_sr, ag_rr, ag_sl, ag_rl))
 
     def block(p, j):
@@ -292,7 +292,9 @@
         @pl.when(c > 0)
         def _():
             for k in range(3):
-                own_copy(3 * c + k, lambda cc: cc.wait())
+                @pl.when(3 * c + k >= head)
+                def _(k=k):
+                    own_copy(3 * c + k, lambda cc: cc.wait())
 
         @pl.loop(0, tokens // rb)
         def _(i):
@@ -320,24 +322,30 @@
         def _():
             gather.arrivals(1)
         for k, (small, big) in enumerate(((dga, in2), (dup, in2), (hid, cot))):
-            for j in range(n):
-                block(3 * c + k, j)[...] = dot_tn(small[...], big[:, pl.ds(j * wz, wz)]).astype(bf16)
+            @pl.loop(0, n)
+            def _(j, k=k, small=small, big=big):
+                lanes = pl.ds(pl.multiple_of(j * wz, wz), wz)
+                block(3 * c + k, j)[...] = dot_tn(small[...], big[:, lanes]).astype(bf16)
+
             reduce.tick(3 * c + k)
+            after = k + ahead - (head - 3)
             if k == 0:
                 @pl.when(c == 0)
                 def _():
-                    for t in range(2, ahead):
-                        if t < 3:
-                            gather.arrivals(t)
-                        else:
-                            gather.tick(t)
-            gather.tick(3 * c + k + ahead)
+                    for t in range(2, after + 1):
+                        gather.arrivals(t) if t < 3 else gather.tick(t)
+
+                @pl.when(c > 0)
+                def _():
+                    gather.tick(3 * c + after)
+            else:
+                gather.tick(3 * c + after)
 
     in2[...] = acc_o[...].astype(bf16)
     cot[...] = acc_g[...].astype(bf16)
     stores = [pltpu.make_async_copy(in2, out_hbm, load_sems.at[0]),
               pltpu.make_async_copy(cot, gin_hbm, load_sems.at[1])]
-    for k in range(3 * left):
+    for k in range(left):
         stores.append(pltpu.make_async_copy(parts.at[(summed + k) % ring], rest_hbm.at[k], rest_sems.at[k]))
     for c in stores:
         c.start()
@@ -347,7 +355,7 @@
         def _(u):
             reduce.tick(u)
 
-    @pl.loop(0, count - 3)
+    @pl.loop(0, count - head)
     def _(p):
         gather.drain(p)
     for p in (summed - 2, summed - 1):
@@ -365,24 +373,25 @@
 
 
 def mlp(in2, cot, w0, wgu, wd, n, left, cid):
+    head = w0.shape[0]
     tokens, width = in2.shape
     ff, wz = wd.shape
     r = piece_rows(ff)
     rb = min(256, tokens)
     nc = ff // r
     count = 3 * nc
-    ring = min(count, 3 * max((n - 1 + 2) // 3, left) + 3)
+    ring = min(count, 3 * max((n - 1 + 2) // 3, (left + 2) // 3) + 3)
     any_spec = pl.BlockSpec(memory_space=pl.ANY)
     acc_dtype = f32 if tokens * width * 8 <= 20 * 2**20 else bf16
     D = pltpu.SemaphoreType.DMA
     return pl.pallas_call(
-        functools.partial(mlp_kernel, n, r, rb, left),
+        functools.partial(mlp_kernel, n, r, rb, head, left),
         out_shape=(
             jax.ShapeDtypeStruct((tokens, width), bf16),
             jax.ShapeDtypeStruct((tokens, width), bf16),
             jax.ShapeDtypeStruct((2, ff, wz), f32),
             jax.ShapeDtypeStruct((ff, wz), f32),
-        ) + (jax.ShapeDtypeStruct((3 * left, r, width), bf16),) * min(left, 1),
+        ) + (jax.ShapeDtypeStruct((left, r, width), bf16),) * min(left, 1),
         in_specs=[any_spec] * 5,
         out_specs=[any_spec] * (4 + min(left, 1)),
         scratch_shapes=[
@@ -395,12 +404,12 @@
             pltpu.VMEM((tokens, r), bf16),
             pltpu.VMEM((tokens, r), bf16),
             pltpu.VMEM((ring, r, width), bf16),
-            pltpu.VMEM((count - 3 * left, n - 1, r, wz), bf16),
-            pltpu.VMEM((count - 3 * left, n - 1, r, wz), bf16),
+            pltpu.VMEM((count - left, n - 1, r, wz), bf16),
+            pltpu.VMEM((count - left, n - 1, r, wz), bf16),
             pltpu.VMEM((2, r, wz), f32),
             D((3,)),
             D((count,)),
-        ] + [D((count - 3, n - 1))] * 4 + [D((count - 3 * left, n - 1))] * 4 + [D((2,)), D((max(3 * left, 1),))],
+        ] + [D((count - head, n - 1))] * 4 + [D((count - left, n - 1))] * 4 + [D((2,)), D((max(left, 1),))],
         compiler_params=pltpu.CompilerParams(
             collective_id=cid, has_side_effects=True, vmem_limit_bytes=64 * 1024 * 1024 - 65536),
         name="mlp",
@@ -408,6 +417,7 @@
 
 
 LANES = 128
+HEAD_PIECES = 4
 PER = LANES // HEAD_DIM
 
 
@@ -658,22 +668,28 @@
     for p in range(last_piece + 1):
         own_copy(p).start()
 
-    r = w0.shape[1]
+    head, r = w0.shape[0], w0.shape[1]
 
     def mlp_own(p, use):
-        @pl.when(p < 2)
-        def _():
-            use(wgu_hbm.at[p, pl.ds(0, r)])
-
-        @pl.when(p == 2)
-        def _():
-            use(wd_hbm.at[pl.ds(0, r)])
+        rows = pl.ds(pl.multiple_of(p // 3 * r, r), r)
+        kind = lax.rem(p, 3)
+
+        @pl.when(kind < 2)
+        def _():
+            use(wgu_hbm.at[kind, rows])
+
+        @pl.when(kind == 2)
+        def _():
+            use(wd_hbm.at[rows])
 
     def mlp_slot(p, source):
         return w0.at[p, :, pl.ds(pl.multiple_of(source * wz, wz), wz)]
 
-    mlp_copies = [pltpu.make_async_copy(wgu_hbm.at[p, pl.ds(0, r)] if p < 2 else wd_hbm.at[pl.ds(0, r)],
-                                        mlp_slot(p, f), own_sems.at[last_piece + 1 + p]) for p in range(3)]
+    mlp_copies = []
+    for p in range(head):
+        rows = pl.ds(p // 3 * r, r)
+        mlp_copies.append(pltpu.make_async_copy(wgu_hbm.at[p % 3, rows] if p % 3 < 2 else wd_hbm.at[rows],
+                                                mlp_slot(p, f), own_sems.at[last_piece + 1 + p]))
     for copy in mlp_copies:
         copy.start()
     cot_rows = pl.ds(pl.multiple_of(s * tok, tok), tok)
@@ -689,7 +705,7 @@
 
     everyone_barrier(me, nf, ns)
     gather = LineGather(f, nf, last_piece + 1, own, slot, (ag_sr, ag_rr, ag_sl, ag_rl))
-    second = LineGather(f, nf, 3, mlp_own, mlp_slot, (m_sr, m_rr, m_sl, m_rl))
+    second = LineGather(f, nf, head, mlp_own, mlp_slot, (m_sr, m_rr, m_sl, m_rl))
     mine = pl.ds(pl.multiple_of(s * tok, tok), tok)
 
     def small(k):
@@ -797,7 +813,8 @@
             seen = lane_of((block_rows, block_rows)) <= lax.broadcasted_iota(jnp.int32, (block_rows, block_rows), 0)
             out = jnp.zeros((block_rows, LANES), f32)
             logs = lse[rows, :]
-            for h in range(PER):
+            def one_head(h, carry):
+                out, logs = carry
                 head = lane // HEAD_DIM == h
                 qm = jnp.where(head, q.astype(f32) * HEAD_DIM ** -0.5, 0.0).astype(bf16)
                 sd = jnp.where(seen, dot_nt(qm, kd), masked_score)
@@ -817,6 +834,9 @@
                     value = value + dot_nn((el * inv).astype(bf16), qkv[2, before, lanes])
                 out = jnp.where(head, value, out)
                 logs = jnp.where(lane == g * PER + h, top + jnp.log(tot), logs)
+                return out, logs
+
+            out, logs = lax.fori_loop(0, PER, one_head, (out, logs))
             att[rows, lanes] = out.astype(bf16)
             lse[rows, :] = logs
 
@@ -844,7 +864,7 @@
                 def _(t=t):
                     gather.tick(t)
                     if t == last_piece + nf - 2:
-                        for p in range(3):
+                        for p in range(head):
                             second.send_own(jnp.int32(p))
         for k in range(1, m):
             @pl.when((g == (0 if k < m - 1 else pairs - 1)) & (step == k))
@@ -856,7 +876,7 @@
             gather.tick(last_piece + nf - 1)
             own_copy(last_piece).wait()
             if pairs == 1:
-                for p in range(3):
+                for p in range(head):
                     second.send_own(jnp.int32(p))
 
         @pl.when(g == pairs)
@@ -871,7 +891,7 @@
             def _():
                 sums.pass_on(d + 1, keep[d + 1])
     second.arrivals(jnp.int32(1))
-    ticks = list(range(2, 3 + nf - 1))
+    ticks = list(range(2, head + nf - 1))
     store(qkv, qkv_hbm, 4)
     store(wq, wq_hbm, 5)
     store(wo, woall_hbm, 6)
@@ -904,7 +924,7 @@
         small(k).wait_send()
     for p in range(last_piece + 1):
         gather.drain(p)
-    for p in range(3):
+    for p in range(head):
         second.drain(p)
     rows_x.drain(x_hbm)
     rows_cot.drain(cot_hbm)
@@ -934,7 +954,7 @@
             S((length, width), bf16), S((length, width), bf16), S((length, width), bf16),
             S((3, length, cols), bf16), S((length, cols), bf16), S((length, LANES), f32),
             S((tok, width), f32), S((3, width, cols), bf16), S((cols, width), bf16),
-            S((8, width), f32), S((length, LANES), f32), S((length, LANES), f32), S((3, r, width), bf16),
+            S((8, width), f32), S((length, LANES), f32), S((length, LANES), f32), S((HEAD_PIECES, r, width), bf16),
         ),
         in_specs=[A, A, M, M, M, M, M, A, A, A, A],
         out_specs=[A] * 13,
@@ -944,9 +964,9 @@
             V((length, cols), bf16), V((length, LANES), f32), V((length, LANES), f32), V((length, LANES), f32),
             V((2 * tok, width), f32), V((m, tok, width), f32), V((m, tok, width), bf16),
             V((m, tok, width), bf16), V((m - 1, tok, width), bf16), V((tok, width), f32), V((tok, width), bf16),
-            V((3, r, width), bf16),
-            D((4,)), D((3 * pairs + 4,)), D((nf * ns,)), D((nf * ns,)),
-        ] + [D((3 * pairs + 1, nf - 1))] * 4 + [D((3, nf - 1))] * 4 + ([D((2 * m,))] * 2 + [D((m,))] * 2) * 3 + [D((m,))] * 2 + [D((2 * m,))] * 2 + [D((11,))],
+            V((HEAD_PIECES, r, width), bf16),
+            D((4,)), D((3 * pairs + 1 + HEAD_PIECES,)), D((nf * ns,)), D((nf * ns,)),
+        ] + [D((3 * pairs + 1, nf - 1))] * 4 + [D((HEAD_PIECES, nf - 1))] * 4 + ([D((2 * m,))] * 2 + [D((m,))] * 2) * 3 + [D((m,))] * 2 + [D((2 * m,))] * 2 + [D((11,))],
         compiler_params=pltpu.CompilerParams(
             collective_id=cid, has_side_effects=True, vmem_limit_bytes=64 * 1024 * 1024 - 65536),
         name="front",
@@ -1013,11 +1033,11 @@
     waiting = []
     if left:
         r = rest.shape[1]
-        first_row = gd_hbm.shape[0] - left * r
+        skipped = 3 * (gd_hbm.shape[0] // r) - left
 
         def rest_out(p, act):
-            kind, sl = lax.rem(p, 3), lax.rem(p, 2)
-            at = pl.ds(pl.multiple_of(first_row + p // 3 * r, 16), r)
+            kind, sl = lax.rem(p + skipped, 3), lax.rem(p, 2)
+            at = pl.ds(pl.multiple_of((p + skipped) // 3 * r, 16), r)
 
             @pl.when(kind < 2)
             def _():
@@ -1043,9 +1063,9 @@
                 rest_stage[sl] += rest_right[p, jnp.minimum(f, nf - 2)].astype(f32)
             rest_out(p, lambda cc: cc.start())
 
-        rest_sum = LineReduce(f, nf, 3 * left, lambda p, k: rest.at[p, :, pl.ds(pl.multiple_of(k * wz, wz), wz)], rest_left, rest_right,
+        rest_sum = LineReduce(f, nf, left, lambda p, k: rest.at[p, :, pl.ds(pl.multiple_of(k * wz, wz), wz)], rest_left, rest_right,
                               (q_sr, q_rr, q_sl, q_rl), rest_finish)
-        waiting = list(range(3 * left + nf - 1))
+        waiting = list(range(left + nf - 1))
 
     def rest_tick(how_many=1):
         for _ in range(how_many):
@@ -1145,7 +1165,7 @@
         both = go * att[rows, lanes].astype(f32)
         logs = lse[rows, :]
         grad_q = jnp.zeros((block_rows, LANES), f32)
-        for h in range(PER):
+        def one_head(h, grad_q):
             head = lane // HEAD_DIM == h
             qm = jnp.where(head, q, 0.0).astype(bf16)
             gm = jnp.where(head, go, 0.0).astype(bf16)
@@ -1164,7 +1184,9 @@
                 dv[at, :] += dot_tn(pr.astype(bf16), gm)
                 dk[at, :] += dot_tn(gs, qm)
                 acc = acc + dot_nn(gs, key)
-            grad_q = jnp.where(head, acc * HEAD_DIM ** -0.5, grad_q)
+            return jnp.where(head, acc * HEAD_DIM ** -0.5, grad_q)
+
+        grad_q = lax.fori_loop(0, PER, one_head, grad_q)
         gq[0, rows, lanes] = turn(grad_q, cos[rows, :], sin[rows, :], -1.0).astype(bf16)
 
     def weight_pieces(g):
@@ -1319,12 +1341,12 @@
     for st in stores:
         st.wait()
     if left:
-        for p in (3 * left - 2, 3 * left - 1):
+        for p in (left - 2, left - 1):
             rest_out(jnp.int32(p), lambda cc: cc.wait())
 
 
 def back(gsum, osum, res, cot, x, vec, qkv, att, lse, in1, wq, wo, cos, sin, rest, ggu, gd, nf, ns, cid):
-    left = 0 if rest is None else rest.shape[0] // 3
+    left = 0 if rest is None else rest.shape[0]
     tok, width = x.shape
     length, cols = att.shape
     wz = width // nf
@@ -1341,8 +1363,8 @@
         r = rest.shape[1]
         extra_in = (rest, ggu, gd)
         extra_out = (S(ggu.shape, f32), S(gd.shape, f32))
-        extra_scratch = [V((3 * left, r, width), bf16), V((3 * left, nf - 1, r, wz), bf16),
-                         V((3 * left, nf - 1, r, wz), bf16), V((2, r, wz), f32), D((2,))] + [D((3 * left, nf - 1))] * 4
+        extra_scratch = [V((left, r, width), bf16), V((left, nf - 1, r, wz), bf16),
+                         V((left, nf - 1, r, wz), bf16), V((2, r, wz), f32), D((2,))] + [D((left, nf - 1))] * 4
     rows_v = V((m, tok, width), bf16)
     offs_v = V((m - 1, tok, width), bf16)
     return pl.pallas_call(
@@ -1389,7 +1411,7 @@
 ):
     fsdp, seq = lax.axis_size("fsdp"), lax.axis_size("seq")
     gate_up = jnp.transpose(gate_up_weight, (1, 2, 0))
-    left = 1 if seq * block_input.shape[1] <= 1024 else 0
+    left = 4 if seq * block_input.shape[1] <= 1024 else 0
     (in_one, cot_all, in_two, qkv, mixed, logs, residual, qkv_full, out_full, vectors, cosine, sine, first) = front(
         block_input[0],
         cotangent[0],

time: 457 us -> 449 us (0.982); the launches traced: 449 us -> 448 us
    pallas_call x1, Pallas kernels: 159 us -> 147 us  [mlp(): pl.pallas_call(functools.partial(mlp_kernel, n, r, rb, head, left), out_s...]
    pallas_call x1, Pallas kernels: 145 us -> 151 us  [back(): pl.pallas_call(functools.partial(back_kernel, nf, ns, left), out_shape=(S...]
where the time goes in v5:
time: 449 us; the launch traced here: 448 us
  Pallas kernels  435 us (97%)
  local copies, waits for them, and re-layouts  12.5 us (3%)
    pallas_call x1, Pallas kernels, back(): pl.pallas_call(functools.partial(back_kernel, nf, ns, left), out_shape=(S...  151 us
    pallas_call x1, Pallas kernels, mlp(): pl.pallas_call(functools.partial(mlp_kernel, n, r, rb, head, left), out_s...  147 us
    pallas_call x1, Pallas kernels, front(): pl.pallas_call(functools.partial(front_kernel, nf, ns), out_shape=(S((len...  136 us
    unnamed x29, local copies, waits for them, and re-layouts  12.5 us

profile of v5, /device:TPU:0, one launch (start us, length us, event | category | flops | bytes accessed | tf_op | source)
XLA Modules:
  0.0 448.4 jit_solution(16633252209831386709)
XLA Ops:
  0.6 136.3 %front.1 = (bf16[1024,2048]{1,0:T(8,128)(2,1)}, bf16[1024,2048]{1,0:T(8,128)(2,1)}, bf16[1024,2048]{1,0:T(8,128)(2,1)}, bf16[3,1024,256]{2,1,0:T(8,128)(2,1)}, b...) custom-call(bf16[128,2048]{1,0:T(8,128)(2,1)} %bitcast.19, ...), custom_call_target="tpu_custom_call" | custom-call | tf_op jit(solution)/shard_map/front/pallas_call | solution.py:951
  137.0 147.4 %mlp.1 = (bf16[1024,2048]{1,0:T(8,128)(2,1)}, bf16[1024,2048]{1,0:T(8,128)(2,1)}, f32[2,704,512]{2,1,0:T(8,128)}, f32[704,512]{1,0:T(8,128)}, bf16[4,176,2048]{2,1,0:T(8,128)(2,1)}) custom-call(bf16[1024,2048]{1,0:T(8,128)(2,1)} %get-tuple-element.40.in2_hbm, bf16[1024,2048]{1,0:T(8,128)(2,1)} %get-tuple-element.41.cot_hbm, ...), custom_call_target="tpu_custom_call" | custom-call | tf_op jit(solution)/shard_map/mlp/pallas_call | solution.py:387
  284.4 151.3 %back.1 = (bf16[128,2048]{1,0:T(8,128)(2,1)}, f32[128,2048]{1,0:T(8,128)}, f32[3,512,256]{2,1,0:T(8,128)}, f32[256,512]{1,0:T(8,128)}, f32[1,64]{1,0:T(1,128)}, ...) custom-call(bf16[1024,2048]{1,0:T(8,128)(2,1)} %get-tuple-element.43, ...), custom_call_target="tpu_custom_call", output_to_operand_aliasing={{9}: (15, {}), {10}: (16, {})} | custom-call | tf_op jit(solution)/shard_map/back/pallas_call | solution.py:1370
  435.8 0.0 copy-start.8
  435.8 0.0 copy-start.7
  435.8 0.0 copy-start.2
  435.8 2.0 copy.37
  437.8 0.0 copy-start
  437.8 2.4 copy.38
  440.3 0.0 copy-done.8
  440.3 0.5 copy.39
  440.8 0.0 copy-done.7
  440.8 0.5 copy.40
  441.3 0.0 copy-done.2
  441.3 1.1 copy.41
  442.5 0.0 copy-done.4
  442.5 0.6 copy.42
  443.0 0.0 copy-done.3
  443.0 0.8 copy.43
  443.8 0.5 copy.44
  444.4 0.5 copy.45
  444.9 1.6 copy.46
  446.5 0.8 copy-done.1
  447.3 1.1 copy.47
  (8 shorter events, 0.0 us)
Async XLA Ops:
  435.8 4.5 %copy-start.8 = (f32[1,64]{1,0:T(1,128)S(1)}, f32[1,64]{1,0:T(1,128)}, u32[]{:S(2)}) copy-start(f32[1,64]{1,0:T(1,128)} %get-tuple-element.60) | copy-start | bytes 772
  435.8 5.0 %copy-start.7 = (f32[1,64]{1,0:T(1,128)S(1)}, f32[1,64]{1,0:T(1,128)}, u32[]{:S(2)}) copy-start(f32[1,64]{1,0:T(1,128)} %get-tuple-element.61) | copy-start | bytes 772
  435.8 5.5 %copy-start.2 = (f32[3,512,256]{2,1,0:T(8,128)S(1)}, f32[3,512,256]{2,1,0:T(8,128)}, u32[]{:S(2)}) copy-start(f32[3,512,256]{2,1,0:T(8,128)} %get-tuple-element.62) | copy-start | bytes 4718596
  437.8 4.6 %copy-start.4 = (f32[3,64]{1,0:T(4,128)S(1)}, f32[3,64]{1,0:T(4,128)}, u32[]{:S(2)}) copy-start(f32[3,64]{1,0:T(4,128)} %get-tuple-element.85) | copy-start | bytes 2308
  437.8 5.2 %copy-start.3 = (f32[256,512]{1,0:T(8,128)S(1)}, f32[256,512]{1,0:T(8,128)}, u32[]{:S(2)}) copy-start(f32[256,512]{1,0:T(8,128)} %get-tuple-element.86) | copy-start | bytes 1572868
  437.8 6.0 %copy-start.6 = (f32[1,64]{1,0:T(1,128)S(1)}, f32[1,64]{1,0:T(1,128)}, u32[]{:S(2)}) copy-start(f32[1,64]{1,0:T(1,128)} %get-tuple-element.65) | copy-start | bytes 772
  437.8 6.5 %copy-start.5 = (f32[1,64]{1,0:T(1,128)S(1)}, f32[1,64]{1,0:T(1,128)}, u32[]{:S(2)}) copy-start(f32[1,64]{1,0:T(1,128)} %get-tuple-element.66) | copy-start | bytes 772
  437.8 7.0 %copy-start = (f32[2,704,512]{2,1,0:T(8,128)S(1)}, f32[2,704,512]{2,1,0:T(8,128)}, u32[]{:S(2)}) copy-start(f32[2,704,512]{2,1,0:T(8,128)} %get-tuple-element.67) | copy-start | bytes 8650756
  444.9 2.4 copy-start.1
